TPU v7x, 32 devices: a whole 2x2x4 slice. The times are simulated.
32 devices in a mesh: xy: 16 (over z, y, core), gz: 2 (over x).
Axes of the slice: x: 2, y: 2, z: 4, core: 2. Of those that a mesh axis runs over, the one named last changes fastest.
Arguments:
- positions: float32 [3, 32, 2, 16, 128], P(None, None, 'gz', 'xy'), may hold values from 0 to 2
- velocities: float32 [3, 32, 2, 16, 128], P(None, None, 'gz', 'xy'), may hold values from -6 to 6
- forces_prev: float32 [3, 32, 2, 16, 128], P(None, None, 'gz', 'xy'), may hold values from -48 to 48
- seeds: int32 [32, 2, 16, 128], P(None, 'gz', 'xy'), may hold values from 0 to 16383
- counts: int32 [2, 16, 128], P('gz', 'xy'), may hold values from 12 to 32, as said below
- offsets: int32 [2], replicated, may hold values from 0 to 127
Outputs:
- forces: float32 [3, 32, 2, 16, 128], P(None, None, 'gz', 'xy')
- velocities_out: float32 [3, 32, 2, 16, 128], P(None, None, 'gz', 'xy')
- stress: float32 [6, 2, 16, 128], P(None, 'gz', 'xy')
Inputs may be any that keep to these rules, and one draw needn't show every extreme that they name: `counts`: each cell holds 12 to 32 beads; every row of 128 cells along x has a full cell.
All inputs are finite; a program needn't handle non-finite values.
Results may differ from a plain program's by a relative error of at most 0.0003.
Values sent between devices are 32-bit elements; how exact they have to be, the bound alone decides.
No kernel may reach another device: no remote copies, remote signals or barrier semaphores. Data moves between devices by JAX's collectives and lax.ppermute only.
A program may use at most 128 MiB of HBM per device.

v0:
```python
import math

import jax
import jax.numpy as jnp
from jax import lax
from jax.sharding import PartitionSpec as P

CONSERVATIVE = 25.0
FRICTION = 4.5
NOISE_LEVEL = 3.0
TIME_STEP = 0.04
SHEAR_SPEED = 1.0
CELL_VOLUME = 8.0
FLOOR_SQUARED = 0.0025
COMPONENT_PAIRS = [(0, 0), (1, 1), (2, 2), (0, 1), (0, 2), (1, 2)]
NEIGHBOURS = [(dz, dy, dx) for dz in (-1, 0, 1) for dy in (-1, 0, 1) for dx in (-1, 0, 1)]


def with_halo(block, sides, width):
    for axis, dim in sides:
        count = lax.axis_size(axis)
        forward = [(i, i + 1) for i in range(count - 1)]
        forward.append((count - 1, 0))
        backward = [(target, source) for source, target in forward]
        low = lax.ppermute(
            lax.slice_in_dim(block, block.shape[dim] - width, None, axis=dim), axis, forward
        )
        high = lax.ppermute(lax.slice_in_dim(block, 0, width, axis=dim), axis, backward)
        block = jnp.concatenate([low, block, high], axis=dim)
    return block


def pair_terms(home_beads, near_beads, offset, same_cell, step):
    slots = home_beads.shape[1]
    shift = jnp.asarray([offset[0], offset[1], offset[2]], jnp.float32)[:, None, None, None]
    separation = home_beads[0:3, :, None, :] - near_beads[0:3, None, :, :] - 2.0 * shift
    velocity_gap = home_beads[3:6, :, None, :] - near_beads[3:6, None, :, :]
    squared = jnp.sum(separation * separation, axis=0)
    distance = jnp.sqrt(jnp.maximum(squared, FLOOR_SQUARED))
    occupied = home_beads[7][:, None, :] * near_beads[7][None, :, :]
    if same_cell:
        occupied = occupied * (1.0 - jnp.eye(slots, dtype=jnp.float32))[:, :, None]
    weight = jnp.maximum(1.0 - distance, 0.0) * occupied
    seed_sum = (
        home_beads[6].astype(jnp.int32)[:, None, :]
        + near_beads[6].astype(jnp.int32)[None, :, :]
        + (7919 * step + 1)
    )
    hashed = seed_sum * (seed_sum + 1) % 65521
    noise = (hashed.astype(jnp.float32) / 65521.0 - 0.5) * math.sqrt(12.0)
    approach = jnp.sum(separation * velocity_gap, axis=0) / distance
    magnitude = (
        CONSERVATIVE * weight
        - FRICTION * weight * weight * approach
        + NOISE_LEVEL * weight * noise / math.sqrt(TIME_STEP)
    ) / distance
    pair_force = magnitude[None] * separation
    home_force = jnp.sum(pair_force, axis=2)
    near_force = -jnp.sum(pair_force, axis=1)
    virial = jnp.stack(
        [
            jnp.sum(separation[first] * pair_force[second], axis=(0, 1))
            for first, second in COMPONENT_PAIRS
        ]
    ) * (0.5 / CELL_VOLUME)
    return (home_force, near_force, virial)


def extend(state, offset_now):
    extended = with_halo(state, (("xy", 3), ("gz", 2)), 1)
    index = lax.axis_index("xy")
    count = lax.axis_size("xy")
    shear = jnp.asarray([0.0, 0.0, 0.0, SHEAR_SPEED, 0.0, 0.0, 0.0, 0.0], jnp.float32)[
        :, None, None, None
    ]
    lower = extended[:, :, :, 0, :]
    upper = extended[:, :, :, -1, :]
    lower = jnp.where(index == 0, jnp.roll(lower, -offset_now, axis=-1) - shear, lower)
    upper = jnp.where(index == count - 1, jnp.roll(upper, offset_now, axis=-1) + shear, upper)
    return extended.at[:, :, :, 0, :].set(lower).at[:, :, :, -1, :].set(upper)


def evaluate(state, offset_now, step):
    extended = extend(state, offset_now)
    slots = state.shape[1]
    depth, rows, width = (state.shape[2], state.shape[3], state.shape[4])

    def home_of(level):
        return lax.dynamic_index_in_dim(state, level, 2, keepdims=False).reshape(8, slots, -1)

    def near_of(level, dz, dy, dx):
        plane = lax.dynamic_index_in_dim(extended, level + 1 + dz, 2, keepdims=False)
        block = plane[:, :, 1 + dy : 1 + dy + rows, :]
        return jnp.roll(block, -dx, axis=-1).reshape(8, slots, -1)

    def plane_full(level):
        home = home_of(level)
        plane_force = jnp.zeros((3, slots, rows * width), jnp.float32)
        plane_virial = jnp.zeros((6, rows * width), jnp.float32)
        for dz, dy, dx in NEIGHBOURS:
            same = (dz, dy, dx) == (0, 0, 0)
            home_force, near_force, virial = pair_terms(
                home, near_of(level, dz, dy, dx), (dx, dy, dz), same, step
            )
            plane_force = plane_force + home_force
            plane_virial = plane_virial + virial
        return (plane_force, plane_virial)

    planes_force, planes_virial = lax.map(plane_full, jnp.arange(depth, dtype=jnp.int32))
    total_force = jnp.moveaxis(planes_force, 0, 2).reshape(3, slots, -1)
    total_virial = jnp.moveaxis(planes_virial, 0, 1).reshape(6, -1)
    return (
        total_force.reshape(3, slots, depth, rows, width),
        total_virial.reshape(6, depth, rows, width),
    )


def shards(positions, velocities, forces_prev, seeds, counts, offsets):
    present = (lax.broadcasted_iota(jnp.int32, seeds.shape, 0) < counts[None]).astype(jnp.float32)
    fixed_part = jnp.stack([seeds.astype(jnp.float32), present])
    position_now = positions
    velocity_now = velocities
    force_now = forces_prev
    stress = None
    for step in range(2):
        half_speed = velocity_now + 0.5 * TIME_STEP * force_now
        position_now = position_now + TIME_STEP * half_speed
        state = jnp.concatenate([position_now, half_speed, fixed_part], axis=0)
        force_now, stress = evaluate(state, offsets[step], step)
        velocity_now = half_speed + 0.5 * TIME_STEP * force_now
    return (force_now, velocity_now * present[None], stress)


def solution(mesh):
    placed = (
        P(None, None, "gz", "xy", None),
        P(None, None, "gz", "xy", None),
        P(None, None, "gz", "xy", None),
        P(None, "gz", "xy", None),
        P("gz", "xy", None),
        P(),
    )
    return jax.shard_map(
        shards,
        mesh=mesh,
        in_specs=placed,
        out_specs=(
            P(None, None, "gz", "xy", None),
            P(None, None, "gz", "xy", None),
            P(None, "gz", "xy", None),
        ),
        check_vma=False,
    )
```

profile of v0, /device:TPU:0, one launch (start us, length us, event | category | flops | bytes accessed | tf_op | source)
XLA Modules:
  0.0 228.0 jit_solution(4456550508063612199)
XLA Ops:
  3.8 5.5 %collective-permute-start.1 = (f32[8,32,1,1,128]{4,1,0,3,2:T(8,128)S(1)}, f32[8,32,1,1,128]{4,1,0,3,2:T(8,128)S(1)}, u32[]{:S(2)}, u32[]{:S(2)}) collective-permute-start(f32[8,32,1,1,128]{4,1,0,3,2:T(8,128)S(1)} %pad_maximum_fusion.4), channel_id=1, source_target_pairs={{2,0},{4,2},{6,4},{8,6},{10,8},{12,10},{14,12},{16,14},{18,16},{20... | collective-permute-start | bytes 393224 | tf_op jit(solution)/shard_map/ppermute | solution.py:28
  11.8 4.6 %collective-permute-done = f32[8,32,1,1,128]{4,1,0,3,2:T(8,128)S(1)} collective-permute-done((f32[8,32,1,1,128]{4,1,0,3,2:T(8,128)S(1)}, f32[8,32,1,1,128]{4,1,0,3,2:T(8,128)S(1)}, u32[]{:S(2)}, u32[]{:S(2)}) %collective-permute-start) | collective-permute-done | bytes 131104 | tf_op jit(solution)/shard_map/ppermute | solution.py:25
  22.5 3.5 %collective-permute-done.3 = f32[8,32,1,3,128]{4,1,0,3,2:T(8,128)S(1)} collective-permute-done((f32[8,32,1,3,128]{4,1,0,3,2:T(8,128)S(1)}, f32[8,32,1,3,128]{4,1,0,3,2:T(8,128)S(1)}, u32[]{:S(2)}, u32[]{:S(2)}) %collective-permute-start.3) | collective-permute-done | bytes 393248 | tf_op jit(solution)/shard_map/ppermute | solution.py:28
  26.0 4.2 %collective-permute-done.2 = f32[8,32,1,3,128]{4,1,0,3,2:T(8,128)S(1)} collective-permute-done((f32[8,32,1,3,128]{4,1,0,3,2:T(8,128)S(1)}, f32[8,32,1,3,128]{4,1,0,3,2:T(8,128)S(1)}, u32[]{:S(2)}, u32[]{:S(2)}) %collective-permute-start.2) | collective-permute-done | bytes 393248 | tf_op jit(solution)/shard_map/ppermute | solution.py:25
  35.5 3.6 %multiply_reduce_fusion.63 = (f32[32,32,128]{2,1,0:T(8,128)S(1)}, f32[32,32,128]{2,1,0:T(8,128)S(1)}, f32[32,32,128]{2,1,0:T(8,128)S(1)}, f32[32,32,128]{2,1,0:T...) fusion(f32[3]{0:T(128)S(1)} %copy-done.116, ...), kind=kLoop, calls=%fused_computation.129 | loop fusion | flops 14942208 | bytes 6979644 | tf_op jit(solution)/shard_map/while/body/eval_jaxpr/reduce_sum | solution.py:38
  39.2 3.4 %multiply_reduce_fusion.57 = (f32[32,32,128]{2,1,0:T(8,128)S(1)}, f32[32,32,128]{2,1,0:T(8,128)S(1)}, f32[32,32,128]{2,1,0:T(8,128)S(1)}, f32[32,32,128]{2,1,0:T...) fusion(f32[3]{0:T(128)S(1)} %copy-done.117, ...), kind=kLoop, calls=%fused_computation.121 | loop fusion | flops 14942208 | bytes 6979644 | tf_op jit(solution)/shard_map/while/body/eval_jaxpr/reduce_sum | solution.py:38
  42.6 3.2 %fusion.340 = (f32[32,32,128]{2,1,0:T(8,128)S(1)}, f32[32,32,128]{2,1,0:T(8,128)S(1)}, f32[32,32,128]{2,1,0:T(8,128)S(1)}, f32[32,32,128]{2,1,0:T(8,128)S(1)}) fusion(f32[32,32,128]{2,1,0:T(8,128)S(1)} %get-tuple-element.525, f32[32,32,128]{2,1,0:T(8,128)S(1)} %get-tuple-element.526, s32[32,128]{1,0:T(8,128)S(1)} %get-tuple-element.927, ...), kind=kLoop, calls=%fused_computation.755 | loop fusion | flops 15728640 | bytes 6455296 | tf_op jit(solution)/shard_map/while/body/eval_jaxpr/div | solution.py:52
  45.9 3.2 %fusion.360 = (f32[32,32,128]{2,1,0:T(8,128)S(1)}, f32[32,32,128]{2,1,0:T(8,128)S(1)}, f32[32,32,128]{2,1,0:T(8,128)S(1)}, f32[32,32,128]{2,1,0:T(8,128)S(1)}) fusion(f32[32,32,128]{2,1,0:T(8,128)S(1)} %get-tuple-element.529, f32[32,32,128]{2,1,0:T(8,128)S(1)} %get-tuple-element.530, s32[32,128]{1,0:T(8,128)S(1)} %get-tuple-element.931, ...), kind=kLoop, calls=%fused_computation.775 | loop fusion | flops 15728640 | bytes 6455296 | tf_op jit(solution)/shard_map/while/body/eval_jaxpr/div | solution.py:52
  49.3 3.6 %multiply_reduce_fusion.66 = (f32[32,32,128]{2,1,0:T(8,128)S(1)}, f32[32,32,128]{2,1,0:T(8,128)S(1)}, f32[32,32,128]{2,1,0:T(8,128)S(1)}, f32[32,32,128]{2,1,0:T...) fusion(f32[3]{0:T(128)S(1)} %copy-done.110, ...), kind=kLoop, calls=%fused_computation.133 | loop fusion | flops 14012416 | bytes 6455356 | tf_op jit(solution)/shard_map/while/body/eval_jaxpr/reduce_sum | solution.py:38
  52.9 3.5 %multiply_reduce_fusion.60 = (f32[32,32,128]{2,1,0:T(8,128)S(1)}, f32[32,32,128]{2,1,0:T(8,128)S(1)}, f32[32,32,128]{2,1,0:T(8,128)S(1)}, f32[32,32,128]{2,1,0:T...) fusion(f32[3]{0:T(128)S(1)} %copy-done.119, ...), kind=kLoop, calls=%fused_computation.125 | loop fusion | flops 14548992 | bytes 6979644 | tf_op jit(solution)/shard_map/while/body/eval_jaxpr/reduce_sum | solution.py:38
  56.5 3.4 %fusion.400 = (f32[32,32,128]{2,1,0:T(8,128)S(1)}, f32[32,32,128]{2,1,0:T(8,128)S(1)}, f32[32,32,128]{2,1,0:T(8,128)S(1)}, f32[32,32,128]{2,1,0:T(8,128)S(1)}) fusion(f32[32,32,128]{2,1,0:T(8,128)S(1)} %get-tuple-element.537, f32[32,32,128]{2,1,0:T(8,128)S(1)} %get-tuple-element.538, s32[32,128]{1,0:T(8,128)S(1)} %get-tuple-element.937, ...), kind=kLoop, calls=%fused_computation.815 | loop fusion | flops 15859712 | bytes 6459392 | tf_op jit(solution)/shard_map/while/body/eval_jaxpr/div | solution.py:52
  59.9 3.3 %multiply_reduce_fusion.124 = (f32[3,32,128]{2,1,0:T(8,128)S(1)}, f32[3,32,128]{2,1,0:T(8,128)S(1)}, f32[32,32,128]{2,1,0:T(8,128)S(1)}, f32[32,32,128]{2,1,0:T(...) fusion(f32[3]{0:T(128)S(1)} %copy-done.107, ...), kind=kLoop, calls=%fused_computation.211 | loop fusion | flops 12689408 | bytes 5931068 | tf_op jit(solution)/shard_map/while/body/eval_jaxpr/reduce_sum | solution.py:58
  63.2 3.2 %fusion.320 = (f32[32,32,128]{2,1,0:T(8,128)S(1)}, f32[32,32,128]{2,1,0:T(8,128)S(1)}, f32[32,32,128]{2,1,0:T(8,128)S(1)}, f32[32,32,128]{2,1,0:T(8,128)S(1)}) fusion(f32[32,32,128]{2,1,0:T(8,128)S(1)} %get-tuple-element.519, f32[32,32,128]{2,1,0:T(8,128)S(1)} %get-tuple-element.520, s32[32,128]{1,0:T(8,128)S(1)} %get-tuple-element.779, ...), kind=kLoop, calls=%fused_computation.735 | loop fusion | flops 15728640 | bytes 6455296 | tf_op jit(solution)/shard_map/while/body/eval_jaxpr/div | solution.py:52
  66.5 3.2 %fusion.300 = (f32[32,32,128]{2,1,0:T(8,128)S(1)}, f32[32,32,128]{2,1,0:T(8,128)S(1)}, f32[32,32,128]{2,1,0:T(8,128)S(1)}, f32[32,32,128]{2,1,0:T(8,128)S(1)}) fusion(f32[32,32,128]{2,1,0:T(8,128)S(1)} %get-tuple-element.515, f32[32,32,128]{2,1,0:T(8,128)S(1)} %get-tuple-element.516, s32[32,128]{1,0:T(8,128)S(1)} %get-tuple-element.929, ...), kind=kLoop, calls=%fused_computation.715 | loop fusion | flops 15728640 | bytes 6455296 | tf_op jit(solution)/shard_map/while/body/eval_jaxpr/div | solution.py:52
  69.7 3.2 %fusion.310 = (f32[32,32,128]{2,1,0:T(8,128)S(1)}, f32[32,32,128]{2,1,0:T(8,128)S(1)}, f32[32,32,128]{2,1,0:T(8,128)S(1)}, f32[32,32,128]{2,1,0:T(8,128)S(1)}) fusion(f32[32,32,128]{2,1,0:T(8,128)S(1)} %get-tuple-element.517, f32[32,32,128]{2,1,0:T(8,128)S(1)} %get-tuple-element.518, s32[32,128]{1,0:T(8,128)S(1)} %get-tuple-element.1112, ...), kind=kLoop, calls=%fused_computation.725 | loop fusion | flops 15728640 | bytes 6455296 | tf_op jit(solution)/shard_map/while/body/eval_jaxpr/div | solution.py:52
  85.3 4.1 %collective-permute-start.5 = (f32[8,32,1,1,128]{4,1,0,2,3:T(8,128)S(1)}, f32[8,32,1,1,128]{4,1,0,2,3:T(8,128)S(1)}, u32[]{:S(2)}, u32[]{:S(2)}) collective-permute-start(f32[8,32,1,1,128]{4,1,0,2,3:T(8,128)S(1)} %pad_maximum_fusion.5), channel_id=1, source_target_pairs={{2,0},{4,2},{6,4},{8,6},{10,8},{12,10},{14,12},{16,14},{18,16},{20... | collective-permute-start | bytes 393224 | tf_op jit(solution)/shard_map/ppermute | solution.py:28
  91.9 4.6 %collective-permute-done.4 = f32[8,32,1,1,128]{4,1,0,2,3:T(8,128)S(1)} collective-permute-done((f32[8,32,1,1,128]{4,1,0,2,3:T(8,128)S(1)}, f32[8,32,1,1,128]{4,1,0,2,3:T(8,128)S(1)}, u32[]{:S(2)}, u32[]{:S(2)}) %collective-permute-start.4) | collective-permute-done | bytes 131104 | tf_op jit(solution)/shard_map/ppermute | solution.py:25
  101.2 4.8 %collective-permute-done.7 = f32[8,32,1,3,128]{4,1,0,2,3:T(8,128)S(1)} collective-permute-done((f32[8,32,1,3,128]{4,1,0,2,3:T(8,128)S(1)}, f32[8,32,1,3,128]{4,1,0,2,3:T(8,128)S(1)}, u32[]{:S(2)}, u32[]{:S(2)}) %collective-permute-start.7) | collective-permute-done | bytes 393248 | tf_op jit(solution)/shard_map/ppermute | solution.py:28
  106.1 4.2 %collective-permute-done.6 = f32[8,32,1,3,128]{4,1,0,2,3:T(8,128)S(1)} collective-permute-done((f32[8,32,1,3,128]{4,1,0,2,3:T(8,128)S(1)}, f32[8,32,1,3,128]{4,1,0,2,3:T(8,128)S(1)}, u32[]{:S(2)}, u32[]{:S(2)}) %collective-permute-start.6) | collective-permute-done | bytes 393248 | tf_op jit(solution)/shard_map/ppermute | solution.py:25
  129.2 3.6 %multiply_reduce_fusion.7 = (f32[32,32,128]{2,1,0:T(8,128)S(1)}, f32[32,32,128]{2,1,0:T(8,128)S(1)}, f32[32,32,128]{2,1,0:T(8,128)S(1)}, f32[32,32,128]{2,1,0:T(...) fusion(f32[3]{0:T(128)S(1)} %copy-done.116, ...), kind=kLoop, calls=%fused_computation.24 | loop fusion | flops 14942208 | bytes 6979644 | tf_op jit(solution)/shard_map/while/body/eval_jaxpr/reduce_sum | solution.py:38
  133.0 3.4 %multiply_reduce_fusion.5 = (f32[32,32,128]{2,1,0:T(8,128)S(1)}, f32[32,32,128]{2,1,0:T(8,128)S(1)}, f32[32,32,128]{2,1,0:T(8,128)S(1)}, f32[32,32,128]{2,1,0:T(...) fusion(f32[3]{0:T(128)S(1)} %copy-done.120, ...), kind=kLoop, calls=%fused_computation.20 | loop fusion | flops 14548992 | bytes 6979644 | tf_op jit(solution)/shard_map/while/body/eval_jaxpr/reduce_sum | solution.py:38
  136.6 3.5 %multiply_reduce_fusion.3 = (f32[32,32,128]{2,1,0:T(8,128)S(1)}, f32[32,32,128]{2,1,0:T(8,128)S(1)}, f32[32,32,128]{2,1,0:T(8,128)S(1)}, f32[32,32,128]{2,1,0:T(...) fusion(f32[3]{0:T(128)S(1)} %copy-done.118, ...), kind=kLoop, calls=%fused_computation.16 | loop fusion | flops 14942208 | bytes 6979644 | tf_op jit(solution)/shard_map/while/body/eval_jaxpr/reduce_sum | solution.py:38
  142.5 4.1 %fusion.560 = (f32[32,32,128]{2,1,0:T(8,128)}, f32[32,32,128]{2,1,0:T(8,128)S(1)}, f32[32,32,128]{2,1,0:T(8,128)}, f32[32,32,128]{2,1,0:T(8,128)S(1)}) fusion(f32[32,32,128]{2,1,0:T(8,128)S(1)} %get-tuple-element.557, f32[32,32,128]{2,1,0:T(8,128)S(1)} %get-tuple-element.558, s32[32,128]{1,0:T(8,128)S(1)} %get-tuple-element.709, ...), kind=kLoop, calls=%fused_computation.975 | loop fusion | flops 15859712 | bytes 6459392 | tf_op jit(solution)/shard_map/while/body/eval_jaxpr/div | solution.py:52
  146.7 4.2 %fusion.917 = (f32[3,32,128]{2,1,0:T(8,128)}, f32[3,32,128]{2,1,0:T(8,128)}, f32[32,32,128]{2,1,0:T(8,128)S(1)}, f32[32,32,128]{2,1,0:T(8,128)S(1)}, f32[32,32,1...) fusion(f32[3,32,128]{2,1,0:T(8,128)S(1)} %get-tuple-element.739, ...), kind=kLoop, calls=%fused_computation.1886 | loop fusion | flops 12689408 | bytes 18513968 | tf_op jit(solution)/shard_map/while/body/eval_jaxpr/reduce_sum | solution.py:58
  162.4 3.9 %fusion.540 = (f32[32,32,128]{2,1,0:T(8,128)}, f32[32,32,128]{2,1,0:T(8,128)S(1)}, f32[32,32,128]{2,1,0:T(8,128)S(1)}, f32[32,32,128]{2,1,0:T(8,128)S(1)}) fusion(f32[32,32,128]{2,1,0:T(8,128)S(1)} %get-tuple-element.553, f32[32,32,128]{2,1,0:T(8,128)S(1)} %get-tuple-element.554, s32[32,128]{1,0:T(8,128)S(1)} %copy-done.67, f32[32,128]{1,0:T(8,128)S(1)} %copy-done.66, ...), kind=kLoop, calls=%fused_computation.955 | loop fusion | flops 15728640 | bytes 6455296 | tf_op jit(solution)/shard_map/while/body/eval_jaxpr/div | solution.py:52
  166.5 3.9 %fusion.550 = (f32[32,32,128]{2,1,0:T(8,128)}, f32[32,32,128]{2,1,0:T(8,128)S(1)}, f32[32,32,128]{2,1,0:T(8,128)S(1)}, f32[32,32,128]{2,1,0:T(8,128)S(1)}) fusion(f32[32,32,128]{2,1,0:T(8,128)S(1)} %get-tuple-element.555, f32[32,32,128]{2,1,0:T(8,128)S(1)} %get-tuple-element.556, s32[32,128]{1,0:T(8,128)S(1)} %copy-done.61, f32[32,128]{1,0:T(8,128)S(1)} %copy-done.60, ...), kind=kLoop, calls=%fused_computation.965 | loop fusion | flops 15728640 | bytes 6455296 | tf_op jit(solution)/shard_map/while/body/eval_jaxpr/div | solution.py:52
  170.5 4.0 %fusion.580 = (f32[32,32,128]{2,1,0:T(8,128)}, f32[32,32,128]{2,1,0:T(8,128)S(1)}, f32[32,32,128]{2,1,0:T(8,128)S(1)}, f32[32,32,128]{2,1,0:T(8,128)}) fusion(f32[32,32,128]{2,1,0:T(8,128)S(1)} %get-tuple-element.561, f32[32,32,128]{2,1,0:T(8,128)S(1)} %get-tuple-element.562, s32[32,128]{1,0:T(8,128)S(1)} %copy-done.57, f32[32,128]{1,0:T(8,128)S(1)} %copy-done.56, ...), kind=kLoop, calls=%fused_computation.995 | loop fusion | flops 15728640 | bytes 6455296 | tf_op jit(solution)/shard_map/while/body/eval_jaxpr/div | solution.py:52
  174.6 5.8 %fusion.1245 = (f32[3,32,128]{2,1,0:T(8,128)}, f32[3,32,128]{2,1,0:T(8,128)}, f32[3,32,128]{2,1,0:T(8,128)}, f32[3,32,128]{2,1,0:T(8,128)}, f32[3,32,128]{2,1,0:...) fusion(f32[3]{0:T(128)S(1)} %copy-done.103, ...), kind=kLoop, calls=%fused_computation.2354 | loop fusion | flops 9363456 | bytes 19513416 | tf_op jit(solution)/shard_map/while/body/eval_jaxpr/reduce_sum | solution.py:58
  187.4 3.2 %fusion.600 = (f32[32,32,128]{2,1,0:T(8,128)S(1)}, f32[32,32,128]{2,1,0:T(8,128)S(1)}, f32[32,32,128]{2,1,0:T(8,128)S(1)}, f32[32,32,128]{2,1,0:T(8,128)S(1)}) fusion(f32[32,32,128]{2,1,0:T(8,128)S(1)} %get-tuple-element.565, f32[32,32,128]{2,1,0:T(8,128)S(1)} %get-tuple-element.566, s32[32,128]{1,0:T(8,128)S(1)} %get-tuple-element.859, ...), kind=kLoop, calls=%fused_computation.1015 | loop fusion | flops 15728640 | bytes 6455296 | tf_op jit(solution)/shard_map/while/body/eval_jaxpr/div | solution.py:52
  190.7 3.8 %fusion.1228 = (f32[3,32,128]{2,1,0:T(8,128)S(1)}, f32[3,32,128]{2,1,0:T(8,128)S(1)}, f32[3,32,128]{2,1,0:T(8,128)S(1)}, f32[3,32,128]{2,1,0:T(8,128)S(1)}, f32[...) fusion(f32[3]{0:T(128)S(1)} %copy-done.109, ...), kind=kLoop, calls=%fused_computation.2337 | loop fusion | flops 9363456 | bytes 21086280 | tf_op jit(solution)/shard_map/while/body/eval_jaxpr/reduce_sum | solution.py:58
  198.5 4.3 %fusion.1229 = (f32[3,32,128]{2,1,0:T(8,128)S(1)}, f32[3,32,128]{2,1,0:T(8,128)S(1)}, f32[3,32,128]{2,1,0:T(8,128)S(1)}, f32[3,32,128]{2,1,0:T(8,128)S(1)}, f32[...) fusion(f32[3]{0:T(128)S(1)} %copy-done.115, ...), kind=kLoop, calls=%fused_computation.2338 | loop fusion | flops 9363456 | bytes 22659144 | tf_op jit(solution)/shard_map/while/body/eval_jaxpr/reduce_sum | solution.py:58
  205.7 4.0 %fusion.915 = (f32[3,32,128]{2,1,0:T(8,128)S(1)}, f32[3,32,128]{2,1,0:T(8,128)S(1)}, f32[3,32,128]{2,1,0:T(8,128)S(1)}, f32[3,32,128]{2,1,0:T(8,128)S(1)}, f32[3...) fusion(f32[3,32,128]{2,1,0:T(8,128)S(1)} %copy-done.19, ...), kind=kLoop, calls=%fused_computation.1884 | loop fusion | flops 9363456 | bytes 22659132 | tf_op jit(solution)/shard_map/while/body/eval_jaxpr/reduce_sum | solution.py:58
  (678 shorter events, 93.9 us)
Async XLA Ops:
  0.6 21.8 %copy-start.153 = (s32[1,1,128]{2,1,0:T(1,128)S(1)}, s32[1,1,128]{2,1,0:T(1,128)}, u32[]{:S(2)}) copy-start(s32[1,1,128]{2,1,0:T(1,128)} %param.76) | copy-start | bytes 1540
  3.8 8.0 %collective-permute-start.1 = (f32[8,32,1,1,128]{4,1,0,3,2:T(8,128)S(1)}, f32[8,32,1,1,128]{4,1,0,3,2:T(8,128)S(1)}, u32[]{:S(2)}, u32[]{:S(2)}) collective-permute-start(f32[8,32,1,1,128]{4,1,0,3,2:T(8,128)S(1)} %pad_maximum_fusion.4), channel_id=1, source_target_pairs={{2,0},{4,2},{6,4},{8,6},{10,8},{12,10},{14,12},{16,14},{18,16},{20... | collective-permute-start | bytes 393224 | tf_op jit(solution)/shard_map/ppermute | solution.py:28
  9.3 7.1 %collective-permute-start = (f32[8,32,1,1,128]{4,1,0,3,2:T(8,128)S(1)}, f32[8,32,1,1,128]{4,1,0,3,2:T(8,128)S(1)}, u32[]{:S(2)}, u32[]{:S(2)}) collective-permute-start(f32[8,32,1,1,128]{4,1,0,3,2:T(8,128)S(1)} %pad_maximum_fusion.4), channel_id=1, source_target_pairs={{0,2},{2,4},{4,6},{6,8},{8,10},{10,12},{12,14},{14,16},{16,18},{18... | collective-permute-start | bytes 393224 | tf_op jit(solution)/shard_map/ppermute | solution.py:25
  16.4 9.6 %collective-permute-start.3 = (f32[8,32,1,3,128]{4,1,0,3,2:T(8,128)S(1)}, f32[8,32,1,3,128]{4,1,0,3,2:T(8,128)S(1)}, u32[]{:S(2)}, u32[]{:S(2)}) collective-permute-start(f32[8,32,1,3,128]{4,1,0,3,2:T(8,128)S(1)} %pad_maximum_fusion.2), channel_id=1, source_target_pairs={{1,0},{0,1},{3,2},{2,3},{5,4},{4,5},{7,6},{6,7},{9,8},{8,9},{11,10... | collective-permute-start | bytes 1179656 | tf_op jit(solution)/shard_map/ppermute | solution.py:28
  18.0 12.2 %collective-permute-start.2 = (f32[8,32,1,3,128]{4,1,0,3,2:T(8,128)S(1)}, f32[8,32,1,3,128]{4,1,0,3,2:T(8,128)S(1)}, u32[]{:S(2)}, u32[]{:S(2)}) collective-permute-start(f32[8,32,1,3,128]{4,1,0,3,2:T(8,128)S(1)} %pad_maximum_fusion.2), channel_id=1, source_target_pairs={{0,1},{1,0},{2,3},{3,2},{4,5},{5,4},{6,7},{7,6},{8,9},{9,8},{10,11... | collective-permute-start | bytes 1179656 | tf_op jit(solution)/shard_map/ppermute | solution.py:25
  85.3 6.6 %collective-permute-start.5 = (f32[8,32,1,1,128]{4,1,0,2,3:T(8,128)S(1)}, f32[8,32,1,1,128]{4,1,0,2,3:T(8,128)S(1)}, u32[]{:S(2)}, u32[]{:S(2)}) collective-permute-start(f32[8,32,1,1,128]{4,1,0,2,3:T(8,128)S(1)} %pad_maximum_fusion.5), channel_id=1, source_target_pairs={{2,0},{4,2},{6,4},{8,6},{10,8},{12,10},{14,12},{16,14},{18,16},{20... | collective-permute-start | bytes 393224 | tf_op jit(solution)/shard_map/ppermute | solution.py:28
  89.4 7.1 %collective-permute-start.4 = (f32[8,32,1,1,128]{4,1,0,2,3:T(8,128)S(1)}, f32[8,32,1,1,128]{4,1,0,2,3:T(8,128)S(1)}, u32[]{:S(2)}, u32[]{:S(2)}) collective-permute-start(f32[8,32,1,1,128]{4,1,0,2,3:T(8,128)S(1)} %pad_maximum_fusion.5), channel_id=1, source_target_pairs={{0,2},{2,4},{4,6},{6,8},{8,10},{10,12},{12,14},{14,16},{16,18},{18... | collective-permute-start | bytes 393224 | tf_op jit(solution)/shard_map/ppermute | solution.py:25
  96.5 9.6 %collective-permute-start.7 = (f32[8,32,1,3,128]{4,1,0,2,3:T(8,128)S(1)}, f32[8,32,1,3,128]{4,1,0,2,3:T(8,128)S(1)}, u32[]{:S(2)}, u32[]{:S(2)}) collective-permute-start(f32[8,32,1,3,128]{4,1,0,2,3:T(8,128)S(1)} %pad_maximum_fusion.3), channel_id=1, source_target_pairs={{1,0},{0,1},{3,2},{2,3},{5,4},{4,5},{7,6},{6,7},{9,8},{8,9},{11,10... | collective-permute-start | bytes 1179656 | tf_op jit(solution)/shard_map/ppermute | solution.py:28
  98.1 12.2 %collective-permute-start.6 = (f32[8,32,1,3,128]{4,1,0,2,3:T(8,128)S(1)}, f32[8,32,1,3,128]{4,1,0,2,3:T(8,128)S(1)}, u32[]{:S(2)}, u32[]{:S(2)}) collective-permute-start(f32[8,32,1,3,128]{4,1,0,2,3:T(8,128)S(1)} %pad_maximum_fusion.3), channel_id=1, source_target_pairs={{0,1},{1,0},{2,3},{3,2},{4,5},{5,4},{6,7},{7,6},{8,9},{9,8},{10,11... | collective-permute-start | bytes 1179656 | tf_op jit(solution)/shard_map/ppermute | solution.py:25
  111.8 21.0 %copy-start.9 = (f32[3,32,128]{2,1,0:T(8,128)}, f32[3,32,128]{2,1,0:T(8,128)S(1)}, u32[]{:S(2)}) copy-start(f32[3,32,128]{2,1,0:T(8,128)S(1)} %get-tuple-element.750) | copy-start | bytes 147460
  111.8 24.6 %copy-start.7 = (f32[3,32,128]{2,1,0:T(8,128)}, f32[3,32,128]{2,1,0:T(8,128)S(1)}, u32[]{:S(2)}) copy-start(f32[3,32,128]{2,1,0:T(8,128)S(1)} %get-tuple-element.748) | copy-start | bytes 147460
  113.2 23.3 %copy-start.11 = (f32[3,32,128]{2,1,0:T(8,128)}, f32[3,32,128]{2,1,0:T(8,128)S(1)}, u32[]{:S(2)}) copy-start(f32[3,32,128]{2,1,0:T(8,128)S(1)} %get-tuple-element.744) | copy-start | bytes 147460
  113.2 33.5 %copy-start.15 = (f32[3,32,128]{2,1,0:T(8,128)}, f32[3,32,128]{2,1,0:T(8,128)S(1)}, u32[]{:S(2)}) copy-start(f32[3,32,128]{2,1,0:T(8,128)S(1)} %get-tuple-element.747) | copy-start | bytes 147460
  115.6 20.9 %copy-start.20 = (f32[3,32,128]{2,1,0:T(8,128)}, f32[3,32,128]{2,1,0:T(8,128)S(1)}, u32[]{:S(2)}) copy-start(f32[3,32,128]{2,1,0:T(8,128)S(1)} %get-tuple-element.890) | copy-start | bytes 147460
  115.8 17.1 %copy-start.16 = (f32[3,32,128]{2,1,0:T(8,128)}, f32[3,32,128]{2,1,0:T(8,128)S(1)}, u32[]{:S(2)}) copy-start(f32[3,32,128]{2,1,0:T(8,128)S(1)} %get-tuple-element.914) | copy-start | bytes 147460
  116.6 16.3 %copy-start.22 = (f32[3,32,128]{2,1,0:T(8,128)}, f32[3,32,128]{2,1,0:T(8,128)S(1)}, u32[]{:S(2)}) copy-start(f32[3,32,128]{2,1,0:T(8,128)S(1)} %get-tuple-element.916) | copy-start | bytes 147460
  116.8 16.1 %copy-start.24 = (f32[3,32,128]{2,1,0:T(8,128)}, f32[3,32,128]{2,1,0:T(8,128)S(1)}, u32[]{:S(2)}) copy-start(f32[3,32,128]{2,1,0:T(8,128)S(1)} %get-tuple-element.918) | copy-start | bytes 147460
  117.6 18.9 %copy-start.26 = (f32[3,32,128]{2,1,0:T(8,128)}, f32[3,32,128]{2,1,0:T(8,128)S(1)}, u32[]{:S(2)}) copy-start(f32[3,32,128]{2,1,0:T(8,128)S(1)} %get-tuple-element.892) | copy-start | bytes 147460
  118.4 18.2 %copy-start.18 = (f32[3,32,128]{2,1,0:T(8,128)}, f32[3,32,128]{2,1,0:T(8,128)S(1)}, u32[]{:S(2)}) copy-start(f32[3,32,128]{2,1,0:T(8,128)S(1)} %get-tuple-element.894) | copy-start | bytes 147460
  119.5 27.1 %copy-start.34 = (f32[3,32,128]{2,1,0:T(8,128)}, f32[3,32,128]{2,1,0:T(8,128)S(1)}, u32[]{:S(2)}) copy-start(f32[3,32,128]{2,1,0:T(8,128)S(1)} %get-tuple-element.896) | copy-start | bytes 147460
  212.0 13.1 %copy-start.172 = (f32[128]{0:T(128)S(1)}, f32[128]{0:T(128)}, u32[]{:S(2)}) copy-start(f32[128]{0:T(128)} %get-tuple-element.380) | copy-start | bytes 1540
  212.1 13.1 %copy-start.171 = (f32[128]{0:T(128)S(1)}, f32[128]{0:T(128)}, u32[]{:S(2)}) copy-start(f32[128]{0:T(128)} %get-tuple-element.381) | copy-start | bytes 1540
  212.1 13.2 %copy-start.170 = (f32[128]{0:T(128)S(1)}, f32[128]{0:T(128)}, u32[]{:S(2)}) copy-start(f32[128]{0:T(128)} %get-tuple-element.379) | copy-start | bytes 1540
  212.1 14.3 %copy-start.37 = (f32[3,32,128]{2,1,0:T(8,128)S(1)}, f32[3,32,128]{2,1,0:T(8,128)}, u32[]{:S(2)}) copy-start(f32[3,32,128]{2,1,0:T(8,128)} %get-tuple-element.611) | copy-start | bytes 147460
  212.1 14.3 %copy-start.38 = (f32[3,32,128]{2,1,0:T(8,128)S(1)}, f32[3,32,128]{2,1,0:T(8,128)}, u32[]{:S(2)}) copy-start(f32[3,32,128]{2,1,0:T(8,128)} %get-tuple-element.612) | copy-start | bytes 147460
  212.1 14.3 %copy-start.44 = (f32[3,32,128]{2,1,0:T(8,128)S(1)}, f32[3,32,128]{2,1,0:T(8,128)}, u32[]{:S(2)}) copy-start(f32[3,32,128]{2,1,0:T(8,128)} %get-tuple-element.702) | copy-start | bytes 147460
  212.1 14.3 %copy-start.45 = (f32[3,32,128]{2,1,0:T(8,128)S(1)}, f32[3,32,128]{2,1,0:T(8,128)}, u32[]{:S(2)}) copy-start(f32[3,32,128]{2,1,0:T(8,128)} %get-tuple-element.621) | copy-start | bytes 147460
  212.1 14.3 %copy-start.46 = (f32[3,32,128]{2,1,0:T(8,128)S(1)}, f32[3,32,128]{2,1,0:T(8,128)}, u32[]{:S(2)}) copy-start(f32[3,32,128]{2,1,0:T(8,128)} %get-tuple-element.622) | copy-start | bytes 147460
  212.1 14.3 %copy-start.47 = (f32[3,32,128]{2,1,0:T(8,128)S(1)}, f32[3,32,128]{2,1,0:T(8,128)}, u32[]{:S(2)}) copy-start(f32[3,32,128]{2,1,0:T(8,128)} %get-tuple-element.623) | copy-start | bytes 147460
  212.1 14.3 %copy-start.48 = (f32[3,32,128]{2,1,0:T(8,128)S(1)}, f32[3,32,128]{2,1,0:T(8,128)}, u32[]{:S(2)}) copy-start(f32[3,32,128]{2,1,0:T(8,128)} %get-tuple-element.624) | copy-start | bytes 147460
  212.1 14.3 %copy-start.49 = (f32[3,32,128]{2,1,0:T(8,128)S(1)}, f32[3,32,128]{2,1,0:T(8,128)}, u32[]{:S(2)}) copy-start(f32[3,32,128]{2,1,0:T(8,128)} %get-tuple-element.625) | copy-start | bytes 147460
  212.2 14.3 %copy-start.50 = (f32[3,32,128]{2,1,0:T(8,128)S(1)}, f32[3,32,128]{2,1,0:T(8,128)}, u32[]{:S(2)}) copy-start(f32[3,32,128]{2,1,0:T(8,128)} %get-tuple-element.626) | copy-start | bytes 147460
  (157 other events, 478.2 us)
where the time goes:
time: 232 us; the launch traced here: 228 us
  other arithmetic  150 us (65%)
  waiting for transfers between devices  30.9 us (13%)
  local copies, waits for them, and re-layouts  23.7 us (10%)
  starting transfers between devices  13.8 us (6%)
  between operations  9.73 us (4%)
    div x14, other arithmetic, pair_terms(): (CONSERVATIVE * weight - FRICTION * weight * weight * approach + NOISE_LE...  47.3 us
    reduce_sum x10, other arithmetic, pair_terms(): home_force = jnp.sum(pair_force, axis=2)  34.6 us
    reduce_sum x8, other arithmetic, pair_terms(): squared = jnp.sum(separation * separation, axis=0)  26.8 us
    ppermute x4, waiting for transfers between devices, with_halo(): lax.ppermute(lax.slice_in_dim(block, block.shape[dim] - width, None, axis...  17.6 us
    unnamed x497, local copies, waits for them, and re-layouts  16.5 us
    reduce_sum x27, other arithmetic, pair_terms(): jnp.sum(separation[first] * pair_force[second], axis=(0, 1))  15.8 us
    ppermute x4, waiting for transfers between devices, with_halo(): lax.ppermute(lax.slice_in_dim(block, 0, width, axis=dim), axis, backward)  13.4 us
    mul x38, other arithmetic, pair_terms(): occupied = home_beads[7][:, None, :] * near_beads[7][None, :, :]  13 us
  transfers between devices with their start and end apart: 8, of which 8 were waited for; matrix products, arithmetic and copies ran while one was open for 1% of the time, Pallas kernels for 0%

commit v1 on v0

v1 whole, which is shorter than its diff:
```python
import functools
import math

import jax
import jax.numpy as jnp
from jax import lax
from jax.experimental import pallas as pl
from jax.experimental.pallas import tpu as pltpu
from jax.sharding import PartitionSpec as P

CONSERVATIVE = 25.0
FRICTION = 4.5
NOISE_LEVEL = 3.0
TIME_STEP = 0.04
SHEAR_SPEED = 1.0
CELL_VOLUME = 8.0
FLOOR_SQUARED = 0.0025
EDGE = 2.0
MODULUS = 65521
COMPONENT_PAIRS = [(0, 0), (1, 1), (2, 2), (0, 1), (0, 2), (1, 2)]

NOISE_UNIT = NOISE_LEVEL * math.sqrt(12.0) / math.sqrt(TIME_STEP)
SHIFT = CONSERVATIVE / NOISE_UNIT - 0.5 - 0.5 / MODULUS
VELOCITY_SCALE = FRICTION / NOISE_UNIT
INVERSE = 1.0 / MODULUS
FAR = 1.0e15
REACH = 1.001
SEED_MIDDLE = 8192
F32 = jnp.float32
SUB = 8


def take_rows(values, index):
    dims = lax.GatherDimensionNumbers(
        offset_dims=(),
        collapsed_slice_dims=(0,),
        start_index_map=(0,),
        operand_batching_dims=(1,),
        start_indices_batching_dims=(1,),
    )
    return lax.gather(
        values,
        index[..., None],
        dims,
        slice_sizes=(1, 1),
        mode=lax.GatherScatterMode.PROMISE_IN_BOUNDS,
    )


def centred(value):
    turns = jnp.round(value.astype(F32) * F32(INVERSE)).astype(jnp.int32)
    return (value - turns * MODULUS).astype(F32)


def home_noise(seed, step):
    a = seed.astype(jnp.int32) + (7919 * step + 1 + SEED_MIDDLE)
    return (
        centred(256 * a),
        centred(2 * a),
        centred(a * (a + 1)) + 0.5,
    )


def near_noise(seed):
    b = seed - SEED_MIDDLE
    high = jnp.floor((b + 64.0) * (1.0 / 128.0))
    low = b - 128.0 * high
    whole = b.astype(jnp.int32)
    return high, low, centred(whole * (whole + 1))


def pair_kernel(
    *refs, slots, lanes, sources, rows, own, step, first, last, virial, has_fixed
):
    refs = list(refs)
    take = lambda n: [refs.pop(0) for _ in range(n)]
    turn_ref, shear_ref, home_ref, home_fixed_ref = take(4)
    near_refs = take(sources)
    fixed_refs = take(sources) if has_fixed else near_refs
    force_in = None if first else take(1)[0]
    virial_in = take(1)[0] if (virial and not first) else None
    if last and virial:
        force_out, velocity_out, virial_out = take(3)
    elif virial:
        force_out, virial_out = take(2)
    else:
        (force_out,) = take(1)
    home, near, box, rank, pick, liste, part, total, tally, sizes = take(10)
    groups = slots // SUB
    capacity = liste.shape[0] // 9
    iota = lax.broadcasted_iota(jnp.int32, (SUB, lanes), 0)
    iota_f = iota.astype(F32)
    fixed_at = 6 * slots

    def block(ref, base, group):
        return ref[base + group * SUB : base + (group + 1) * SUB, :]

    def spread(row):
        return jnp.broadcast_to(row, (SUB, lanes))

    home_count = spread(home_fixed_ref[fixed_at + slots : fixed_at + slots + 1, :])
    low = [jnp.full((SUB, lanes), FAR, F32) for _ in range(3)]
    high = [jnp.full((SUB, lanes), -FAR, F32) for _ in range(3)]
    home_there = []
    for g in range(groups):
        there = iota_f + F32(g * SUB) < home_count
        home_there.append(there)
        for a in range(3):
            p = block(home_ref, a * slots, g)
            low[a] = jnp.minimum(low[a], jnp.where(there, p, FAR))
            high[a] = jnp.maximum(high[a], jnp.where(there, p, -FAR))
            home[(a * slots + g * SUB) : (a * slots + (g + 1) * SUB), :] = (
                jnp.where(there, p, -FAR) if a == 0 else p
            )
            home[((3 + a) * slots + g * SUB) : ((3 + a) * slots + (g + 1) * SUB), :] = (
                block(home_ref, (3 + a) * slots, g) * F32(VELOCITY_SCALE)
            )
        for a, value in enumerate(home_noise(block(home_fixed_ref, fixed_at, g), step)):
            at = (6 + a) * slots + g * SUB
            home[at : at + SUB, :] = value
    home_low = [spread(jnp.min(v, axis=0, keepdims=True)) - REACH for v in low]
    home_high = [spread(jnp.max(v, axis=0, keepdims=True)) + REACH for v in high]

    for r, (source, offset, dz, dy) in enumerate(rows):
        data, fixed = near_refs[source], fixed_refs[source]
        base = r * 7 * slots
        amount = turn_ref[0 if dy < 0 else 1] if dy else None
        turned = (lambda v: pltpu.roll(v, amount, 1)) if dy else (lambda v: v)
        count = turned(spread(fixed[offset[1] + fixed_at + slots : offset[1] + fixed_at + slots + 1, :]))
        for g in range(groups):
            there = iota_f + F32(g * SUB) < count
            for c in range(7):
                ref, at = (fixed, offset[1]) if c == 6 else (data, offset[0])
                v = turned(block(ref, at + c * slots, g))
                if c == 0:
                    v = jnp.where(there, v, FAR)
                if c == 1 and dy:
                    v = v + F32(EDGE * dy)
                if c == 2 and dz:
                    v = v + F32(EDGE * dz)
                if c == 3 and dy:
                    v = v + shear_ref[0 if dy < 0 else 1]
                if 3 <= c < 6:
                    v = v * F32(VELOCITY_SCALE)
                near[base + c * slots + g * SUB : base + c * slots + (g + 1) * SUB, :] = v

    def ranked(slot, marks):
        before = jnp.zeros((SUB, lanes), F32)
        for g in range(groups):
            run = jnp.where(marks[g], 1.0, 0.0)
            for d in (1, 2, 4):
                run = run + jnp.where(iota >= d, pltpu.roll(run, d, 0), 0.0)
            place = jnp.where(marks[g], run + (before - 1.0), -1.0)
            rank[(slot * slots + g * SUB) : (slot * slots + (g + 1) * SUB), :] = place
            before = before + spread(run[SUB - 1 : SUB, :])
        sizes[slot] = jnp.max(before).astype(jnp.int32)

    for r, (source, offset, dz, dy) in enumerate(rows):
        base = r * 7 * slots
        near_low = [jnp.full((SUB, lanes), FAR, F32) for _ in range(2)]
        near_high = [jnp.full((SUB, lanes), -FAR, F32) for _ in range(2)]
        for d, dx in enumerate((0, -1, 1)):
            marks = []
            for g in range(groups):
                pos = [
                    near[base + a * slots + g * SUB : base + a * slots + (g + 1) * SUB, :]
                    for a in range(3)
                ]
                if dx:
                    pos = [pltpu.roll(v, (-dx) % lanes, 1) for v in pos]
                    pos[0] = pos[0] + F32(EDGE * dx)
                mark = (pos[0] > home_low[0]) & (pos[0] < home_high[0])
                for a in (1, 2):
                    mark = mark & (pos[a] > home_low[a]) & (pos[a] < home_high[a])
                marks.append(mark)
                if not own:
                    for a in (1, 2):
                        near_low[a - 1] = jnp.minimum(near_low[a - 1], jnp.where(mark, pos[a], FAR))
                        near_high[a - 1] = jnp.maximum(near_high[a - 1], jnp.where(mark, pos[a], -FAR))
            ranked(4 * r + d, marks)
        if not own:
            bounds = [
                (
                    spread(jnp.min(near_low[a], axis=0, keepdims=True)) - REACH,
                    spread(jnp.max(near_high[a], axis=0, keepdims=True)) + REACH,
                )
                for a in range(2)
            ]
            marks = []
            for g in range(groups):
                mark = home_there[g]
                for a in range(2):
                    p = home[(a + 1) * slots + g * SUB : (a + 1) * slots + (g + 1) * SUB, :]
                    mark = mark & (p > bounds[a][0]) & (p < bounds[a][1])
                marks.append(mark)
            ranked(4 * r + 3, marks)

    def choose(slot, k):
        target = iota_f + (k * SUB).astype(F32)
        index = jnp.full((SUB, lanes), -1, jnp.int32)
        for s in range(slots):
            index = jnp.where(rank[pl.ds(slot * slots + s, SUB, stride=0), :] == target, s, index)
        return index

    def gathered(ref, base, index):
        within = index & (SUB - 1)
        result = take_rows(ref[pl.ds(base, SUB), :], within)
        for g in range(1, groups):
            result = jnp.where(
                index >= g * SUB, take_rows(ref[pl.ds(base + g * SUB, SUB), :], within), result
            )
        return result

    def aligned(value):
        return pl.multiple_of(value, SUB)

    def run_pairs(count, where_home, blocks):
        def one(j, carry):
            carry = list(carry)
            n = [liste[pl.ds(c * capacity + j, SUB, stride=0), :] for c in range(9)]
            tot = [None] * 3
            for b in range(blocks):
                h = [where_home[c * slots + b * SUB : c * slots + (b + 1) * SUB, :] for c in range(9)]
                rx, ry, rz = h[0] - n[0], h[1] - n[1], h[2] - n[2]
                squared = jnp.maximum(rx * rx + ry * ry + rz * rz, FLOOR_SQUARED)
                inverse = lax.rsqrt(squared)
                weight = jnp.maximum(1.0 - squared * inverse, 0.0)
                u = weight * inverse
                rv = rx * (h[3] - n[3]) + ry * (h[4] - n[4]) + rz * (h[5] - n[5])
                t = ((h[6] * n[6] + h[7] * n[7]) + (h[8] + n[8])) * F32(INVERSE)
                y = (t - jnp.floor(t)) + F32(SHIFT)
                magnitude = u * (y - u * rv)
                f = [magnitude * rx, magnitude * ry, magnitude * rz]
                for a in range(3):
                    carry[3 * b + a] = carry[3 * b + a] + f[a]
                    tot[a] = f[a] if tot[a] is None else tot[a] + f[a]
            if virial:
                for i, (a, b) in enumerate(COMPONENT_PAIRS):
                    carry[3 * blocks + i] = carry[3 * blocks + i] - n[a] * tot[b]
            return tuple(carry)

        def two(i, carry):
            return one(2 * i + 1, one(2 * i, carry))

        zero = jnp.zeros((SUB, lanes), F32)
        start = (zero,) * (3 * blocks + (6 if virial else 0))
        done = lax.fori_loop(0, (count + 1) // 2, two, start)
        for b in range(blocks):
            for a in range(3):
                part[a * slots + b * SUB : a * slots + (b + 1) * SUB, :] = done[3 * b + a]
        if virial:
            for i, (a, b) in enumerate(COMPONENT_PAIRS):
                value = tally[i * SUB : (i + 1) * SUB, :] + done[3 * blocks + i]
                for g in range(blocks):
                    value = value + (
                        where_home[a * slots + g * SUB : a * slots + (g + 1) * SUB, :] * done[3 * g + b]
                    )
                tally[i * SUB : (i + 1) * SUB, :] = value

    for c in range(3):
        for g in range(groups):
            at = c * slots + g * SUB
            total[at : at + SUB, :] = (
                jnp.zeros((SUB, lanes), F32) if first else force_in[at : at + SUB, :]
            )
    if virial:
        for i in range(6):
            tally[i * SUB : (i + 1) * SUB, :] = (
                jnp.zeros((SUB, lanes), F32) if first else virial_in[i * SUB : (i + 1) * SUB, :]
            )

    def direction(r, _):
        base = r * (7 * slots)
        filled = jnp.int32(0)
        for d, dx in enumerate((0, -1, 1)):
            slot = 4 * r + d
            size = sizes[slot]

            def fill(k, _, slot=slot, dx=dx, filled=filled):
                index = choose(slot, k)
                valid = index >= 0
                values = [
                    gathered_near(base + c * slots, index, dx) for c in range(7)
                ]
                values[0] = jnp.where(valid, values[0] + F32(EDGE * dx), FAR)
                values = values[:6] + list(near_noise(values[6]))
                for c in range(9):
                    liste[pl.ds(c * capacity + filled + k * SUB, SUB), :] = values[c]
                return 0

            def gathered_near(at, index, dx):
                within = index & (SUB - 1)
                result = None
                for g in range(groups):
                    v = near[pl.ds(aligned(at + g * SUB), SUB), :]
                    if dx:
                        v = pltpu.roll(v, (-dx) % lanes, 1)
                    v = take_rows(v, within)
                    result = v if g == 0 else jnp.where(index >= g * SUB, v, result)
                return result

            lax.fori_loop(0, (size + SUB - 1) // SUB, fill, 0)
            filled = filled + size
        liste[pl.ds(filled, SUB), :] = jnp.full((SUB, lanes), FAR, F32)
        for c in range(1, 9):
            liste[pl.ds(c * capacity + filled, SUB), :] = jnp.zeros((SUB, lanes), F32)
        if own:
            run_pairs(filled, home, groups)
            for c in range(3):
                for g in range(groups):
                    at = c * slots + g * SUB
                    total[at : at + SUB, :] = total[at : at + SUB, :] + part[at : at + SUB, :]
            return 0
        slot = 4 * r + 3
        needed = (sizes[slot] + SUB - 1) // SUB

        def fill_home(k, _):
            index = choose(slot, k)
            for c in range(9):
                v = gathered(home, c * slots, index)
                if c == 0:
                    v = jnp.where(index >= 0, v, -FAR)
                pick[pl.ds(aligned(c * slots + k * SUB), SUB), :] = v
            return 0

        lax.fori_loop(0, needed, fill_home, 0)
        for blocks in range(1, groups + 1):
            pl.when(needed == blocks)(functools.partial(run_pairs, filled, pick, blocks))

        def back(k, _):
            for g in range(groups):
                place = rank[pl.ds(aligned(slot * slots + g * SUB), SUB), :].astype(jnp.int32)
                mine = (place >= k * SUB) & (place < (k + 1) * SUB)
                within = place & (SUB - 1)
                for c in range(3):
                    at = c * slots + g * SUB
                    v = take_rows(part[pl.ds(aligned(c * slots + k * SUB), SUB), :], within)
                    total[at : at + SUB, :] = total[at : at + SUB, :] + jnp.where(mine, v, 0.0)
            return 0

        lax.fori_loop(0, needed, back, 0)
        return 0

    if len(rows) == 1:
        direction(jnp.int32(0), 0)
    else:
        lax.fori_loop(0, len(rows), direction, 0)

    half = F32(0.5 * TIME_STEP)
    for c in range(3):
        for g in range(groups):
            at = c * slots + g * SUB
            f = total[at : at + SUB, :]
            if not last:
                force_out[at : at + SUB, :] = f
                continue
            f = f * F32(NOISE_UNIT)
            v = block(home_ref, (3 + c) * slots, g) + half * f
            if virial:
                force_out[at : at + SUB, :] = f
                velocity_out[at : at + SUB, :] = jnp.where(home_there[g], v, 0.0)
            else:
                v = v + half * f
                force_out[at : at + SUB, :] = block(home_ref, c * slots, g) + F32(TIME_STEP) * v
                force_out[3 * slots + at : 3 * slots + at + SUB, :] = v
    if virial:
        for i in range(6):
            v = tally[i * SUB : (i + 1) * SUB, :]
            if last:
                virial_out[i : i + 1, :] = jnp.sum(v, axis=0, keepdims=True) * F32(
                    NOISE_UNIT * 0.5 / CELL_VOLUME
                )
            else:
                virial_out[i * SUB : (i + 1) * SUB, :] = v


def pairs(turn, shear, home, home_fixed, nears, fixed, carried, rows, step, last, virial, slots, cost):
    lanes = home.shape[-1]
    own = len(rows) == 1
    first = carried is None
    operands = [turn, shear, home, home_fixed, *nears]
    if fixed is not None:
        operands += list(fixed)
    if not first:
        operands += list(carried)
    shape = lambda n: jax.ShapeDtypeStruct((n, lanes), F32)
    if last and virial:
        outs = (shape(3 * slots), shape(3 * slots), shape(6))
    elif virial:
        outs = (shape(3 * slots), shape(6 * SUB))
    elif last:
        outs = (shape(6 * slots),)
    else:
        outs = (shape(3 * slots),)
    vmem = pl.BlockSpec(memory_space=pltpu.VMEM)
    smem = pl.BlockSpec(memory_space=pltpu.SMEM)
    capacity = 3 * slots + 2 * SUB
    count = len(rows)
    return pl.pallas_call(
        functools.partial(
            pair_kernel,
            slots=slots,
            lanes=lanes,
            sources=len(nears),
            rows=rows,
            own=own,
            step=step,
            first=first,
            last=last,
            virial=virial,
            has_fixed=fixed is not None,
        ),
        out_shape=outs,
        in_specs=[smem, smem] + [vmem] * (len(operands) - 2),
        out_specs=tuple(vmem for _ in outs),
        scratch_shapes=[
            pltpu.VMEM((9 * slots, lanes), F32),
            pltpu.VMEM((count * 7 * slots, lanes), F32),
            pltpu.VMEM((SUB, lanes), F32),
            pltpu.VMEM((count * 4 * slots, lanes), F32),
            pltpu.VMEM((9 * slots, lanes), F32),
            pltpu.VMEM((9 * capacity, lanes), F32),
            pltpu.VMEM((3 * slots, lanes), F32),
            pltpu.VMEM((3 * slots, lanes), F32),
            pltpu.VMEM((6 * SUB, lanes), F32),
            pltpu.SMEM((4 * count,), jnp.int32),
        ],
        cost_estimate=pl.CostEstimate(flops=cost, bytes_accessed=1, transcendentals=0),
        name=f"pairs_{count}_{step}",
    )(*operands)


def kick_kernel(position, velocity, force, seed, count, out, *, slots, lanes):
    for c in range(3):
        for g in range(slots // SUB):
            at = c * slots + g * SUB
            rows = slice(at, at + SUB)
            v = velocity[rows, :] + F32(0.5 * TIME_STEP) * force[rows, :]
            out[rows, :] = position[rows, :] + F32(TIME_STEP) * v
            out[3 * slots + at : 3 * slots + at + SUB, :] = v
    out[6 * slots : 7 * slots, :] = seed[...].astype(F32)
    out[7 * slots : 7 * slots + SUB, :] = jnp.broadcast_to(count[...], (SUB, lanes)).astype(F32)


def ring(count, by):
    return [(i, (i + by) % count) for i in range(count)]


def shards(positions, velocities, forces_prev, seeds, counts, offsets):
    slots, depth, width, lanes = seeds.shape
    assert depth == 1 and width == 1
    gz, xy = lax.axis_size("gz"), lax.axis_size("xy")
    index = lax.axis_index("xy")
    flat = lambda a: a.reshape(-1, lanes)
    tall = 7 * slots + SUB
    state = pl.pallas_call(
        functools.partial(kick_kernel, slots=slots, lanes=lanes),
        out_shape=jax.ShapeDtypeStruct((tall, lanes), F32),
        in_specs=[pl.BlockSpec(memory_space=pltpu.VMEM)] * 5,
        out_specs=pl.BlockSpec(memory_space=pltpu.VMEM),
        name="kick",
    )(flat(positions), flat(velocities), flat(forces_prev), flat(seeds), flat(counts))
    first_lower, first_upper = index == 0, index == xy - 1
    shear = jnp.stack(
        [jnp.where(first_lower, -SHEAR_SPEED, 0.0), jnp.where(first_upper, SHEAR_SPEED, 0.0)]
    ).astype(F32)
    home_fixed = state
    kept = None
    for step in range(2):
        offset = offsets[step]
        turn = jnp.stack(
            [
                jnp.where(first_lower, (lanes - offset) % lanes, 0),
                jnp.where(first_upper, offset % lanes, 0),
            ]
        ).astype(jnp.int32)
        final = step == 1
        high = state.shape[0]
        planes = [lax.ppermute(state, "gz", ring(gz, -1))]
        if gz > 2:
            planes.append(lax.ppermute(state, "gz", ring(gz, 1)))
        up, down = 0, len(planes) - 1
        stacked = jnp.concatenate([state, *planes], axis=0)
        lower = lax.ppermute(stacked, "xy", ring(xy, 1))
        upper = lax.ppermute(stacked, "xy", ring(xy, -1))
        if not final:
            kept = (planes, lower, upper)
            fixed = [None] * 3
        else:
            fixed = [[home_fixed], kept[0], [kept[1], kept[2]]]
        call = functools.partial(
            pairs, turn, shear, state, home_fixed, step=step, virial=final, slots=slots
        )
        here = (0, 0)
        carried = call(
            [state], fixed[0], None, rows=((0, here, 0, 0),), last=False, cost=4_000_000
        )
        carried = call(
            planes,
            fixed[1],
            carried,
            rows=((down, here, -1, 0), (up, here, 1, 0)),
            last=False,
            cost=4_000_000,
        )
        rows = []
        for source, dy in ((0, -1), (1, 1)):
            for dz, place in ((0, 0), (-1, 1 + down), (1, 1 + up)):
                rows.append((source, (place * high, place * tall), dz, dy))
        outs = call(
            [lower, upper], fixed[2], carried, rows=tuple(rows), last=True, cost=8_000_000
        )
        if not final:
            state = outs[0]
    force, velocity, stress = outs
    return (
        force.reshape(positions.shape),
        velocity.reshape(positions.shape),
        stress.reshape(6, depth, width, lanes),
    )


def solution(mesh):
    beads = P(None, None, "gz", "xy", None)
    return jax.shard_map(
        shards,
        mesh=mesh,
        in_specs=(beads, beads, beads, P(None, "gz", "xy", None), P("gz", "xy", None), P()),
        out_specs=(beads, beads, P(None, "gz", "xy", None)),
        check_vma=False,
    )
```

time: 232 us -> 75.3 us (0.32); the launches traced: 228 us -> 74.1 us
  other arithmetic: 150 us -> 3.78 us
  Pallas kernels: 0 us -> 41.6 us
  waiting for transfers between devices: 30.9 us -> 6.64 us
  local copies, waits for them, and re-layouts: 23.7 us -> 4.03 us
  between operations: 9.73 us -> 5.9 us
    reduce_sum x45 -> x0, other arithmetic: 77.2 us -> none  [the longest x10 34.6 us: pair_terms(): home_force = jnp.sum(pair_force, axis=2)]
    div x14 -> x0, other arithmetic: 47.3 us -> none  [pair_terms(): (CONSERVATIVE * weight - FRICTION * weight * weight * approach + NOISE_LE...]
    pallas_call x0 -> x7, Pallas kernels: none -> 41.6 us  [the longest x6 40.1 us: pairs(): pl.pallas_call(functools.partial(pair_kernel, slots=slots, lanes=lanes, s...]
    ppermute x8 -> x6, waiting for transfers between devices: 30.9 us -> 6.64 us  [the longest x2 6.63 us: shards(): planes = [lax.ppermute(state, 'gz', ring(gz, -1))]]
    mul x40 -> x0, other arithmetic: 14.9 us -> none  [the longest x38 13 us: pair_terms(): occupied = home_beads[7][:, None, :] * near_beads[7][None, :, :]]
    unnamed x497 -> x15, local copies, waits for them, and re-layouts: 16.5 us -> 3.38 us
    sub x35 -> x0, other arithmetic: 5.81 us -> none  [the longest x23 4.78 us: pair_terms(): home_beads[0:3, :, None, :] - near_beads[0:3, None, :, :] - 2.0 * shift]
    slice x11 -> x1, local copies, waits for them, and re-layouts: 3.37 us -> 0.65 us  [shards(): offset = offsets[step]]
  transfers between devices with their start and end apart: 8 -> 6, of which waited for: 8 -> 2; matrix products, arithmetic and copies ran while one was open for 1% -> 3% of each run, Pallas kernels for 0% -> 27%
where the time goes in v1:
time: 75.3 us; the launch traced here: 74.1 us
  Pallas kernels  41.6 us (55%)
  starting transfers between devices  12.1 us (16%)
  waiting for transfers between devices  6.64 us (9%)
  between operations  5.9 us (8%)
  local copies, waits for them, and re-layouts  4.03 us (5%)
  other arithmetic  3.78 us (5%)
    pallas_call x6, Pallas kernels, pairs(): pl.pallas_call(functools.partial(pair_kernel, slots=slots, lanes=lanes, s...  40.1 us
    ppermute x2, starting transfers between devices, shards(): upper = lax.ppermute(stacked, 'xy', ring(xy, -1))  7.46 us
    ppermute x2, waiting for transfers between devices, shards(): planes = [lax.ppermute(state, 'gz', ring(gz, -1))]  6.63 us
    ppermute x2, starting transfers between devices, shards(): planes = [lax.ppermute(state, 'gz', ring(gz, -1))]  4.6 us
    unnamed x15, local copies, waits for them, and re-layouts  3.38 us
    concatenate x2, other arithmetic, shards(): stacked = jnp.concatenate([state, *planes], axis=0)  1.9 us
    pallas_call x1, Pallas kernels, shards(): pl.pallas_call(functools.partial(kick_kernel, slots=slots, lanes=lanes),...  1.53 us
  transfers between devices with their start and end apart: 6, of which 2 were waited for; matrix products, arithmetic and copies ran while one was open for 3% of the time, Pallas kernels for 27%

profile of v1, /device:TPU:0, one launch (start us, length us, event | category | flops | bytes accessed | tf_op | source)
XLA Modules:
  0.0 74.1 jit_solution(15096610482534205263)
XLA Ops:
  0.6 1.5 %kick.1.refs_2_.refs_3_.refs_4_.refs_5_ = f32[232,128]{1,0:T(8,128)} custom-call(f32[96,128]{1,0:T(8,128)} %bitcast.20, f32[96,128]{1,0:T(8,128)} %bitcast.21, f32[96,128]{1,0:T(8,128)} %bitcast.22, s32[32,128]{1,0:T(8,128)} %bitcast.23, s32[1,128]{1,0:T(1,128)} %bitcast.25), custom_call_target="tpu_custom_call" | custom-call | tf_op jit(solution)/shard_map/kick/pallas_call | solution.py:456
  2.2 3.0 %collective-permute-start = (f32[232,128]{1,0:T(8,128)}, f32[232,128]{1,0:T(8,128)S(1)}, u32[]{:S(2)}, u32[]{:S(2)}) collective-permute-start(f32[232,128]{1,0:T(8,128)} %kick.1.refs_2_.refs_3_.refs_4_.refs_5_), channel_id=1, source_target_pairs={{0,1},{1,0},{2,3},{3,2},{4,5},{5,4},{6,7},{7,6},{8,9},{9,8},{10,11... | collective-permute-start | bytes 356360 | tf_op jit(solution)/shard_map/ppermute | solution.py:479
  5.1 3.4 %collective-permute-done.refs_4_.refs_5_ = f32[232,128]{1,0:T(8,128)S(1)} collective-permute-done((f32[232,128]{1,0:T(8,128)}, f32[232,128]{1,0:T(8,128)S(1)}, u32[]{:S(2)}, u32[]{:S(2)}) %collective-permute-start) | collective-permute-done | bytes 118816 | tf_op jit(solution)/shard_map/ppermute | solution.py:479
  8.6 1.0 %pad_maximum_fusion = f32[464,128]{1,0:T(8,128)S(1)} fusion(f32[232,128]{1,0:T(8,128)S(1)} %collective-permute-done.refs_4_.refs_5_, f32[232,128]{1,0:T(8,128)} %kick.1.refs_2_.refs_3_.refs_4_.refs_5_), kind=kLoop, calls=%fused_computation | loop fusion | flops 59392 | bytes 475136 | tf_op jit(solution)/shard_map/concatenate | solution.py:483
  9.5 0.0 copy-done
  9.5 3.4 %collective-permute-start.2 = (f32[464,128]{1,0:T(8,128)S(1)}, f32[464,128]{1,0:T(8,128)S(1)}, u32[]{:S(2)}, u32[]{:S(2)}) collective-permute-start(f32[464,128]{1,0:T(8,128)S(1)} %pad_maximum_fusion), channel_id=1, source_target_pairs={{0,30},{2,0},{4,2},{6,4},{8,6},{10,8},{12,10},{14,12},{16,14},{18,... | collective-permute-start | bytes 712712 | tf_op jit(solution)/shard_map/ppermute | solution.py:485
  13.0 0.0 collective-permute-start.1
  13.0 0.0 copy-done.6
  13.0 0.6 fusion
  16.3 0.6 pad_maximum_fusion.2.refs_1_
  16.9 0.6 pad_add_fusion.1.refs_0_
  17.5 4.8 %pairs_1_0.1.refs_5_ = f32[96,128]{1,0:T(8,128)} custom-call(s32[2]{0:T(128)} %pad_add_fusion.1.refs_0_, f32[2]{0:T(128)} %pad_maximum_fusion.2.refs_1_, f32[232,128]{1,0:T(8,128)} %kick.1.refs_2_.refs_3_.refs_4_.refs_5_, f32[232,128]{1,0:T(8,128)} %kick.1.refs_2_.refs_3_.refs_4_.refs_5_, f32[232,128]{1,0:T(8,128)} %kick.1.refs_2_.refs_3_.refs_4_.refs_5_), custom_call_target="tpu_custom_call" | custom-call | flops 4000000 | bytes 1 | tf_op jit(solution)/shard_map/pairs_1_0/pallas_call | solution.py:399
  22.3 5.2 %pairs_2_0.1.refs_6_ = f32[96,128]{1,0:T(8,128)} custom-call(s32[2]{0:T(128)} %pad_add_fusion.1.refs_0_, f32[2]{0:T(128)} %pad_maximum_fusion.2.refs_1_, f32[232,128]{1,0:T(8,128)} %kick.1.refs_2_.refs_3_.refs_4_.refs_5_, f32[232,128]{1,0:T(8,128)} %kick.1.refs_2_.refs_3_.refs_4_.refs_5_, f32[232,128]{1,0:T(8,128)} %copy-done, f32[96,128]{1,0:T(8,128)} %pairs_1_0.1.refs_5_), custom_call_target="tpu_custom_call" | custom-call | flops 4000000 | bytes 1 | tf_op jit(solution)/shard_map/pairs_2_0/pallas_call | solution.py:399
  27.4 0.0 collective-permute-done.2.refs_5_.refs_7_
  27.4 0.0 collective-permute-done.1.refs_4_.refs_6_
  27.5 0.7 copy-done.1
  28.1 0.7 copy-done.2
  28.8 9.8 %pairs_6_0.1.refs_2_.refs_4_ = f32[192,128]{1,0:T(8,128)} custom-call(s32[2]{0:T(128)} %pad_add_fusion.1.refs_0_, f32[2]{0:T(128)} %pad_maximum_fusion.2.refs_1_, f32[232,128]{1,0:T(8,128)} %kick.1.refs_2_.refs_3_.refs_4_.refs_5_, f32[232,128]{1,0:T(8,128)} %kick.1.refs_2_.refs_3_.refs_4_.refs_5_, f32[464,128]{1,0:T(8,128)} %copy-done.2, ...), custom_call_target="tpu_custom_call" | custom-call | flops 8000000 | bytes 1 | tf_op jit(solution)/shard_map/pairs_6_0/pallas_call | solution.py:399
  38.7 1.6 %collective-permute-start.3 = (f32[192,128]{1,0:T(8,128)}, f32[192,128]{1,0:T(8,128)S(1)}, u32[]{:S(2)}, u32[]{:S(2)}) collective-permute-start(f32[192,128]{1,0:T(8,128)} %pairs_6_0.1.refs_2_.refs_4_), channel_id=1, source_target_pairs={{0,1},{1,0},{2,3},{3,2},{4,5},{5,4},{6,7},{7,6},{8,9},{9,8},{10,11... | collective-permute-start | bytes 294920 | tf_op jit(solution)/shard_map/ppermute | solution.py:479
  40.3 3.2 %collective-permute-done.3.refs_4_ = f32[192,128]{1,0:T(8,128)S(1)} collective-permute-done((f32[192,128]{1,0:T(8,128)}, f32[192,128]{1,0:T(8,128)S(1)}, u32[]{:S(2)}, u32[]{:S(2)}) %collective-permute-start.3) | collective-permute-done | bytes 98336 | tf_op jit(solution)/shard_map/ppermute | solution.py:479
  43.5 0.9 %pad_maximum_fusion.1 = f32[384,128]{1,0:T(8,128)S(1)} fusion(f32[192,128]{1,0:T(8,128)S(1)} %collective-permute-done.3.refs_4_, f32[192,128]{1,0:T(8,128)} %pairs_6_0.1.refs_2_.refs_4_), kind=kLoop, calls=%fused_computation.1 | loop fusion | flops 49152 | bytes 393216 | tf_op jit(solution)/shard_map/concatenate | solution.py:483
  44.5 4.0 %collective-permute-start.5 = (f32[384,128]{1,0:T(8,128)S(1)}, f32[384,128]{1,0:T(8,128)S(1)}, u32[]{:S(2)}, u32[]{:S(2)}) collective-permute-start(f32[384,128]{1,0:T(8,128)S(1)} %pad_maximum_fusion.1), channel_id=1, source_target_pairs={{0,30},{2,0},{4,2},{6,4},{8,6},{10,8},{12,10},{14,12},{16,14},{18,... | collective-permute-start | bytes 589832 | tf_op jit(solution)/shard_map/ppermute | solution.py:485
  48.5 0.0 collective-permute-start.4
  51.0 0.6 pad_add_fusion.refs_0_
  51.7 5.0 %pairs_1_1.1 = (f32[96,128]{1,0:T(8,128)}, f32[48,128]{1,0:T(8,128)}) custom-call(s32[2]{0:T(128)} %pad_add_fusion.refs_0_, f32[2]{0:T(128)} %pad_maximum_fusion.2.refs_1_, f32[192,128]{1,0:T(8,128)} %pairs_6_0.1.refs_2_.refs_4_, f32[232,128]{1,0:T(8,128)} %kick.1.refs_2_.refs_3_.refs_4_.refs_5_, f32[192,128]{1,0:T(8,128)} %pairs_6_0.1.refs_2_.refs_4_, ...), custom_call_target="tpu_custom_call" | custom-call | flops 4000000 | bytes 1 | tf_op jit(solution)/shard_map/pairs_1_1/pallas_call | solution.py:399
  56.7 5.4 %pairs_2_1.1 = (f32[96,128]{1,0:T(8,128)}, f32[48,128]{1,0:T(8,128)}) custom-call(s32[2]{0:T(128)} %pad_add_fusion.refs_0_, f32[2]{0:T(128)} %pad_maximum_fusion.2.refs_1_, f32[192,128]{1,0:T(8,128)} %pairs_6_0.1.refs_2_.refs_4_, f32[232,128]{1,0:T(8,128)} %kick.1.refs_2_.refs_3_.refs_4_.refs_5_, f32[192,128]{1,0:T(8,128)} %copy-done.3, f32[232,128]{1,0:T(8,128)} %copy-done, ...), custom_call_target="tpu_custom_call" | custom-call | flops 4000000 | bytes 1 | tf_op jit(solution)/shard_map/pairs_2_1/pallas_call | solution.py:399
  62.1 0.0 collective-permute-done.5.refs_5_
  62.1 0.0 collective-permute-done.4.refs_4_
  62.1 0.7 copy-done.4
  62.7 0.1 copy-done.5
  62.8 10.0 %pairs_6_1.1 = (f32[96,128]{1,0:T(8,128)}, f32[96,128]{1,0:T(8,128)}, f32[6,128]{1,0:T(8,128)}) custom-call(s32[2]{0:T(128)} %pad_add_fusion.refs_0_, f32[2]{0:T(128)} %pad_maximum_fusion.2.refs_1_, f32[192,128]{1,0:T(8,128)} %pairs_6_0.1.refs_2_.refs_4_, f32[232,128]{1,0:T(8,128)} %kick.1.refs_2_.refs_3_.refs_4_.refs_5_, f32[384,128]{1,0:T(8,128)} %copy-done.5, ...), custom_call_target="tpu_custom_call" | custom-call | flops 8000000 | bytes 1 | tf_op jit(solution)/shard_map/pairs_6_1/pallas_call | solution.py:399
  72.8 1.3 %copy.11 = f32[6,1,1,128]{3,2,1,0:T(1,128)} copy(f32[6,1,1,128]{3,0,2,1:T(8,128)} %bitcast.24) | data formatting | bytes 6144
  (8 shorter events, 0.0 us)
Async XLA Ops:
  2.2 10.8 %copy-start.6 = (s32[2]{0:T(128)S(1)}, s32[2]{0:T(128)}, u32[]{:S(2)}) copy-start(s32[2]{0:T(128)} %param.11) | copy-start | bytes 28
  2.2 6.4 %collective-permute-start = (f32[232,128]{1,0:T(8,128)}, f32[232,128]{1,0:T(8,128)S(1)}, u32[]{:S(2)}, u32[]{:S(2)}) collective-permute-start(f32[232,128]{1,0:T(8,128)} %kick.1.refs_2_.refs_3_.refs_4_.refs_5_), channel_id=1, source_target_pairs={{0,1},{1,0},{2,3},{3,2},{4,5},{5,4},{6,7},{7,6},{8,9},{9,8},{10,11... | collective-permute-start | bytes 356360 | tf_op jit(solution)/shard_map/ppermute | solution.py:479
  8.6 1.0 %copy-start = (f32[232,128]{1,0:T(8,128)}, f32[232,128]{1,0:T(8,128)S(1)}, u32[]{:S(2)}) copy-start(f32[232,128]{1,0:T(8,128)S(1)} %collective-permute-done.refs_4_.refs_5_) | copy-start | bytes 356356
  9.5 17.9 %collective-permute-start.2 = (f32[464,128]{1,0:T(8,128)S(1)}, f32[464,128]{1,0:T(8,128)S(1)}, u32[]{:S(2)}, u32[]{:S(2)}) collective-permute-start(f32[464,128]{1,0:T(8,128)S(1)} %pad_maximum_fusion), channel_id=1, source_target_pairs={{0,30},{2,0},{4,2},{6,4},{8,6},{10,8},{12,10},{14,12},{16,14},{18,... | collective-permute-start | bytes 712712 | tf_op jit(solution)/shard_map/ppermute | solution.py:485
  13.0 14.5 %collective-permute-start.1 = (f32[464,128]{1,0:T(8,128)S(1)}, f32[464,128]{1,0:T(8,128)S(1)}, u32[]{:S(2)}, u32[]{:S(2)}) collective-permute-start(f32[464,128]{1,0:T(8,128)S(1)} %pad_maximum_fusion), channel_id=1, source_target_pairs={{0,2},{2,4},{4,6},{6,8},{8,10},{10,12},{12,14},{14,16},{16,18},{18... | collective-permute-start | bytes 712712 | tf_op jit(solution)/shard_map/ppermute | solution.py:484
  27.4 0.7 copy-start.1
  28.1 0.7 copy-start.2
  38.7 4.8 %collective-permute-start.3 = (f32[192,128]{1,0:T(8,128)}, f32[192,128]{1,0:T(8,128)S(1)}, u32[]{:S(2)}, u32[]{:S(2)}) collective-permute-start(f32[192,128]{1,0:T(8,128)} %pairs_6_0.1.refs_2_.refs_4_), channel_id=1, source_target_pairs={{0,1},{1,0},{2,3},{3,2},{4,5},{5,4},{6,7},{7,6},{8,9},{9,8},{10,11... | collective-permute-start | bytes 294920 | tf_op jit(solution)/shard_map/ppermute | solution.py:479
  43.5 0.9 %copy-start.3 = (f32[192,128]{1,0:T(8,128)}, f32[192,128]{1,0:T(8,128)S(1)}, u32[]{:S(2)}) copy-start(f32[192,128]{1,0:T(8,128)S(1)} %collective-permute-done.3.refs_4_) | copy-start | bytes 294916
  44.5 17.6 %collective-permute-start.5 = (f32[384,128]{1,0:T(8,128)S(1)}, f32[384,128]{1,0:T(8,128)S(1)}, u32[]{:S(2)}, u32[]{:S(2)}) collective-permute-start(f32[384,128]{1,0:T(8,128)S(1)} %pad_maximum_fusion.1), channel_id=1, source_target_pairs={{0,30},{2,0},{4,2},{6,4},{8,6},{10,8},{12,10},{14,12},{16,14},{18,... | collective-permute-start | bytes 589832 | tf_op jit(solution)/shard_map/ppermute | solution.py:485
  48.5 13.6 %collective-permute-start.4 = (f32[384,128]{1,0:T(8,128)S(1)}, f32[384,128]{1,0:T(8,128)S(1)}, u32[]{:S(2)}, u32[]{:S(2)}) collective-permute-start(f32[384,128]{1,0:T(8,128)S(1)} %pad_maximum_fusion.1), channel_id=1, source_target_pairs={{0,2},{2,4},{4,6},{6,8},{8,10},{10,12},{12,14},{14,16},{16,18},{18... | collective-permute-start | bytes 589832 | tf_op jit(solution)/shard_map/ppermute | solution.py:484
  62.1 0.7 copy-start.4
  62.1 0.7 copy-start.5

commit v2 on v1

--- a/solution.py
+++ b/solution.py
@@ -28,6 +28,8 @@
 SEED_MIDDLE = 8192
 F32 = jnp.float32
 SUB = 8
+VMEM_LIMIT = 6 * 2**20
+KICK_LIMIT = 67043328 - 160 * 1024
 
 
 def take_rows(values, index):
@@ -74,7 +76,7 @@
 ):
     refs = list(refs)
     take = lambda n: [refs.pop(0) for _ in range(n)]
-    turn_ref, shear_ref, home_ref, home_fixed_ref = take(4)
+    offset_ref, home_ref, home_fixed_ref = take(3)
     near_refs = take(sources)
     fixed_refs = take(sources) if has_fixed else near_refs
     force_in = None if first else take(1)[0]
@@ -91,6 +93,18 @@
     iota = lax.broadcasted_iota(jnp.int32, (SUB, lanes), 0)
     iota_f = iota.astype(F32)
     fixed_at = 6 * slots
+    turns = shears = None
+    if any(dy for _, _, _, dy in rows):
+        index, count = lax.axis_index("xy"), lax.axis_size("xy")
+        amount = offset_ref[step]
+        turns = (
+            jnp.where((index == 0) & (amount > 0), lanes - amount, 0),
+            jnp.where(index == count - 1, amount, 0),
+        )
+        shears = (
+            jnp.where(index == 0, F32(-SHEAR_SPEED), F32(0.0)),
+            jnp.where(index == count - 1, F32(SHEAR_SPEED), F32(0.0)),
+        )
 
     def block(ref, base, group):
         return ref[base + group * SUB : base + (group + 1) * SUB, :]
@@ -124,7 +138,7 @@
     for r, (source, offset, dz, dy) in enumerate(rows):
         data, fixed = near_refs[source], fixed_refs[source]
         base = r * 7 * slots
-        amount = turn_ref[0 if dy < 0 else 1] if dy else None
+        amount = turns[0 if dy < 0 else 1] if dy else None
         turned = (lambda v: pltpu.roll(v, amount, 1)) if dy else (lambda v: v)
         count = turned(spread(fixed[offset[1] + fixed_at + slots : offset[1] + fixed_at + slots + 1, :]))
         for g in range(groups):
@@ -139,7 +153,7 @@
                 if c == 2 and dz:
                     v = v + F32(EDGE * dz)
                 if c == 3 and dy:
-                    v = v + shear_ref[0 if dy < 0 else 1]
+                    v = v + shears[0 if dy < 0 else 1]
                 if 3 <= c < 6:
                     v = v * F32(VELOCITY_SCALE)
                 near[base + c * slots + g * SUB : base + c * slots + (g + 1) * SUB, :] = v
@@ -224,8 +238,7 @@
                 rx, ry, rz = h[0] - n[0], h[1] - n[1], h[2] - n[2]
                 squared = jnp.maximum(rx * rx + ry * ry + rz * rz, FLOOR_SQUARED)
                 inverse = lax.rsqrt(squared)
-                weight = jnp.maximum(1.0 - squared * inverse, 0.0)
-                u = weight * inverse
+                u = jnp.maximum(inverse - 1.0, 0.0)
                 rv = rx * (h[3] - n[3]) + ry * (h[4] - n[4]) + rz * (h[5] - n[5])
                 t = ((h[6] * n[6] + h[7] * n[7]) + (h[8] + n[8])) * F32(INVERSE)
                 y = (t - jnp.floor(t)) + F32(SHIFT)
@@ -367,25 +380,25 @@
         for i in range(6):
             v = tally[i * SUB : (i + 1) * SUB, :]
             if last:
-                virial_out[i : i + 1, :] = jnp.sum(v, axis=0, keepdims=True) * F32(
+                virial_out[i] = jnp.sum(v, axis=0, keepdims=True) * F32(
                     NOISE_UNIT * 0.5 / CELL_VOLUME
                 )
             else:
                 virial_out[i * SUB : (i + 1) * SUB, :] = v
 
 
-def pairs(turn, shear, home, home_fixed, nears, fixed, carried, rows, step, last, virial, slots, cost):
+def pairs(offsets, home, home_fixed, nears, fixed, carried, rows, step, last, virial, slots, cost):
     lanes = home.shape[-1]
     own = len(rows) == 1
     first = carried is None
-    operands = [turn, shear, home, home_fixed, *nears]
+    operands = [offsets, home, home_fixed, *nears]
     if fixed is not None:
         operands += list(fixed)
     if not first:
         operands += list(carried)
     shape = lambda n: jax.ShapeDtypeStruct((n, lanes), F32)
     if last and virial:
-        outs = (shape(3 * slots), shape(3 * slots), shape(6))
+        outs = (shape(3 * slots), shape(3 * slots), jax.ShapeDtypeStruct((6, 1, lanes), F32))
     elif virial:
         outs = (shape(3 * slots), shape(6 * SUB))
     elif last:
@@ -411,7 +424,7 @@
             has_fixed=fixed is not None,
         ),
         out_shape=outs,
-        in_specs=[smem, smem] + [vmem] * (len(operands) - 2),
+        in_specs=[smem] + [vmem] * (len(operands) - 1),
         out_specs=tuple(vmem for _ in outs),
         scratch_shapes=[
             pltpu.VMEM((9 * slots, lanes), F32),
@@ -425,12 +438,23 @@
             pltpu.VMEM((6 * SUB, lanes), F32),
             pltpu.SMEM((4 * count,), jnp.int32),
         ],
+        compiler_params=pltpu.CompilerParams(vmem_limit_bytes=VMEM_LIMIT),
         cost_estimate=pl.CostEstimate(flops=cost, bytes_accessed=1, transcendentals=0),
         name=f"pairs_{count}_{step}",
     )(*operands)
 
 
-def kick_kernel(position, velocity, force, seed, count, out, *, slots, lanes):
+def kick_kernel(*refs, slots, lanes):
+    sources, out, held, done = refs[:5], refs[5], refs[6:11], refs[11]
+    copies = [
+        pltpu.make_async_copy(source, target, done.at[i])
+        for i, (source, target) in enumerate(zip(sources, held))
+    ]
+    for copy in copies:
+        copy.start()
+    for copy in copies:
+        copy.wait()
+    position, velocity, force, seed, count = held
     for c in range(3):
         for g in range(slots // SUB):
             at = c * slots + g * SUB
@@ -450,67 +474,62 @@
     slots, depth, width, lanes = seeds.shape
     assert depth == 1 and width == 1
     gz, xy = lax.axis_size("gz"), lax.axis_size("xy")
-    index = lax.axis_index("xy")
     flat = lambda a: a.reshape(-1, lanes)
     tall = 7 * slots + SUB
+    inputs = [flat(a) for a in (positions, velocities, forces_prev, seeds, counts)]
     state = pl.pallas_call(
         functools.partial(kick_kernel, slots=slots, lanes=lanes),
         out_shape=jax.ShapeDtypeStruct((tall, lanes), F32),
-        in_specs=[pl.BlockSpec(memory_space=pltpu.VMEM)] * 5,
+        in_specs=[pl.BlockSpec(memory_space=pltpu.HBM)] * 5,
         out_specs=pl.BlockSpec(memory_space=pltpu.VMEM),
+        scratch_shapes=[pltpu.VMEM(a.shape, a.dtype) for a in inputs]
+        + [pltpu.SemaphoreType.DMA((5,))],
+        compiler_params=pltpu.CompilerParams(vmem_limit_bytes=KICK_LIMIT),
         name="kick",
-    )(flat(positions), flat(velocities), flat(forces_prev), flat(seeds), flat(counts))
-    first_lower, first_upper = index == 0, index == xy - 1
-    shear = jnp.stack(
-        [jnp.where(first_lower, -SHEAR_SPEED, 0.0), jnp.where(first_upper, SHEAR_SPEED, 0.0)]
-    ).astype(F32)
+    )(*inputs)
     home_fixed = state
     kept = None
     for step in range(2):
-        offset = offsets[step]
-        turn = jnp.stack(
-            [
-                jnp.where(first_lower, (lanes - offset) % lanes, 0),
-                jnp.where(first_upper, offset % lanes, 0),
-            ]
-        ).astype(jnp.int32)
         final = step == 1
         high = state.shape[0]
         planes = [lax.ppermute(state, "gz", ring(gz, -1))]
         if gz > 2:
             planes.append(lax.ppermute(state, "gz", ring(gz, 1)))
         up, down = 0, len(planes) - 1
+        near_fixed = lambda at: None if not final else kept[at]
+        call = functools.partial(
+            pairs, offsets, state, home_fixed, step=step, virial=final, slots=slots
+        )
+        here = (0, 0)
+        carried = call(
+            [state],
+            [home_fixed] if final else None,
+            None,
+            rows=((0, here, 0, 0),),
+            last=False,
+            cost=100_000_000,
+        )
+        planes, carried = lax.optimization_barrier((planes, carried))
         stacked = jnp.concatenate([state, *planes], axis=0)
         lower = lax.ppermute(stacked, "xy", ring(xy, 1))
         upper = lax.ppermute(stacked, "xy", ring(xy, -1))
-        if not final:
-            kept = (planes, lower, upper)
-            fixed = [None] * 3
-        else:
-            fixed = [[home_fixed], kept[0], [kept[1], kept[2]]]
-        call = functools.partial(
-            pairs, turn, shear, state, home_fixed, step=step, virial=final, slots=slots
-        )
-        here = (0, 0)
-        carried = call(
-            [state], fixed[0], None, rows=((0, here, 0, 0),), last=False, cost=4_000_000
-        )
         carried = call(
             planes,
-            fixed[1],
+            near_fixed(0),
             carried,
             rows=((down, here, -1, 0), (up, here, 1, 0)),
             last=False,
-            cost=4_000_000,
+            cost=100_000_000,
         )
         rows = []
         for source, dy in ((0, -1), (1, 1)):
             for dz, place in ((0, 0), (-1, 1 + down), (1, 1 + up)):
                 rows.append((source, (place * high, place * tall), dz, dy))
         outs = call(
-            [lower, upper], fixed[2], carried, rows=tuple(rows), last=True, cost=8_000_000
+            [lower, upper], near_fixed(1), carried, rows=tuple(rows), last=True, cost=200_000_000
         )
         if not final:
+            kept = (planes, [lower, upper])
             state = outs[0]
     force, velocity, stress = outs
     return (

time: 75.3 us -> 53.5 us (0.71); the launches traced: 74.1 us -> 53.6 us
  between operations: 5.9 us -> 0.74 us
  Pallas kernels: 41.6 us -> 36.7 us
  starting transfers between devices: 12.1 us -> 8.29 us
  other arithmetic: 3.78 us -> 0.03 us
  local copies, waits for them, and re-layouts: 4.03 us -> 0.94 us
    ppermute x2, waiting for transfers between devices: 0.01 us -> 6.87 us  [shards(): lower = lax.ppermute(stacked, 'xy', ring(xy, 1))]
    ppermute x2, waiting for transfers between devices: 6.63 us -> 0.01 us  [shards(): planes = [lax.ppermute(state, 'gz', ring(gz, -1))]]
    pallas_call x6, Pallas kernels: 40.1 us -> 35.1 us  [pairs(): pl.pallas_call(functools.partial(pair_kernel, slots=slots, lanes=lanes, s...]
    ppermute x2, starting transfers between devices: 7.46 us -> 3.67 us  [shards(): upper = lax.ppermute(stacked, 'xy', ring(xy, -1))]
    unnamed x15 -> x6, local copies, waits for them, and re-layouts: 3.38 us -> 0.94 us
    another operation x3 -> x0, other arithmetic: 1.88 us -> none  [the longest x2 1.23 us: shards(): jnp.stack([jnp.where(first_lower, (lanes - offset) % lanes, 0), jnp.where...]
    concatenate x2, other arithmetic: 1.9 us -> 0.03 us  [shards(): stacked = jnp.concatenate([state, *planes], axis=0)]
  transfers between devices with their start and end apart: 6 -> 6, of which waited for: 2 -> 2; matrix products, arithmetic and copies ran while one was open for 3% -> 0% of each run, Pallas kernels for 27% -> 30%
where the time goes in v2:
time: 53.5 us; the launch traced here: 53.6 us
  Pallas kernels  36.7 us (69%)
  starting transfers between devices  8.29 us (15%)
  waiting for transfers between devices  6.88 us (13%)
  local copies, waits for them, and re-layouts  0.94 us (2%)
  between operations  0.74 us (1%)
    pallas_call x6, Pallas kernels, pairs(): pl.pallas_call(functools.partial(pair_kernel, slots=slots, lanes=lanes, s...  35.1 us
    ppermute x2, waiting for transfers between devices, shards(): lower = lax.ppermute(stacked, 'xy', ring(xy, 1))  6.87 us
    ppermute x2, starting transfers between devices, shards(): planes = [lax.ppermute(state, 'gz', ring(gz, -1))]  4.12 us
    ppermute x2, starting transfers between devices, shards(): upper = lax.ppermute(stacked, 'xy', ring(xy, -1))  3.67 us
    pallas_call x1, Pallas kernels, shards(): pl.pallas_call(functools.partial(kick_kernel, slots=slots, lanes=lanes),...  1.54 us
  transfers between devices with their start and end apart: 6, of which 2 were waited for; matrix products, arithmetic and copies ran while one was open for 0% of the time, Pallas kernels for 30%

profile of v2, /device:TPU:0, one launch (start us, length us, event | category | flops | bytes accessed | tf_op | source)
XLA Modules:
  0.0 53.6 jit_solution(11516071911168463437)
XLA Ops:
  0.6 0.0 copy-start.2
  0.6 1.5 %kick.1.refs_1_.refs_2_.refs_3_.refs_4_ = f32[232,128]{1,0:T(8,128)} custom-call(f32[96,128]{1,0:T(8,128)} %bitcast.14, f32[96,128]{1,0:T(8,128)} %bitcast.15, f32[96,128]{1,0:T(8,128)} %bitcast.16, s32[32,128]{1,0:T(8,128)} %bitcast.17, s32[1,128]{1,0:T(1,128)} %bitcast.18), custom_call_target="tpu_custom_call" | custom-call | tf_op jit(solution)/shard_map/kick/pallas_call | solution.py:480
  2.2 3.0 %collective-permute-start = (f32[232,128]{1,0:T(8,128)}, f32[232,128]{1,0:T(8,128)S(1)}, u32[]{:S(2)}, u32[]{:S(2)}) collective-permute-start(f32[232,128]{1,0:T(8,128)} %kick.1.refs_1_.refs_2_.refs_3_.refs_4_), channel_id=1, source_target_pairs={{0,1},{1,0},{2,3},{3,2},{4,5},{5,4},{6,7},{7,6},{8,9},{9,8},{10,11... | collective-permute-start | bytes 356360 | tf_op jit(solution)/shard_map/ppermute | solution.py:495
  5.2 0.0 copy-done.2
  5.2 0.0 copy-start
  5.2 0.9 %copy-done = f32[232,128]{1,0:T(8,128)S(1)} copy-done((f32[232,128]{1,0:T(8,128)S(1)}, f32[232,128]{1,0:T(8,128)}, u32[]{:S(2)}) %copy-start) | copy-done | bytes 118808
  6.2 0.0 copy-start.1
  6.2 3.6 %pairs_1_0.1.refs_4_ = f32[96,128]{1,0:T(8,128)S(1)} custom-call(s32[2]{0:T(128)S(1)} %copy-done.2, f32[232,128]{1,0:T(8,128)S(1)} %copy-done, f32[232,128]{1,0:T(8,128)S(1)} %copy-done, f32[232,128]{1,0:T(8,128)S(1)} %copy-done), custom_call_target="tpu_custom_call" | custom-call | flops 100000000 | bytes 1 | tf_op jit(solution)/shard_map/pairs_1_0/pallas_call | solution.py:412
  9.7 0.0 collective-permute-done.refs_3_.refs_4_
  9.8 0.0 copy-done.1
  9.8 3.6 %collective-permute-start.2 = (f32[464,128]{1,0:T(8,128)S(1)}, f32[464,128]{1,0:T(8,128)S(1)}, u32[]{:S(2)}, u32[]{:S(2)}) collective-permute-start(f32[464,128]{1,0:T(8,128)S(1)} %pad_maximum_fusion), channel_id=1, source_target_pairs={{0,30},{2,0},{4,2},{6,4},{8,6},{10,8},{12,10},{14,12},{16,14},{18,... | collective-permute-start | bytes 712712 | tf_op jit(solution)/shard_map/ppermute | solution.py:515
  13.4 0.0 collective-permute-start.1
  13.4 4.2 %pairs_2_0.1.refs_5_ = f32[96,128]{1,0:T(8,128)S(1)} custom-call(s32[2]{0:T(128)S(1)} %copy-done.2, f32[232,128]{1,0:T(8,128)S(1)} %copy-done.1, f32[232,128]{1,0:T(8,128)S(1)} %copy-done.1, f32[232,128]{1,0:T(8,128)S(1)} %collective-permute-done.refs_3_.refs_4_, f32[96,128]{1,0:T(8,128)S(1)} %pairs_1_0.1.refs_4_), custom_call_target="tpu_custom_call" | custom-call | flops 100000000 | bytes 1 | tf_op jit(solution)/shard_map/pairs_2_0/pallas_call | solution.py:412
  17.6 0.0 collective-permute-done.2.refs_4_.refs_6_
  17.7 4.0 %collective-permute-done.1.refs_3_.refs_5_ = f32[464,128]{1,0:T(8,128)S(1)} collective-permute-done((f32[464,128]{1,0:T(8,128)S(1)}, f32[464,128]{1,0:T(8,128)S(1)}, u32[]{:S(2)}, u32[]{:S(2)}) %collective-permute-start.1) | collective-permute-done | bytes 237600 | tf_op jit(solution)/shard_map/ppermute | solution.py:514
  21.6 9.0 %pairs_6_0.1.refs_1_.refs_3_ = f32[192,128]{1,0:T(8,128)S(1)} custom-call(s32[2]{0:T(128)S(1)} %copy-done.2, f32[232,128]{1,0:T(8,128)S(1)} %copy-done.1, f32[232,128]{1,0:T(8,128)S(1)} %copy-done.1, f32[464,128]{1,0:T(8,128)S(1)} %collective-permute-done.1.refs_3_.refs_5_, f32[464,128]{1,0:T(8,128)S(1)} %collective-permute-done.2.refs_4_.refs_6_, ...), custom_call_target="tpu_custom_call" | custom-call | flops 200000000 | bytes 1 | tf_op jit(solution)/shard_map/pairs_6_0/pallas_call | solution.py:412
  30.7 1.1 %collective-permute-start.3 = (f32[192,128]{1,0:T(8,128)S(1)}, f32[192,128]{1,0:T(8,128)S(1)}, u32[]{:S(2)}, u32[]{:S(2)}) collective-permute-start(f32[192,128]{1,0:T(8,128)S(1)} %pairs_6_0.1.refs_1_.refs_3_), channel_id=1, source_target_pairs={{0,1},{1,0},{2,3},{3,2},{4,5},{5,4},{6,7},{7,6},{8,9},{9,8},{10,11... | collective-permute-start | bytes 294920 | tf_op jit(solution)/shard_map/ppermute | solution.py:495
  31.8 3.7 %pairs_1_1.1 = (f32[96,128]{1,0:T(8,128)S(1)}, f32[48,128]{1,0:T(8,128)S(1)}) custom-call(s32[2]{0:T(128)S(1)} %copy-done.2, f32[192,128]{1,0:T(8,128)S(1)} %pairs_6_0.1.refs_1_.refs_3_, f32[232,128]{1,0:T(8,128)S(1)} %copy-done.1, f32[192,128]{1,0:T(8,128)S(1)} %pairs_6_0.1.refs_1_.refs_3_, f32[232,128]{1,0:T(8,128)S(1)} %copy-done.1), custom_call_target="tpu_custom_call" | custom-call | flops 100000000 | bytes 1 | tf_op jit(solution)/shard_map/pairs_1_1/pallas_call | solution.py:412
  35.4 0.0 collective-permute-done.3.refs_3_
  35.4 0.1 collective-permute-start.5
  35.5 0.5 collective-permute-start.4
  36.0 4.4 %pairs_2_1.1 = (f32[96,128]{1,0:T(8,128)S(1)}, f32[48,128]{1,0:T(8,128)S(1)}) custom-call(s32[2]{0:T(128)S(1)} %copy-done.2, f32[192,128]{1,0:T(8,128)S(1)} %pairs_6_0.1.refs_1_.refs_3_, f32[232,128]{1,0:T(8,128)S(1)} %copy-done.1, f32[192,128]{1,0:T(8,128)S(1)} %collective-permute-done.3.refs_3_, f32[232,128]{1,0:T(8,128)S(1)} %collective-permute-done.refs_3_.refs_4_, ...), custom_call_target="tpu_custom_call" | custom-call | flops 100000000 | bytes 1 | tf_op jit(solution)/shard_map/pairs_2_1/pallas_call | solution.py:412
  40.5 0.0 collective-permute-done.5.refs_4_
  40.5 2.9 %collective-permute-done.4.refs_3_ = f32[384,128]{1,0:T(8,128)S(1)} collective-permute-done((f32[384,128]{1,0:T(8,128)S(1)}, f32[384,128]{1,0:T(8,128)S(1)}, u32[]{:S(2)}, u32[]{:S(2)}) %collective-permute-start.4) | collective-permute-done | bytes 196640 | tf_op jit(solution)/shard_map/ppermute | solution.py:514
  43.4 10.2 %pairs_6_1.1 = (f32[96,128]{1,0:T(8,128)}, f32[96,128]{1,0:T(8,128)}, f32[6,1,128]{2,1,0:T(1,128)}) custom-call(s32[2]{0:T(128)S(1)} %copy-done.2, f32[192,128]{1,0:T(8,128)S(1)} %pairs_6_0.1.refs_1_.refs_3_, f32[232,128]{1,0:T(8,128)S(1)} %copy-done.1, f32[384,128]{1,0:T(8,128)S(1)} %collective-permute-done.4.refs_3_, ...), custom_call_target="tpu_custom_call" | custom-call | flops 200000000 | bytes 1 | tf_op jit(solution)/shard_map/pairs_6_1/pallas_call | solution.py:412
  (2 shorter events, 0.0 us)
Async XLA Ops:
  0.6 4.6 %copy-start.2 = (s32[2]{0:T(128)S(1)}, s32[2]{0:T(128)}, u32[]{:S(2)}) copy-start(s32[2]{0:T(128)} %refs_0_.11) | copy-start | bytes 28
  2.2 7.6 %collective-permute-start = (f32[232,128]{1,0:T(8,128)}, f32[232,128]{1,0:T(8,128)S(1)}, u32[]{:S(2)}, u32[]{:S(2)}) collective-permute-start(f32[232,128]{1,0:T(8,128)} %kick.1.refs_1_.refs_2_.refs_3_.refs_4_), channel_id=1, source_target_pairs={{0,1},{1,0},{2,3},{3,2},{4,5},{5,4},{6,7},{7,6},{8,9},{9,8},{10,11... | collective-permute-start | bytes 356360 | tf_op jit(solution)/shard_map/ppermute | solution.py:495
  5.2 0.9 %copy-start = (f32[232,128]{1,0:T(8,128)S(1)}, f32[232,128]{1,0:T(8,128)}, u32[]{:S(2)}) copy-start(f32[232,128]{1,0:T(8,128)} %kick.1.refs_1_.refs_2_.refs_3_.refs_4_) | copy-start | bytes 356356
  6.2 3.6 %copy-start.1 = (f32[232,128]{1,0:T(8,128)S(1)}, f32[232,128]{1,0:T(8,128)}, u32[]{:S(2)}) copy-start(f32[232,128]{1,0:T(8,128)} %kick.1.refs_1_.refs_2_.refs_3_.refs_4_) | copy-start | bytes 356356
  9.8 7.9 %collective-permute-start.2 = (f32[464,128]{1,0:T(8,128)S(1)}, f32[464,128]{1,0:T(8,128)S(1)}, u32[]{:S(2)}, u32[]{:S(2)}) collective-permute-start(f32[464,128]{1,0:T(8,128)S(1)} %pad_maximum_fusion), channel_id=1, source_target_pairs={{0,30},{2,0},{4,2},{6,4},{8,6},{10,8},{12,10},{14,12},{16,14},{18,... | collective-permute-start | bytes 712712 | tf_op jit(solution)/shard_map/ppermute | solution.py:515
  13.4 8.2 %collective-permute-start.1 = (f32[464,128]{1,0:T(8,128)S(1)}, f32[464,128]{1,0:T(8,128)S(1)}, u32[]{:S(2)}, u32[]{:S(2)}) collective-permute-start(f32[464,128]{1,0:T(8,128)S(1)} %pad_maximum_fusion), channel_id=1, source_target_pairs={{0,2},{2,4},{4,6},{6,8},{8,10},{10,12},{12,14},{14,16},{16,18},{18... | collective-permute-start | bytes 712712 | tf_op jit(solution)/shard_map/ppermute | solution.py:514
  30.7 4.8 %collective-permute-start.3 = (f32[192,128]{1,0:T(8,128)S(1)}, f32[192,128]{1,0:T(8,128)S(1)}, u32[]{:S(2)}, u32[]{:S(2)}) collective-permute-start(f32[192,128]{1,0:T(8,128)S(1)} %pairs_6_0.1.refs_1_.refs_3_), channel_id=1, source_target_pairs={{0,1},{1,0},{2,3},{3,2},{4,5},{5,4},{6,7},{7,6},{8,9},{9,8},{10,11... | collective-permute-start | bytes 294920 | tf_op jit(solution)/shard_map/ppermute | solution.py:495
  35.4 5.0 %collective-permute-start.5 = (f32[384,128]{1,0:T(8,128)S(1)}, f32[384,128]{1,0:T(8,128)S(1)}, u32[]{:S(2)}, u32[]{:S(2)}) collective-permute-start(f32[384,128]{1,0:T(8,128)S(1)} %pad_maximum_fusion.1), channel_id=1, source_target_pairs={{0,30},{2,0},{4,2},{6,4},{8,6},{10,8},{12,10},{14,12},{16,14},{18,... | collective-permute-start | bytes 589832 | tf_op jit(solution)/shard_map/ppermute | solution.py:515
  35.5 7.8 %collective-permute-start.4 = (f32[384,128]{1,0:T(8,128)S(1)}, f32[384,128]{1,0:T(8,128)S(1)}, u32[]{:S(2)}, u32[]{:S(2)}) collective-permute-start(f32[384,128]{1,0:T(8,128)S(1)} %pad_maximum_fusion.1), channel_id=1, source_target_pairs={{0,2},{2,4},{4,6},{6,8},{8,10},{10,12},{12,14},{14,16},{16,18},{18... | collective-permute-start | bytes 589832 | tf_op jit(solution)/shard_map/ppermute | solution.py:514

commit v3 on v2

--- a/solution.py
+++ b/solution.py
@@ -26,8 +26,10 @@
 FAR = 1.0e15
 REACH = 1.001
 SEED_MIDDLE = 8192
+NEAR_SIDE, FAR_SIDE = 1, 2
 F32 = jnp.float32
 SUB = 8
+UNROLL = 4
 VMEM_LIMIT = 6 * 2**20
 KICK_LIMIT = 67043328 - 160 * 1024
 
@@ -72,7 +74,7 @@
 
 
 def pair_kernel(
-    *refs, slots, lanes, sources, rows, own, step, first, last, virial, has_fixed
+    *refs, slots, lanes, sources, rows, own, step, first, last, virial, has_fixed, side
 ):
     refs = list(refs)
     take = lambda n: [refs.pop(0) for _ in range(n)]
@@ -87,24 +89,25 @@
         force_out, virial_out = take(2)
     else:
         (force_out,) = take(1)
-    home, near, box, rank, pick, liste, part, total, tally, sizes = take(10)
+    home, near, answer, rank, pick, liste, part, total, tally, sizes = take(10)
     groups = slots // SUB
+    pitch = slots + SUB
     capacity = liste.shape[0] // 9
     iota = lax.broadcasted_iota(jnp.int32, (SUB, lanes), 0)
     iota_f = iota.astype(F32)
     fixed_at = 6 * slots
-    turns = shears = None
-    if any(dy for _, _, _, dy in rows):
+    if side:
         index, count = lax.axis_index("xy"), lax.axis_size("xy")
+        upper = (lax.rem(index, 2) == 0) == (side == NEAR_SIDE)
+        across = jnp.where(upper, F32(1.0), F32(-1.0))
+        wraps = jnp.where(upper, index == count - 1, index == 0)
         amount = offset_ref[step]
-        turns = (
-            jnp.where((index == 0) & (amount > 0), lanes - amount, 0),
-            jnp.where(index == count - 1, amount, 0),
-        )
-        shears = (
-            jnp.where(index == 0, F32(-SHEAR_SPEED), F32(0.0)),
-            jnp.where(index == count - 1, F32(SHEAR_SPEED), F32(0.0)),
-        )
+        turn = jnp.where(upper, amount, lax.rem(lanes - amount, lanes))
+        turn = jnp.where(wraps, turn, 0)
+        shear = jnp.where(wraps, across * F32(SHEAR_SPEED), F32(0.0))
+        turning = side != NEAR_SIDE
+    else:
+        turning = False
 
     def block(ref, base, group):
         return ref[base + group * SUB : base + (group + 1) * SUB, :]
@@ -123,24 +126,26 @@
             p = block(home_ref, a * slots, g)
             low[a] = jnp.minimum(low[a], jnp.where(there, p, FAR))
             high[a] = jnp.maximum(high[a], jnp.where(there, p, -FAR))
-            home[(a * slots + g * SUB) : (a * slots + (g + 1) * SUB), :] = (
+            home[(a * pitch + g * SUB) : (a * pitch + (g + 1) * SUB), :] = (
                 jnp.where(there, p, -FAR) if a == 0 else p
             )
-            home[((3 + a) * slots + g * SUB) : ((3 + a) * slots + (g + 1) * SUB), :] = (
+            home[((3 + a) * pitch + g * SUB) : ((3 + a) * pitch + (g + 1) * SUB), :] = (
                 block(home_ref, (3 + a) * slots, g) * F32(VELOCITY_SCALE)
             )
         for a, value in enumerate(home_noise(block(home_fixed_ref, fixed_at, g), step)):
-            at = (6 + a) * slots + g * SUB
+            at = (6 + a) * pitch + g * SUB
             home[at : at + SUB, :] = value
     home_low = [spread(jnp.min(v, axis=0, keepdims=True)) - REACH for v in low]
     home_high = [spread(jnp.max(v, axis=0, keepdims=True)) + REACH for v in high]
 
-    for r, (source, offset, dz, dy) in enumerate(rows):
+    reach = {}
+    for r, (source, offset, dz) in enumerate(rows):
         data, fixed = near_refs[source], fixed_refs[source]
-        base = r * 7 * slots
-        amount = turns[0 if dy < 0 else 1] if dy else None
-        turned = (lambda v: pltpu.roll(v, amount, 1)) if dy else (lambda v: v)
+        base = r * 7 * pitch
+        turned = (lambda v: pltpu.roll(v, turn, 1)) if turning else (lambda v: v)
         count = turned(spread(fixed[offset[1] + fixed_at + slots : offset[1] + fixed_at + slots + 1, :]))
+        reach_low = [jnp.full((SUB, lanes), FAR, F32) for _ in range(2)]
+        reach_high = [jnp.full((SUB, lanes), -FAR, F32) for _ in range(2)]
         for g in range(groups):
             there = iota_f + F32(g * SUB) < count
             for c in range(7):
@@ -148,36 +153,51 @@
                 v = turned(block(ref, at + c * slots, g))
                 if c == 0:
                     v = jnp.where(there, v, FAR)
-                if c == 1 and dy:
-                    v = v + F32(EDGE * dy)
+                if c == 1 and side:
+                    v = v + F32(EDGE) * across
                 if c == 2 and dz:
                     v = v + F32(EDGE * dz)
-                if c == 3 and dy:
-                    v = v + shears[0 if dy < 0 else 1]
+                if c == 3 and turning:
+                    v = v + shear
                 if 3 <= c < 6:
                     v = v * F32(VELOCITY_SCALE)
-                near[base + c * slots + g * SUB : base + c * slots + (g + 1) * SUB, :] = v
+                if c in (1, 2) and not own:
+                    a = c - 1
+                    reach_low[a] = jnp.minimum(reach_low[a], jnp.where(there, v, FAR))
+                    reach_high[a] = jnp.maximum(reach_high[a], jnp.where(there, v, -FAR))
+                near[base + c * pitch + g * SUB : base + c * pitch + (g + 1) * SUB, :] = v
+        if not own:
+            for a in range(2):
+                least = jnp.min(reach_low[a], axis=0, keepdims=True)
+                most = jnp.max(reach_high[a], axis=0, keepdims=True)
+                least, most = spread(least), spread(most)
+                least = jnp.minimum(least, jnp.minimum(pltpu.roll(least, 1, 1), pltpu.roll(least, lanes - 1, 1)))
+                most = jnp.maximum(most, jnp.maximum(pltpu.roll(most, 1, 1), pltpu.roll(most, lanes - 1, 1)))
+                reach[(r, a)] = (least - REACH, most + REACH)
+
+    below = lax.broadcasted_iota(jnp.int32, (slots, slots), 0) >= lax.broadcasted_iota(
+        jnp.int32, (slots, slots), 1
+    )
+    triangle = jnp.where(below, 1.0, 0.0).astype(jnp.bfloat16)
 
     def ranked(slot, marks):
-        before = jnp.zeros((SUB, lanes), F32)
+        ones = jnp.concatenate([jnp.where(m, 1.0, 0.0) for m in marks], axis=0)
+        upto = jnp.dot(triangle, ones.astype(jnp.bfloat16), preferred_element_type=F32)
         for g in range(groups):
-            run = jnp.where(marks[g], 1.0, 0.0)
-            for d in (1, 2, 4):
-                run = run + jnp.where(iota >= d, pltpu.roll(run, d, 0), 0.0)
-            place = jnp.where(marks[g], run + (before - 1.0), -1.0)
+            rows_of = slice(g * SUB, (g + 1) * SUB)
+            place = jnp.where(marks[g], upto[rows_of, :] - 1.0, -1.0)
             rank[(slot * slots + g * SUB) : (slot * slots + (g + 1) * SUB), :] = place
-            before = before + spread(run[SUB - 1 : SUB, :])
-        sizes[slot] = jnp.max(before).astype(jnp.int32)
-
-    for r, (source, offset, dz, dy) in enumerate(rows):
-        base = r * 7 * slots
-        near_low = [jnp.full((SUB, lanes), FAR, F32) for _ in range(2)]
-        near_high = [jnp.full((SUB, lanes), -FAR, F32) for _ in range(2)]
+        sizes[slot] = jnp.max(upto[slots - 1 : slots, :]).astype(jnp.int32)
+
+    for r, (source, offset, dz) in enumerate(rows):
+        base = r * 7 * pitch
         for d, dx in enumerate((0, -1, 1)):
+            if own and d < 2:
+                continue
             marks = []
             for g in range(groups):
                 pos = [
-                    near[base + a * slots + g * SUB : base + a * slots + (g + 1) * SUB, :]
+                    near[base + a * pitch + g * SUB : base + a * pitch + (g + 1) * SUB, :]
                     for a in range(3)
                 ]
                 if dx:
@@ -187,33 +207,24 @@
                 for a in (1, 2):
                     mark = mark & (pos[a] > home_low[a]) & (pos[a] < home_high[a])
                 marks.append(mark)
-                if not own:
-                    for a in (1, 2):
-                        near_low[a - 1] = jnp.minimum(near_low[a - 1], jnp.where(mark, pos[a], FAR))
-                        near_high[a - 1] = jnp.maximum(near_high[a - 1], jnp.where(mark, pos[a], -FAR))
             ranked(4 * r + d, marks)
         if not own:
-            bounds = [
-                (
-                    spread(jnp.min(near_low[a], axis=0, keepdims=True)) - REACH,
-                    spread(jnp.max(near_high[a], axis=0, keepdims=True)) + REACH,
-                )
-                for a in range(2)
-            ]
             marks = []
             for g in range(groups):
                 mark = home_there[g]
                 for a in range(2):
-                    p = home[(a + 1) * slots + g * SUB : (a + 1) * slots + (g + 1) * SUB, :]
-                    mark = mark & (p > bounds[a][0]) & (p < bounds[a][1])
+                    p = home[(a + 1) * pitch + g * SUB : (a + 1) * pitch + (g + 1) * SUB, :]
+                    mark = mark & (p > reach[(r, a)][0]) & (p < reach[(r, a)][1])
                 marks.append(mark)
             ranked(4 * r + 3, marks)
 
     def choose(slot, k):
-        target = iota_f + (k * SUB).astype(F32)
-        index = jnp.full((SUB, lanes), -1, jnp.int32)
+        target = iota_f + (k * (2 * SUB)).astype(F32)
+        index = [jnp.full((SUB, lanes), -1, jnp.int32) for _ in range(2)]
         for s in range(slots):
-            index = jnp.where(rank[pl.ds(slot * slots + s, SUB, stride=0), :] == target, s, index)
+            place = rank[pl.ds(slot * slots + s, SUB, stride=0), :]
+            for i in range(2):
+                index[i] = jnp.where(place == target + F32(i * SUB), s, index[i])
         return index
 
     def gathered(ref, base, index):
@@ -228,17 +239,16 @@
     def aligned(value):
         return pl.multiple_of(value, SUB)
 
-    def run_pairs(count, where_home, blocks):
+    def run_pairs(count, where_home, blocks, start=0, react=False):
         def one(j, carry):
             carry = list(carry)
-            n = [liste[pl.ds(c * capacity + j, SUB, stride=0), :] for c in range(9)]
+            n = [liste[pl.ds(c * capacity + start + j, SUB, stride=0), :] for c in range(9)]
             tot = [None] * 3
             for b in range(blocks):
-                h = [where_home[c * slots + b * SUB : c * slots + (b + 1) * SUB, :] for c in range(9)]
+                h = [where_home[c * pitch + b * SUB : c * pitch + (b + 1) * SUB, :] for c in range(9)]
                 rx, ry, rz = h[0] - n[0], h[1] - n[1], h[2] - n[2]
                 squared = jnp.maximum(rx * rx + ry * ry + rz * rz, FLOOR_SQUARED)
-                inverse = lax.rsqrt(squared)
-                u = jnp.maximum(inverse - 1.0, 0.0)
+                u = jnp.maximum(lax.rsqrt(squared) - 1.0, 0.0)
                 rv = rx * (h[3] - n[3]) + ry * (h[4] - n[4]) + rz * (h[5] - n[5])
                 t = ((h[6] * n[6] + h[7] * n[7]) + (h[8] + n[8])) * F32(INVERSE)
                 y = (t - jnp.floor(t)) + F32(SHIFT)
@@ -250,25 +260,32 @@
             if virial:
                 for i, (a, b) in enumerate(COMPONENT_PAIRS):
                     carry[3 * blocks + i] = carry[3 * blocks + i] - n[a] * tot[b]
+            if react:
+                for a in range(3):
+                    answer[pl.ds(a * slots + j, 1), :] = jnp.sum(tot[a], axis=0, keepdims=True)
             return tuple(carry)
 
-        def two(i, carry):
-            return one(2 * i + 1, one(2 * i, carry))
+        def several(i, carry):
+            for k in range(UNROLL):
+                carry = one(UNROLL * i + k, carry)
+            return carry
 
         zero = jnp.zeros((SUB, lanes), F32)
-        start = (zero,) * (3 * blocks + (6 if virial else 0))
-        done = lax.fori_loop(0, (count + 1) // 2, two, start)
+        begin = (zero,) * (3 * blocks + (6 if virial else 0))
+        done = lax.fori_loop(0, (count + UNROLL - 1) // UNROLL, several, begin)
         for b in range(blocks):
             for a in range(3):
                 part[a * slots + b * SUB : a * slots + (b + 1) * SUB, :] = done[3 * b + a]
         if virial:
             for i, (a, b) in enumerate(COMPONENT_PAIRS):
-                value = tally[i * SUB : (i + 1) * SUB, :] + done[3 * blocks + i]
+                value = done[3 * blocks + i]
                 for g in range(blocks):
                     value = value + (
-                        where_home[a * slots + g * SUB : a * slots + (g + 1) * SUB, :] * done[3 * g + b]
+                        where_home[a * pitch + g * SUB : a * pitch + (g + 1) * SUB, :] * done[3 * g + b]
                     )
-                tally[i * SUB : (i + 1) * SUB, :] = value
+                if react:
+                    value = value + pltpu.roll(value, 1, 1)
+                tally[i * SUB : (i + 1) * SUB, :] = tally[i * SUB : (i + 1) * SUB, :] + value
 
     for c in range(3):
         for g in range(groups):
@@ -282,61 +299,89 @@
                 jnp.zeros((SUB, lanes), F32) if first else virial_in[i * SUB : (i + 1) * SUB, :]
             )
 
-    def direction(r, _):
-        base = r * (7 * slots)
-        filled = jnp.int32(0)
-        for d, dx in enumerate((0, -1, 1)):
-            slot = 4 * r + d
-            size = sizes[slot]
-
-            def fill(k, _, slot=slot, dx=dx, filled=filled):
-                index = choose(slot, k)
+    def gather_near(at, index, dx):
+        v = gathered(near, at, index)
+        return pltpu.roll(v, (-dx) % lanes, 1) if dx else v
+
+    def fill_near(base, slot, dx, filled):
+        def fill(k, _):
+            for i, index in enumerate(choose(slot, k)):
                 valid = index >= 0
-                values = [
-                    gathered_near(base + c * slots, index, dx) for c in range(7)
-                ]
+                if dx:
+                    index = pltpu.roll(index, dx % lanes, 1)
+                values = [gather_near(base + c * pitch, index, dx) for c in range(7)]
                 values[0] = jnp.where(valid, values[0] + F32(EDGE * dx), FAR)
                 values = values[:6] + list(near_noise(values[6]))
                 for c in range(9):
-                    liste[pl.ds(c * capacity + filled + k * SUB, SUB), :] = values[c]
-                return 0
-
-            def gathered_near(at, index, dx):
-                within = index & (SUB - 1)
-                result = None
-                for g in range(groups):
-                    v = near[pl.ds(aligned(at + g * SUB), SUB), :]
-                    if dx:
-                        v = pltpu.roll(v, (-dx) % lanes, 1)
-                    v = take_rows(v, within)
-                    result = v if g == 0 else jnp.where(index >= g * SUB, v, result)
-                return result
-
-            lax.fori_loop(0, (size + SUB - 1) // SUB, fill, 0)
-            filled = filled + size
+                    at = c * capacity + filled + k * (2 * SUB) + i * SUB
+                    liste[pl.ds(at, SUB), :] = values[c]
+            return 0
+
+        size = sizes[slot]
+        lax.fori_loop(0, (size + 2 * SUB - 1) // (2 * SUB), fill, 0)
+        return filled + size
+
+    def close(filled):
         liste[pl.ds(filled, SUB), :] = jnp.full((SUB, lanes), FAR, F32)
         for c in range(1, 9):
             liste[pl.ds(c * capacity + filled, SUB), :] = jnp.zeros((SUB, lanes), F32)
-        if own:
-            run_pairs(filled, home, groups)
-            for c in range(3):
-                for g in range(groups):
+
+    def collect():
+        for c in range(3):
+            for g in range(groups):
+                at = c * slots + g * SUB
+                total[at : at + SUB, :] = total[at : at + SUB, :] + part[at : at + SUB, :]
+
+    def own_row():
+        for g in range(groups):
+            values = [near[c * pitch + g * SUB : c * pitch + (g + 1) * SUB, :] for c in range(7)]
+            values = values[:6] + list(near_noise(values[6]))
+            for c in range(9):
+                at = c * capacity + g * SUB
+                liste[at : at + SUB, :] = values[c]
+        close(fill_near(0, 2, 1, slots))
+        run_pairs(slots, home, groups)
+        collect()
+        size = sizes[2]
+        run_pairs(size, home, groups, start=slots, react=True)
+        collect()
+
+        def back(k, _):
+            forces = [
+                pltpu.roll(answer[pl.ds(aligned(c * slots + k * SUB), SUB), :], 1, 1) for c in range(3)
+            ]
+            for g in range(groups):
+                place = rank[(2 * slots + g * SUB) : (2 * slots + (g + 1) * SUB), :]
+                place = pltpu.roll(place, 1, 1).astype(jnp.int32)
+                mine = (place >= k * SUB) & (place < (k + 1) * SUB)
+                within = place & (SUB - 1)
+                for c in range(3):
                     at = c * slots + g * SUB
-                    total[at : at + SUB, :] = total[at : at + SUB, :] + part[at : at + SUB, :]
+                    v = take_rows(forces[c], within)
+                    total[at : at + SUB, :] = total[at : at + SUB, :] - jnp.where(mine, v, 0.0)
             return 0
+
+        lax.fori_loop(0, (size + SUB - 1) // SUB, back, 0)
+
+    def direction(r, _):
+        base = r * (7 * pitch)
+        filled = jnp.int32(0)
+        for d, dx in enumerate((0, -1, 1)):
+            filled = fill_near(base, 4 * r + d, dx, filled)
+        close(filled)
         slot = 4 * r + 3
         needed = (sizes[slot] + SUB - 1) // SUB
 
         def fill_home(k, _):
-            index = choose(slot, k)
-            for c in range(9):
-                v = gathered(home, c * slots, index)
-                if c == 0:
-                    v = jnp.where(index >= 0, v, -FAR)
-                pick[pl.ds(aligned(c * slots + k * SUB), SUB), :] = v
+            for i, index in enumerate(choose(slot, k)):
+                for c in range(9):
+                    v = gathered(home, c * pitch, index)
+                    if c == 0:
+                        v = jnp.where(index >= 0, v, -FAR)
+                    pick[pl.ds(aligned(c * pitch + k * (2 * SUB) + i * SUB), SUB), :] = v
             return 0
 
-        lax.fori_loop(0, needed, fill_home, 0)
+        lax.fori_loop(0, (needed + 1) // 2, fill_home, 0)
         for blocks in range(1, groups + 1):
             pl.when(needed == blocks)(functools.partial(run_pairs, filled, pick, blocks))
 
@@ -354,8 +399,8 @@
         lax.fori_loop(0, needed, back, 0)
         return 0
 
-    if len(rows) == 1:
-        direction(jnp.int32(0), 0)
+    if own:
+        own_row()
     else:
         lax.fori_loop(0, len(rows), direction, 0)
 
@@ -387,7 +432,7 @@
                 virial_out[i * SUB : (i + 1) * SUB, :] = v
 
 
-def pairs(offsets, home, home_fixed, nears, fixed, carried, rows, step, last, virial, slots, cost):
+def pairs(offsets, home, home_fixed, nears, fixed, carried, rows, step, last, virial, slots, cost, side=0):
     lanes = home.shape[-1]
     own = len(rows) == 1
     first = carried is None
@@ -407,7 +452,8 @@
         outs = (shape(3 * slots),)
     vmem = pl.BlockSpec(memory_space=pltpu.VMEM)
     smem = pl.BlockSpec(memory_space=pltpu.SMEM)
-    capacity = 3 * slots + 2 * SUB
+    pitch = slots + SUB
+    capacity = 3 * slots + 2 * SUB + 1
     count = len(rows)
     return pl.pallas_call(
         functools.partial(
@@ -422,16 +468,17 @@
             last=last,
             virial=virial,
             has_fixed=fixed is not None,
+            side=side,
         ),
         out_shape=outs,
         in_specs=[smem] + [vmem] * (len(operands) - 1),
         out_specs=tuple(vmem for _ in outs),
         scratch_shapes=[
-            pltpu.VMEM((9 * slots, lanes), F32),
-            pltpu.VMEM((count * 7 * slots, lanes), F32),
-            pltpu.VMEM((SUB, lanes), F32),
+            pltpu.VMEM((9 * pitch, lanes), F32),
+            pltpu.VMEM((count * 7 * pitch, lanes), F32),
+            pltpu.VMEM((4 * slots, lanes), F32),
             pltpu.VMEM((count * 4 * slots, lanes), F32),
-            pltpu.VMEM((9 * slots, lanes), F32),
+            pltpu.VMEM((9 * pitch, lanes), F32),
             pltpu.VMEM((9 * capacity, lanes), F32),
             pltpu.VMEM((3 * slots, lanes), F32),
             pltpu.VMEM((3 * slots, lanes), F32),
@@ -440,7 +487,7 @@
         ],
         compiler_params=pltpu.CompilerParams(vmem_limit_bytes=VMEM_LIMIT),
         cost_estimate=pl.CostEstimate(flops=cost, bytes_accessed=1, transcendentals=0),
-        name=f"pairs_{count}_{step}",
+        name=f"pairs_{side}_{step}",
     )(*operands)
 
 
@@ -468,6 +515,12 @@
 
 def ring(count, by):
     return [(i, (i + by) % count) for i in range(count)]
+
+
+def swap(count, first):
+    assert count % 2 == 0
+    pairs_of = [((first + i) % count, (first + i + 1) % count) for i in range(0, count, 2)]
+    return pairs_of + [(b, a) for a, b in pairs_of]
 
 
 def shards(positions, velocities, forces_prev, seeds, counts, offsets):
@@ -496,7 +549,6 @@
         if gz > 2:
             planes.append(lax.ppermute(state, "gz", ring(gz, 1)))
         up, down = 0, len(planes) - 1
-        near_fixed = lambda at: None if not final else kept[at]
         call = functools.partial(
             pairs, offsets, state, home_fixed, step=step, virial=final, slots=slots
         )
@@ -505,31 +557,40 @@
             [state],
             [home_fixed] if final else None,
             None,
-            rows=((0, here, 0, 0),),
+            rows=((0, here, 0),),
             last=False,
             cost=100_000_000,
         )
         planes, carried = lax.optimization_barrier((planes, carried))
         stacked = jnp.concatenate([state, *planes], axis=0)
-        lower = lax.ppermute(stacked, "xy", ring(xy, 1))
-        upper = lax.ppermute(stacked, "xy", ring(xy, -1))
+        far = lax.ppermute(stacked, "xy", swap(xy, 1))
+        near = lax.ppermute(stacked, "xy", swap(xy, 0))
+        arrived = (planes, [near], [far])
+        if not final:
+            kept = arrived
         carried = call(
             planes,
-            near_fixed(0),
+            kept[0] if final else None,
             carried,
-            rows=((down, here, -1, 0), (up, here, 1, 0)),
+            rows=((down, here, -1), (up, here, 1)),
             last=False,
             cost=100_000_000,
         )
-        rows = []
-        for source, dy in ((0, -1), (1, 1)):
-            for dz, place in ((0, 0), (-1, 1 + down), (1, 1 + up)):
-                rows.append((source, (place * high, place * tall), dz, dy))
-        outs = call(
-            [lower, upper], near_fixed(1), carried, rows=tuple(rows), last=True, cost=200_000_000
+        beside = tuple(
+            (0, (place * high, place * tall), dz) for dz, place in ((0, 0), (-1, 1 + down), (1, 1 + up))
         )
+        for side in (NEAR_SIDE, FAR_SIDE):
+            carried = call(
+                arrived[side],
+                kept[side] if final else None,
+                carried,
+                rows=beside,
+                last=side == FAR_SIDE,
+                cost=100_000_000,
+                side=side,
+            )
+        outs = carried
         if not final:
-            kept = (planes, [lower, upper])
             state = outs[0]
     force, velocity, stress = outs
     return (

time: 53.5 us -> 47.2 us (0.88)
  waiting for transfers between devices: 6.88 us -> 0.28 us
  starting transfers between devices: 8.29 us -> 9.76 us
  Pallas kernels: 36.7 us -> 35.4 us
    ppermute x4, waiting for transfers between devices: 6.87 us -> 0.01 us  [the longest x2 0.01 us: shards(): near = lax.ppermute(stacked, 'xy', swap(xy, 0))]
    pallas_call x6 -> x8, Pallas kernels: 35.1 us -> 33.9 us  [pairs(): pl.pallas_call(functools.partial(pair_kernel, slots=slots, lanes=lanes, s...]
    ppermute x4, starting transfers between devices: 4.17 us -> 5.31 us  [the longest x2 5.17 us: shards(): far = lax.ppermute(stacked, 'xy', swap(xy, 1))]
  transfers between devices with their start and end apart: 6 -> 6, of which waited for: 2 -> 1; matrix products, arithmetic and copies ran while one was open for 0% -> 0% of each run, Pallas kernels for 30% -> 51%
where the time goes in v3:
time: 47.2 us
  Pallas kernels  35.4 us (75%)
  starting transfers between devices  9.76 us (21%)
  local copies, waits for them, and re-layouts  0.94 us (2%)
  between operations  0.76 us (2%)
    pallas_call x8, Pallas kernels, pairs(): pl.pallas_call(functools.partial(pair_kernel, slots=slots, lanes=lanes, s...  33.9 us
    ppermute x2, starting transfers between devices, shards(): far = lax.ppermute(stacked, 'xy', swap(xy, 1))  5.17 us
    ppermute x2, starting transfers between devices, shards(): planes = [lax.ppermute(state, 'gz', ring(gz, -1))]  4.45 us
    pallas_call x1, Pallas kernels, shards(): pl.pallas_call(functools.partial(kick_kernel, slots=slots, lanes=lanes),...  1.55 us
  transfers between devices with their start and end apart: 6, of which 1 were waited for; matrix products, arithmetic and copies ran while one was open for 0% of the time, Pallas kernels for 51%

profile of v3, /device:TPU:0, one launch (start us, length us, event | category | flops | bytes accessed | tf_op | source)
XLA Modules:
  0.0 47.2 jit_solution(3701300462021000244)
XLA Ops:
  0.6 0.0 copy-start.2
  0.6 1.6 %kick.1.refs_1_.refs_2_.refs_3_.refs_4_ = f32[232,128]{1,0:T(8,128)} custom-call(f32[96,128]{1,0:T(8,128)} %bitcast.14, f32[96,128]{1,0:T(8,128)} %bitcast.15, f32[96,128]{1,0:T(8,128)} %bitcast.16, s32[32,128]{1,0:T(8,128)} %bitcast.17, s32[1,128]{1,0:T(1,128)} %bitcast.18), custom_call_target="tpu_custom_call" | custom-call | tf_op jit(solution)/shard_map/kick/pallas_call | solution.py:533
  2.2 3.0 %collective-permute-start = (f32[232,128]{1,0:T(8,128)}, f32[232,128]{1,0:T(8,128)S(1)}, u32[]{:S(2)}, u32[]{:S(2)}) collective-permute-start(f32[232,128]{1,0:T(8,128)} %kick.1.refs_1_.refs_2_.refs_3_.refs_4_), channel_id=1, source_target_pairs={{0,1},{1,0},{2,3},{3,2},{4,5},{5,4},{6,7},{7,6},{8,9},{9,8},{10,11... | collective-permute-start | bytes 356360 | tf_op jit(solution)/shard_map/ppermute | solution.py:548
  5.2 0.0 copy-done.2
  5.2 0.0 copy-start
  5.2 0.9 %copy-done = f32[232,128]{1,0:T(8,128)S(1)} copy-done((f32[232,128]{1,0:T(8,128)S(1)}, f32[232,128]{1,0:T(8,128)}, u32[]{:S(2)}) %copy-start) | copy-done | bytes 118808
  6.2 0.0 copy-start.1
  6.2 2.9 %pairs_0_0.2.refs_4_ = f32[96,128]{1,0:T(8,128)S(1)} custom-call(s32[2]{0:T(128)S(1)} %copy-done.2, f32[232,128]{1,0:T(8,128)S(1)} %copy-done, f32[232,128]{1,0:T(8,128)S(1)} %copy-done, f32[232,128]{1,0:T(8,128)S(1)} %copy-done), custom_call_target="tpu_custom_call" | custom-call | flops 100000000 | bytes 1 | tf_op jit(solution)/shard_map/pairs_0_0/pallas_call | solution.py:458
  9.1 0.0 collective-permute-done.refs_3_.refs_4_
  9.1 0.0 copy-done.1
  9.1 0.1 collective-permute-start.2
  9.2 4.5 %collective-permute-start.1 = (f32[464,128]{1,0:T(8,128)S(1)}, f32[464,128]{1,0:T(8,128)S(1)}, u32[]{:S(2)}, u32[]{:S(2)}) collective-permute-start(f32[464,128]{1,0:T(8,128)S(1)} %pad_maximum_fusion), channel_id=1, source_target_pairs={{2,4},{6,8},{10,12},{14,16},{18,20},{22,24},{26,28},{30,0},{4,2},{... | collective-permute-start | bytes 712712 | tf_op jit(solution)/shard_map/ppermute | solution.py:566
  13.7 3.9 %pairs_0_0.3.refs_4_ = f32[96,128]{1,0:T(8,128)S(1)} custom-call(s32[2]{0:T(128)S(1)} %copy-done.2, f32[232,128]{1,0:T(8,128)S(1)} %copy-done.1, f32[232,128]{1,0:T(8,128)S(1)} %copy-done.1, f32[232,128]{1,0:T(8,128)S(1)} %collective-permute-done.refs_3_.refs_4_, f32[96,128]{1,0:T(8,128)S(1)} %pairs_0_0.2.refs_4_), custom_call_target="tpu_custom_call" | custom-call | flops 100000000 | bytes 1 | tf_op jit(solution)/shard_map/pairs_0_0/pallas_call | solution.py:458
  17.7 0.0 collective-permute-done.2.refs_3_.refs_4_
  17.7 4.7 %pairs_1_0.1.refs_4_ = f32[96,128]{1,0:T(8,128)S(1)} custom-call(s32[2]{0:T(128)S(1)} %copy-done.2, f32[232,128]{1,0:T(8,128)S(1)} %copy-done.1, f32[232,128]{1,0:T(8,128)S(1)} %copy-done.1, f32[464,128]{1,0:T(8,128)S(1)} %collective-permute-done.2.refs_3_.refs_4_, f32[96,128]{1,0:T(8,128)S(1)} %pairs_0_0.3.refs_4_), custom_call_target="tpu_custom_call" | custom-call | flops 100000000 | bytes 1 | tf_op jit(solution)/shard_map/pairs_1_0/pallas_call | solution.py:458
  22.4 0.0 collective-permute-done.1.refs_3_.refs_4_
  22.4 4.3 %pairs_2_0.1.refs_1_.refs_3_ = f32[192,128]{1,0:T(8,128)S(1)} custom-call(s32[2]{0:T(128)S(1)} %copy-done.2, f32[232,128]{1,0:T(8,128)S(1)} %copy-done.1, f32[232,128]{1,0:T(8,128)S(1)} %copy-done.1, f32[464,128]{1,0:T(8,128)S(1)} %collective-permute-done.1.refs_3_.refs_4_, f32[96,128]{1,0:T(8,128)S(1)} %pairs_1_0.1.refs_4_), custom_call_target="tpu_custom_call" | custom-call | flops 100000000 | bytes 1 | tf_op jit(solution)/shard_map/pairs_2_0/pallas_call | solution.py:458
  26.7 1.4 %collective-permute-start.3 = (f32[192,128]{1,0:T(8,128)S(1)}, f32[192,128]{1,0:T(8,128)S(1)}, u32[]{:S(2)}, u32[]{:S(2)}) collective-permute-start(f32[192,128]{1,0:T(8,128)S(1)} %pairs_2_0.1.refs_1_.refs_3_), channel_id=1, source_target_pairs={{0,1},{1,0},{2,3},{3,2},{4,5},{5,4},{6,7},{7,6},{8,9},{9,8},{10,11... | collective-permute-start | bytes 294920 | tf_op jit(solution)/shard_map/ppermute | solution.py:548
  28.1 3.0 %pairs_0_1.2 = (f32[96,128]{1,0:T(8,128)S(1)}, f32[48,128]{1,0:T(8,128)S(1)}) custom-call(s32[2]{0:T(128)S(1)} %copy-done.2, f32[192,128]{1,0:T(8,128)S(1)} %pairs_2_0.1.refs_1_.refs_3_, f32[232,128]{1,0:T(8,128)S(1)} %copy-done.1, f32[192,128]{1,0:T(8,128)S(1)} %pairs_2_0.1.refs_1_.refs_3_, f32[232,128]{1,0:T(8,128)S(1)} %copy-done.1), custom_call_target="tpu_custom_call" | custom-call | flops 100000000 | bytes 1 | tf_op jit(solution)/shard_map/pairs_0_1/pallas_call | solution.py:458
  31.1 0.3 collective-permute-done.3.refs_3_
  31.4 0.1 collective-permute-start.5
  31.5 0.6 %collective-permute-start.4 = (f32[384,128]{1,0:T(8,128)S(1)}, f32[384,128]{1,0:T(8,128)S(1)}, u32[]{:S(2)}, u32[]{:S(2)}) collective-permute-start(f32[384,128]{1,0:T(8,128)S(1)} %pad_maximum_fusion.1), channel_id=1, source_target_pairs={{2,4},{6,8},{10,12},{14,16},{18,20},{22,24},{26,28},{30,0},{4,2},{... | collective-permute-start | bytes 589832 | tf_op jit(solution)/shard_map/ppermute | solution.py:566
  32.1 4.5 %pairs_0_1.3 = (f32[96,128]{1,0:T(8,128)S(1)}, f32[48,128]{1,0:T(8,128)S(1)}) custom-call(s32[2]{0:T(128)S(1)} %copy-done.2, f32[192,128]{1,0:T(8,128)S(1)} %pairs_2_0.1.refs_1_.refs_3_, f32[232,128]{1,0:T(8,128)S(1)} %copy-done.1, f32[192,128]{1,0:T(8,128)S(1)} %collective-permute-done.3.refs_3_, f32[232,128]{1,0:T(8,128)S(1)} %collective-permute-done.refs_3_.refs_4_, ...), custom_call_target="tpu_custom_call" | custom-call | flops 100000000 | bytes 1 | tf_op jit(solution)/shard_map/pairs_0_1/pallas_call | solution.py:458
  36.6 0.0 collective-permute-done.5.refs_3_
  36.6 5.2 %pairs_1_1.1 = (f32[96,128]{1,0:T(8,128)S(1)}, f32[48,128]{1,0:T(8,128)S(1)}) custom-call(s32[2]{0:T(128)S(1)} %copy-done.2, f32[192,128]{1,0:T(8,128)S(1)} %pairs_2_0.1.refs_1_.refs_3_, f32[232,128]{1,0:T(8,128)S(1)} %copy-done.1, f32[384,128]{1,0:T(8,128)S(1)} %collective-permute-done.5.refs_3_, f32[464,128]{1,0:T(8,128)S(1)} %collective-permute-done.2.refs_3_.refs_4_, ...), custom_call_target="tpu_custom_call" | custom-call | flops 100000000 | bytes 1 | tf_op jit(solution)/shard_map/pairs_1_1/pallas_call | solution.py:458
  41.9 0.0 collective-permute-done.4.refs_3_
  41.9 5.3 %pairs_2_1.1 = (f32[96,128]{1,0:T(8,128)}, f32[96,128]{1,0:T(8,128)}, f32[6,1,128]{2,1,0:T(1,128)}) custom-call(s32[2]{0:T(128)S(1)} %copy-done.2, f32[192,128]{1,0:T(8,128)S(1)} %pairs_2_0.1.refs_1_.refs_3_, f32[232,128]{1,0:T(8,128)S(1)} %copy-done.1, f32[384,128]{1,0:T(8,128)S(1)} %collective-permute-done.4.refs_3_, ...), custom_call_target="tpu_custom_call" | custom-call | flops 100000000 | bytes 1 | tf_op jit(solution)/shard_map/pairs_2_1/pallas_call | solution.py:458
  (2 shorter events, 0.0 us)
Async XLA Ops:
  0.6 4.6 %copy-start.2 = (s32[2]{0:T(128)S(1)}, s32[2]{0:T(128)}, u32[]{:S(2)}) copy-start(s32[2]{0:T(128)} %refs_0_.15) | copy-start | bytes 28
  2.2 6.9 %collective-permute-start = (f32[232,128]{1,0:T(8,128)}, f32[232,128]{1,0:T(8,128)S(1)}, u32[]{:S(2)}, u32[]{:S(2)}) collective-permute-start(f32[232,128]{1,0:T(8,128)} %kick.1.refs_1_.refs_2_.refs_3_.refs_4_), channel_id=1, source_target_pairs={{0,1},{1,0},{2,3},{3,2},{4,5},{5,4},{6,7},{7,6},{8,9},{9,8},{10,11... | collective-permute-start | bytes 356360 | tf_op jit(solution)/shard_map/ppermute | solution.py:548
  5.2 0.9 %copy-start = (f32[232,128]{1,0:T(8,128)S(1)}, f32[232,128]{1,0:T(8,128)}, u32[]{:S(2)}) copy-start(f32[232,128]{1,0:T(8,128)} %kick.1.refs_1_.refs_2_.refs_3_.refs_4_) | copy-start | bytes 356356
  6.2 2.9 %copy-start.1 = (f32[232,128]{1,0:T(8,128)S(1)}, f32[232,128]{1,0:T(8,128)}, u32[]{:S(2)}) copy-start(f32[232,128]{1,0:T(8,128)} %kick.1.refs_1_.refs_2_.refs_3_.refs_4_) | copy-start | bytes 356356
  9.1 8.5 %collective-permute-start.2 = (f32[464,128]{1,0:T(8,128)S(1)}, f32[464,128]{1,0:T(8,128)S(1)}, u32[]{:S(2)}, u32[]{:S(2)}) collective-permute-start(f32[464,128]{1,0:T(8,128)S(1)} %pad_maximum_fusion), channel_id=1, source_target_pairs={{0,2},{4,6},{8,10},{12,14},{16,18},{20,22},{24,26},{28,30},{2,0},{... | collective-permute-start | bytes 712712 | tf_op jit(solution)/shard_map/ppermute | solution.py:567
  9.2 13.2 %collective-permute-start.1 = (f32[464,128]{1,0:T(8,128)S(1)}, f32[464,128]{1,0:T(8,128)S(1)}, u32[]{:S(2)}, u32[]{:S(2)}) collective-permute-start(f32[464,128]{1,0:T(8,128)S(1)} %pad_maximum_fusion), channel_id=1, source_target_pairs={{2,4},{6,8},{10,12},{14,16},{18,20},{22,24},{26,28},{30,0},{4,2},{... | collective-permute-start | bytes 712712 | tf_op jit(solution)/shard_map/ppermute | solution.py:566
  26.7 4.7 %collective-permute-start.3 = (f32[192,128]{1,0:T(8,128)S(1)}, f32[192,128]{1,0:T(8,128)S(1)}, u32[]{:S(2)}, u32[]{:S(2)}) collective-permute-start(f32[192,128]{1,0:T(8,128)S(1)} %pairs_2_0.1.refs_1_.refs_3_), channel_id=1, source_target_pairs={{0,1},{1,0},{2,3},{3,2},{4,5},{5,4},{6,7},{7,6},{8,9},{9,8},{10,11... | collective-permute-start | bytes 294920 | tf_op jit(solution)/shard_map/ppermute | solution.py:548
  31.4 5.2 %collective-permute-start.5 = (f32[384,128]{1,0:T(8,128)S(1)}, f32[384,128]{1,0:T(8,128)S(1)}, u32[]{:S(2)}, u32[]{:S(2)}) collective-permute-start(f32[384,128]{1,0:T(8,128)S(1)} %pad_maximum_fusion.1), channel_id=1, source_target_pairs={{0,2},{4,6},{8,10},{12,14},{16,18},{20,22},{24,26},{28,30},{2,0},{... | collective-permute-start | bytes 589832 | tf_op jit(solution)/shard_map/ppermute | solution.py:567
  31.5 10.4 %collective-permute-start.4 = (f32[384,128]{1,0:T(8,128)S(1)}, f32[384,128]{1,0:T(8,128)S(1)}, u32[]{:S(2)}, u32[]{:S(2)}) collective-permute-start(f32[384,128]{1,0:T(8,128)S(1)} %pad_maximum_fusion.1), channel_id=1, source_target_pairs={{2,4},{6,8},{10,12},{14,16},{18,20},{22,24},{26,28},{30,0},{4,2},{... | collective-permute-start | bytes 589832 | tf_op jit(solution)/shard_map/ppermute | solution.py:566

commit v4 on v3

--- a/solution.py
+++ b/solution.py
@@ -78,7 +78,9 @@
 ):
     refs = list(refs)
     take = lambda n: [refs.pop(0) for _ in range(n)]
-    offset_ref, home_ref, home_fixed_ref = take(3)
+    turning = side == FAR_SIDE
+    home_ref, home_fixed_ref = take(2)
+    home = None if own else take(1)[0]
     near_refs = take(sources)
     fixed_refs = take(sources) if has_fixed else near_refs
     force_in = None if first else take(1)[0]
@@ -89,7 +91,9 @@
         force_out, virial_out = take(2)
     else:
         (force_out,) = take(1)
-    home, near, answer, rank, pick, liste, part, total, tally, sizes = take(10)
+    if own:
+        (home,) = take(1)
+    near, answer, rank, pick, liste, part, total, tally, sizes = take(9)
     groups = slots // SUB
     pitch = slots + SUB
     capacity = liste.shape[0] // 9
@@ -100,14 +104,13 @@
         index, count = lax.axis_index("xy"), lax.axis_size("xy")
         upper = (lax.rem(index, 2) == 0) == (side == NEAR_SIDE)
         across = jnp.where(upper, F32(1.0), F32(-1.0))
+    if turning:
         wraps = jnp.where(upper, index == count - 1, index == 0)
-        amount = offset_ref[step]
+        strain_at = fixed_at + slots + 1 + step
+        amount = jnp.max(home_fixed_ref[strain_at : strain_at + 1, :]).astype(jnp.int32)
         turn = jnp.where(upper, amount, lax.rem(lanes - amount, lanes))
         turn = jnp.where(wraps, turn, 0)
         shear = jnp.where(wraps, across * F32(SHEAR_SPEED), F32(0.0))
-        turning = side != NEAR_SIDE
-    else:
-        turning = False
 
     def block(ref, base, group):
         return ref[base + group * SUB : base + (group + 1) * SUB, :]
@@ -115,28 +118,32 @@
     def spread(row):
         return jnp.broadcast_to(row, (SUB, lanes))
 
-    home_count = spread(home_fixed_ref[fixed_at + slots : fixed_at + slots + 1, :])
-    low = [jnp.full((SUB, lanes), FAR, F32) for _ in range(3)]
-    high = [jnp.full((SUB, lanes), -FAR, F32) for _ in range(3)]
-    home_there = []
-    for g in range(groups):
-        there = iota_f + F32(g * SUB) < home_count
-        home_there.append(there)
-        for a in range(3):
-            p = block(home_ref, a * slots, g)
-            low[a] = jnp.minimum(low[a], jnp.where(there, p, FAR))
-            high[a] = jnp.maximum(high[a], jnp.where(there, p, -FAR))
-            home[(a * pitch + g * SUB) : (a * pitch + (g + 1) * SUB), :] = (
-                jnp.where(there, p, -FAR) if a == 0 else p
-            )
-            home[((3 + a) * pitch + g * SUB) : ((3 + a) * pitch + (g + 1) * SUB), :] = (
-                block(home_ref, (3 + a) * slots, g) * F32(VELOCITY_SCALE)
-            )
-        for a, value in enumerate(home_noise(block(home_fixed_ref, fixed_at, g), step)):
-            at = (6 + a) * pitch + g * SUB
-            home[at : at + SUB, :] = value
-    home_low = [spread(jnp.min(v, axis=0, keepdims=True)) - REACH for v in low]
-    home_high = [spread(jnp.max(v, axis=0, keepdims=True)) + REACH for v in high]
+    box_at = 9 * pitch
+    if own:
+        home_count = spread(home_fixed_ref[fixed_at + slots : fixed_at + slots + 1, :])
+        low = [jnp.full((SUB, lanes), FAR, F32) for _ in range(3)]
+        high = [jnp.full((SUB, lanes), -FAR, F32) for _ in range(3)]
+        for g in range(groups):
+            there = iota_f + F32(g * SUB) < home_count
+            for a in range(3):
+                p = block(home_ref, a * slots, g)
+                low[a] = jnp.minimum(low[a], jnp.where(there, p, FAR))
+                high[a] = jnp.maximum(high[a], jnp.where(there, p, -FAR))
+                at = a * pitch + g * SUB
+                home[at : at + SUB, :] = jnp.where(there, p, -FAR) if a == 0 else p
+                at = (3 + a) * pitch + g * SUB
+                home[at : at + SUB, :] = block(home_ref, (3 + a) * slots, g) * F32(VELOCITY_SCALE)
+            for a, value in enumerate(home_noise(block(home_fixed_ref, fixed_at, g), step)):
+                at = (6 + a) * pitch + g * SUB
+                home[at : at + SUB, :] = value
+        home_low = [spread(jnp.min(v, axis=0, keepdims=True)) - REACH for v in low]
+        home_high = [spread(jnp.max(v, axis=0, keepdims=True)) + REACH for v in high]
+        for i, v in enumerate(home_low + home_high):
+            home[box_at + i * SUB : box_at + (i + 1) * SUB, :] = v
+    else:
+        walls = [home[box_at + i * SUB : box_at + (i + 1) * SUB, :] for i in range(6)]
+        home_low, home_high = walls[:3], walls[3:]
+        home_there = [home[g * SUB : (g + 1) * SUB, :] > F32(-0.5 * FAR) for g in range(groups)]
 
     reach = {}
     for r, (source, offset, dz) in enumerate(rows):
@@ -432,11 +439,11 @@
                 virial_out[i * SUB : (i + 1) * SUB, :] = v
 
 
-def pairs(offsets, home, home_fixed, nears, fixed, carried, rows, step, last, virial, slots, cost, side=0):
+def pairs(home, home_fixed, beads, nears, fixed, carried, rows, step, last, virial, slots, cost, side=0):
     lanes = home.shape[-1]
     own = len(rows) == 1
     first = carried is None
-    operands = [offsets, home, home_fixed, *nears]
+    operands = [home, home_fixed, *beads, *nears]
     if fixed is not None:
         operands += list(fixed)
     if not first:
@@ -450,9 +457,10 @@
         outs = (shape(6 * slots),)
     else:
         outs = (shape(3 * slots),)
+    pitch = slots + SUB
+    if own:
+        outs += (shape(9 * pitch + 6 * SUB),)
     vmem = pl.BlockSpec(memory_space=pltpu.VMEM)
-    smem = pl.BlockSpec(memory_space=pltpu.SMEM)
-    pitch = slots + SUB
     capacity = 3 * slots + 2 * SUB + 1
     count = len(rows)
     return pl.pallas_call(
@@ -471,10 +479,9 @@
             side=side,
         ),
         out_shape=outs,
-        in_specs=[smem] + [vmem] * (len(operands) - 1),
+        in_specs=[vmem] * len(operands),
         out_specs=tuple(vmem for _ in outs),
         scratch_shapes=[
-            pltpu.VMEM((9 * pitch, lanes), F32),
             pltpu.VMEM((count * 7 * pitch, lanes), F32),
             pltpu.VMEM((4 * slots, lanes), F32),
             pltpu.VMEM((count * 4 * slots, lanes), F32),
@@ -492,7 +499,7 @@
 
 
 def kick_kernel(*refs, slots, lanes):
-    sources, out, held, done = refs[:5], refs[5], refs[6:11], refs[11]
+    sources, out, held, done = refs[:6], refs[6], refs[7:13], refs[13]
     copies = [
         pltpu.make_async_copy(source, target, done.at[i])
         for i, (source, target) in enumerate(zip(sources, held))
@@ -501,7 +508,7 @@
         copy.start()
     for copy in copies:
         copy.wait()
-    position, velocity, force, seed, count = held
+    position, velocity, force, seed, count, strain = held
     for c in range(3):
         for g in range(slots // SUB):
             at = c * slots + g * SUB
@@ -510,7 +517,11 @@
             out[rows, :] = position[rows, :] + F32(TIME_STEP) * v
             out[3 * slots + at : 3 * slots + at + SUB, :] = v
     out[6 * slots : 7 * slots, :] = seed[...].astype(F32)
-    out[7 * slots : 7 * slots + SUB, :] = jnp.broadcast_to(count[...], (SUB, lanes)).astype(F32)
+    aside = jnp.broadcast_to(count[...], (SUB, lanes)).astype(F32)
+    row = lax.broadcasted_iota(jnp.int32, (SUB, lanes), 0)
+    for step in range(strain.shape[1]):
+        aside = jnp.where(row == 1 + step, strain[:, step : step + 1].astype(F32), aside)
+    out[7 * slots : 7 * slots + SUB, :] = aside
 
 
 def ring(count, by):
@@ -530,13 +541,14 @@
     flat = lambda a: a.reshape(-1, lanes)
     tall = 7 * slots + SUB
     inputs = [flat(a) for a in (positions, velocities, forces_prev, seeds, counts)]
+    inputs.append(offsets.reshape(1, -1))
     state = pl.pallas_call(
         functools.partial(kick_kernel, slots=slots, lanes=lanes),
         out_shape=jax.ShapeDtypeStruct((tall, lanes), F32),
-        in_specs=[pl.BlockSpec(memory_space=pltpu.HBM)] * 5,
+        in_specs=[pl.BlockSpec(memory_space=pltpu.HBM)] * len(inputs),
         out_specs=pl.BlockSpec(memory_space=pltpu.VMEM),
         scratch_shapes=[pltpu.VMEM(a.shape, a.dtype) for a in inputs]
-        + [pltpu.SemaphoreType.DMA((5,))],
+        + [pltpu.SemaphoreType.DMA((len(inputs),))],
         compiler_params=pltpu.CompilerParams(vmem_limit_bytes=KICK_LIMIT),
         name="kick",
     )(*inputs)
@@ -550,10 +562,11 @@
             planes.append(lax.ppermute(state, "gz", ring(gz, 1)))
         up, down = 0, len(planes) - 1
         call = functools.partial(
-            pairs, offsets, state, home_fixed, step=step, virial=final, slots=slots
+            pairs, state, home_fixed, step=step, virial=final, slots=slots
         )
         here = (0, 0)
-        carried = call(
+        *carried, beads = call(
+            [],
             [state],
             [home_fixed] if final else None,
             None,
@@ -561,7 +574,7 @@
             last=False,
             cost=100_000_000,
         )
-        planes, carried = lax.optimization_barrier((planes, carried))
+        planes, carried, beads = lax.optimization_barrier((planes, carried, beads))
         stacked = jnp.concatenate([state, *planes], axis=0)
         far = lax.ppermute(stacked, "xy", swap(xy, 1))
         near = lax.ppermute(stacked, "xy", swap(xy, 0))
@@ -569,6 +582,7 @@
         if not final:
             kept = arrived
         carried = call(
+            [beads],
             planes,
             kept[0] if final else None,
             carried,
@@ -581,6 +595,7 @@
         )
         for side in (NEAR_SIDE, FAR_SIDE):
             carried = call(
+                [beads],
                 arrived[side],
                 kept[side] if final else None,
                 carried,

time: 47.2 us -> 44 us (0.932); the launches traced: 47.2 us -> 43.4 us
  Pallas kernels: 35.4 us -> 31.3 us
  waiting for transfers between devices: 0.28 us -> 1.16 us
  starting transfers between devices: 9.76 us -> 9.22 us
    pallas_call x8, Pallas kernels: 33.9 us -> 29.7 us  [pairs(): pl.pallas_call(functools.partial(pair_kernel, slots=slots, lanes=lanes, s...]
    ppermute x2, waiting for transfers between devices: 0.27 us -> 1.15 us  [shards(): planes = [lax.ppermute(state, 'gz', ring(gz, -1))]]
  transfers between devices with their start and end apart: 6 -> 6, of which waited for: 1 -> 2; matrix products, arithmetic and copies ran while one was open for 0% -> 0% of each run, Pallas kernels for 51% -> 47%
where the time goes in v4:
time: 44 us; the launch traced here: 43.4 us
  Pallas kernels  31.3 us (71%)
  starting transfers between devices  9.22 us (21%)
  waiting for transfers between devices  1.16 us (3%)
  local copies, waits for them, and re-layouts  0.94 us (2%)
  between operations  0.74 us (2%)
    pallas_call x8, Pallas kernels, pairs(): pl.pallas_call(functools.partial(pair_kernel, slots=slots, lanes=lanes, s...  29.7 us
    ppermute x2, starting transfers between devices, shards(): far = lax.ppermute(stacked, 'xy', swap(xy, 1))  4.98 us
    ppermute x2, starting transfers between devices, shards(): planes = [lax.ppermute(state, 'gz', ring(gz, -1))]  4.1 us
    pallas_call x1, Pallas kernels, shards(): pl.pallas_call(functools.partial(kick_kernel, slots=slots, lanes=lanes),...  1.62 us
    ppermute x2, waiting for transfers between devices, shards(): planes = [lax.ppermute(state, 'gz', ring(gz, -1))]  1.15 us
    unnamed x4, local copies, waits for them, and re-layouts  0.94 us
  transfers between devices with their start and end apart: 6, of which 2 were waited for; matrix products, arithmetic and copies ran while one was open for 0% of the time, Pallas kernels for 47%

profile of v4, /device:TPU:0, one launch (start us, length us, event | category | flops | bytes accessed | tf_op | source)
XLA Modules:
  0.0 43.4 jit_solution(17199780716160035537)
XLA Ops:
  0.6 1.6 %kick.1.refs_0_.refs_1_.refs_2_.refs_3_ = f32[232,128]{1,0:T(8,128)} custom-call(f32[96,128]{1,0:T(8,128)} %bitcast.15, f32[96,128]{1,0:T(8,128)} %bitcast.16, f32[96,128]{1,0:T(8,128)} %bitcast.17, s32[32,128]{1,0:T(8,128)} %bitcast.18, s32[1,128]{1,0:T(1,128)} %bitcast.19, s32[1,2]{1,0:T(1,128)} %bitcast.20), custom_call_target="tpu_custom_call" | custom-call | tf_op jit(solution)/shard_map/kick/pallas_call | solution.py:545
  2.3 3.0 %collective-permute-start = (f32[232,128]{1,0:T(8,128)}, f32[232,128]{1,0:T(8,128)S(1)}, u32[]{:S(2)}, u32[]{:S(2)}) collective-permute-start(f32[232,128]{1,0:T(8,128)} %kick.1.refs_0_.refs_1_.refs_2_.refs_3_), channel_id=1, source_target_pairs={{0,1},{1,0},{2,3},{3,2},{4,5},{5,4},{6,7},{7,6},{8,9},{9,8},{10,11... | collective-permute-start | bytes 356360 | tf_op jit(solution)/shard_map/ppermute | solution.py:560
  5.3 0.0 copy-start
  5.3 0.9 %copy-done = f32[232,128]{1,0:T(8,128)S(1)} copy-done((f32[232,128]{1,0:T(8,128)S(1)}, f32[232,128]{1,0:T(8,128)}, u32[]{:S(2)}) %copy-start) | copy-done | bytes 118808
  6.2 0.0 copy-start.1
  6.2 2.4 %pairs_0_0.2 = (f32[96,128]{1,0:T(8,128)S(1)}, f32[408,128]{1,0:T(8,128)S(1)}) custom-call(f32[232,128]{1,0:T(8,128)S(1)} %copy-done, f32[232,128]{1,0:T(8,128)S(1)} %copy-done, f32[232,128]{1,0:T(8,128)S(1)} %copy-done), custom_call_target="tpu_custom_call" | custom-call | flops 100000000 | bytes 1 | tf_op jit(solution)/shard_map/pairs_0_0/pallas_call | solution.py:466
  8.6 0.1 collective-permute-done.refs_3_.refs_4_
  8.7 0.0 copy-done.1
  8.8 0.1 collective-permute-start.2
  8.8 4.9 %collective-permute-start.1 = (f32[464,128]{1,0:T(8,128)S(1)}, f32[464,128]{1,0:T(8,128)S(1)}, u32[]{:S(2)}, u32[]{:S(2)}) collective-permute-start(f32[464,128]{1,0:T(8,128)S(1)} %pad_maximum_fusion), channel_id=1, source_target_pairs={{2,4},{6,8},{10,12},{14,16},{18,20},{22,24},{26,28},{30,0},{4,2},{... | collective-permute-start | bytes 712712 | tf_op jit(solution)/shard_map/ppermute | solution.py:579
  13.7 3.4 %pairs_0_0.3.refs_4_ = f32[96,128]{1,0:T(8,128)S(1)} custom-call(f32[232,128]{1,0:T(8,128)S(1)} %copy-done.1, f32[232,128]{1,0:T(8,128)S(1)} %copy-done.1, f32[408,128]{1,0:T(8,128)S(1)} %get-tuple-element.24.refs_2_, f32[232,128]{1,0:T(8,128)S(1)} %collective-permute-done.refs_3_.refs_4_, f32[96,128]{1,0:T(8,128)S(1)} %get-tuple-element.26.refs_4_), custom_call_target="tpu_custom_call" | custom-call | flops 100000000 | bytes 1 | tf_op jit(solution)/shard_map/pairs_0_0/pallas_call | solution.py:466
  17.1 0.0 collective-permute-done.2.refs_3_.refs_4_
  17.1 4.3 %pairs_1_0.1.refs_4_ = f32[96,128]{1,0:T(8,128)S(1)} custom-call(f32[232,128]{1,0:T(8,128)S(1)} %copy-done.1, f32[232,128]{1,0:T(8,128)S(1)} %copy-done.1, f32[408,128]{1,0:T(8,128)S(1)} %get-tuple-element.24.refs_2_, f32[464,128]{1,0:T(8,128)S(1)} %collective-permute-done.2.refs_3_.refs_4_, f32[96,128]{1,0:T(8,128)S(1)} %pairs_0_0.3.refs_4_), custom_call_target="tpu_custom_call" | custom-call | flops 100000000 | bytes 1 | tf_op jit(solution)/shard_map/pairs_1_0/pallas_call | solution.py:466
  21.5 0.0 collective-permute-done.1.refs_3_.refs_4_
  21.5 4.1 %pairs_2_0.1.refs_0_.refs_2_ = f32[192,128]{1,0:T(8,128)S(1)} custom-call(f32[232,128]{1,0:T(8,128)S(1)} %copy-done.1, f32[232,128]{1,0:T(8,128)S(1)} %copy-done.1, f32[408,128]{1,0:T(8,128)S(1)} %get-tuple-element.24.refs_2_, f32[464,128]{1,0:T(8,128)S(1)} %collective-permute-done.1.refs_3_.refs_4_, f32[96,128]{1,0:T(8,128)S(1)} %pairs_1_0.1.refs_4_), custom_call_target="tpu_custom_call" | custom-call | flops 100000000 | bytes 1 | tf_op jit(solution)/shard_map/pairs_2_0/pallas_call | solution.py:466
  25.6 1.1 %collective-permute-start.3 = (f32[192,128]{1,0:T(8,128)S(1)}, f32[192,128]{1,0:T(8,128)S(1)}, u32[]{:S(2)}, u32[]{:S(2)}) collective-permute-start(f32[192,128]{1,0:T(8,128)S(1)} %pairs_2_0.1.refs_0_.refs_2_), channel_id=1, source_target_pairs={{0,1},{1,0},{2,3},{3,2},{4,5},{5,4},{6,7},{7,6},{8,9},{9,8},{10,11... | collective-permute-start | bytes 294920 | tf_op jit(solution)/shard_map/ppermute | solution.py:560
  26.7 2.6 %pairs_0_1.2 = (f32[96,128]{1,0:T(8,128)S(1)}, f32[48,128]{1,0:T(8,128)S(1)}, f32[408,128]{1,0:T(8,128)S(1)}) custom-call(f32[192,128]{1,0:T(8,128)S(1)} %pairs_2_0.1.refs_0_.refs_2_, f32[232,128]{1,0:T(8,128)S(1)} %copy-done.1, f32[192,128]{1,0:T(8,128)S(1)} %pairs_2_0.1.refs_0_.refs_2_, f32[232,128]{1,0:T(8,128)S(1)} %copy-done.1), custom_call_target="tpu_custom_call" | custom-call | flops 100000000 | bytes 1 | tf_op jit(solution)/shard_map/pairs_0_1/pallas_call | solution.py:466
  29.3 1.0 %collective-permute-done.3.refs_3_ = f32[192,128]{1,0:T(8,128)S(1)} collective-permute-done((f32[192,128]{1,0:T(8,128)S(1)}, f32[192,128]{1,0:T(8,128)S(1)}, u32[]{:S(2)}, u32[]{:S(2)}) %collective-permute-start.3) | collective-permute-done | bytes 98336 | tf_op jit(solution)/shard_map/ppermute | solution.py:560
  30.3 0.1 collective-permute-start.5
  30.4 0.1 collective-permute-start.4
  30.5 3.5 %pairs_0_1.3 = (f32[96,128]{1,0:T(8,128)S(1)}, f32[48,128]{1,0:T(8,128)S(1)}) custom-call(f32[192,128]{1,0:T(8,128)S(1)} %pairs_2_0.1.refs_0_.refs_2_, f32[232,128]{1,0:T(8,128)S(1)} %copy-done.1, f32[408,128]{1,0:T(8,128)S(1)} %get-tuple-element.30.refs_2_, f32[192,128]{1,0:T(8,128)S(1)} %collective-permute-done.3.refs_3_, ...), custom_call_target="tpu_custom_call" | custom-call | flops 100000000 | bytes 1 | tf_op jit(solution)/shard_map/pairs_0_1/pallas_call | solution.py:466
  34.0 0.0 collective-permute-done.5.refs_3_
  34.1 4.3 %pairs_1_1.1 = (f32[96,128]{1,0:T(8,128)S(1)}, f32[48,128]{1,0:T(8,128)S(1)}) custom-call(f32[192,128]{1,0:T(8,128)S(1)} %pairs_2_0.1.refs_0_.refs_2_, f32[232,128]{1,0:T(8,128)S(1)} %copy-done.1, f32[408,128]{1,0:T(8,128)S(1)} %get-tuple-element.30.refs_2_, f32[384,128]{1,0:T(8,128)S(1)} %collective-permute-done.5.refs_3_, ...), custom_call_target="tpu_custom_call" | custom-call | flops 100000000 | bytes 1 | tf_op jit(solution)/shard_map/pairs_1_1/pallas_call | solution.py:466
  38.4 0.0 collective-permute-done.4.refs_3_
  38.4 5.0 %pairs_2_1.1 = (f32[96,128]{1,0:T(8,128)}, f32[96,128]{1,0:T(8,128)}, f32[6,1,128]{2,1,0:T(1,128)}) custom-call(f32[192,128]{1,0:T(8,128)S(1)} %pairs_2_0.1.refs_0_.refs_2_, f32[232,128]{1,0:T(8,128)S(1)} %copy-done.1, f32[408,128]{1,0:T(8,128)S(1)} %get-tuple-element.30.refs_2_, f32[384,128]{1,0:T(8,128)S(1)} %collective-permute-done.4.refs_3_, ...), custom_call_target="tpu_custom_call" | custom-call | flops 100000000 | bytes 1 | tf_op jit(solution)/shard_map/pairs_2_1/pallas_call | solution.py:466
  (2 shorter events, 0.0 us)
Async XLA Ops:
  2.3 6.5 %collective-permute-start = (f32[232,128]{1,0:T(8,128)}, f32[232,128]{1,0:T(8,128)S(1)}, u32[]{:S(2)}, u32[]{:S(2)}) collective-permute-start(f32[232,128]{1,0:T(8,128)} %kick.1.refs_0_.refs_1_.refs_2_.refs_3_), channel_id=1, source_target_pairs={{0,1},{1,0},{2,3},{3,2},{4,5},{5,4},{6,7},{7,6},{8,9},{9,8},{10,11... | collective-permute-start | bytes 356360 | tf_op jit(solution)/shard_map/ppermute | solution.py:560
  5.3 0.9 %copy-start = (f32[232,128]{1,0:T(8,128)S(1)}, f32[232,128]{1,0:T(8,128)}, u32[]{:S(2)}) copy-start(f32[232,128]{1,0:T(8,128)} %kick.1.refs_0_.refs_1_.refs_2_.refs_3_) | copy-start | bytes 356356
  6.2 2.5 %copy-start.1 = (f32[232,128]{1,0:T(8,128)S(1)}, f32[232,128]{1,0:T(8,128)}, u32[]{:S(2)}) copy-start(f32[232,128]{1,0:T(8,128)} %kick.1.refs_0_.refs_1_.refs_2_.refs_3_) | copy-start | bytes 356356
  8.8 8.4 %collective-permute-start.2 = (f32[464,128]{1,0:T(8,128)S(1)}, f32[464,128]{1,0:T(8,128)S(1)}, u32[]{:S(2)}, u32[]{:S(2)}) collective-permute-start(f32[464,128]{1,0:T(8,128)S(1)} %pad_maximum_fusion), channel_id=1, source_target_pairs={{0,2},{4,6},{8,10},{12,14},{16,18},{20,22},{24,26},{28,30},{2,0},{... | collective-permute-start | bytes 712712 | tf_op jit(solution)/shard_map/ppermute | solution.py:580
  8.8 12.7 %collective-permute-start.1 = (f32[464,128]{1,0:T(8,128)S(1)}, f32[464,128]{1,0:T(8,128)S(1)}, u32[]{:S(2)}, u32[]{:S(2)}) collective-permute-start(f32[464,128]{1,0:T(8,128)S(1)} %pad_maximum_fusion), channel_id=1, source_target_pairs={{2,4},{6,8},{10,12},{14,16},{18,20},{22,24},{26,28},{30,0},{4,2},{... | collective-permute-start | bytes 712712 | tf_op jit(solution)/shard_map/ppermute | solution.py:579
  25.6 4.7 %collective-permute-start.3 = (f32[192,128]{1,0:T(8,128)S(1)}, f32[192,128]{1,0:T(8,128)S(1)}, u32[]{:S(2)}, u32[]{:S(2)}) collective-permute-start(f32[192,128]{1,0:T(8,128)S(1)} %pairs_2_0.1.refs_0_.refs_2_), channel_id=1, source_target_pairs={{0,1},{1,0},{2,3},{3,2},{4,5},{5,4},{6,7},{7,6},{8,9},{9,8},{10,11... | collective-permute-start | bytes 294920 | tf_op jit(solution)/shard_map/ppermute | solution.py:560
  30.3 3.7 %collective-permute-start.5 = (f32[384,128]{1,0:T(8,128)S(1)}, f32[384,128]{1,0:T(8,128)S(1)}, u32[]{:S(2)}, u32[]{:S(2)}) collective-permute-start(f32[384,128]{1,0:T(8,128)S(1)} %pad_maximum_fusion.1), channel_id=1, source_target_pairs={{0,2},{4,6},{8,10},{12,14},{16,18},{20,22},{24,26},{28,30},{2,0},{... | collective-permute-start | bytes 589832 | tf_op jit(solution)/shard_map/ppermute | solution.py:580
  30.4 8.0 %collective-permute-start.4 = (f32[384,128]{1,0:T(8,128)S(1)}, f32[384,128]{1,0:T(8,128)S(1)}, u32[]{:S(2)}, u32[]{:S(2)}) collective-permute-start(f32[384,128]{1,0:T(8,128)S(1)} %pad_maximum_fusion.1), channel_id=1, source_target_pairs={{2,4},{6,8},{10,12},{14,16},{18,20},{22,24},{26,28},{30,0},{4,2},{... | collective-permute-start | bytes 589832 | tf_op jit(solution)/shard_map/ppermute | solution.py:579

commit v5 on v4

--- a/solution.py
+++ b/solution.py
@@ -310,23 +310,35 @@
         v = gathered(near, at, index)
         return pltpu.roll(v, (-dx) % lanes, 1) if dx else v
 
-    def fill_near(base, slot, dx, filled):
-        def fill(k, _):
-            for i, index in enumerate(choose(slot, k)):
-                valid = index >= 0
-                if dx:
-                    index = pltpu.roll(index, dx % lanes, 1)
-                values = [gather_near(base + c * pitch, index, dx) for c in range(7)]
-                values[0] = jnp.where(valid, values[0] + F32(EDGE * dx), FAR)
-                values = values[:6] + list(near_noise(values[6]))
-                for c in range(9):
-                    at = c * capacity + filled + k * (2 * SUB) + i * SUB
-                    liste[pl.ds(at, SUB), :] = values[c]
+    def fill_near(base, slot, dx, filled, k):
+        for i, index in enumerate(choose(slot, k)):
+            valid = index >= 0
+            if dx:
+                index = pltpu.roll(index, dx % lanes, 1)
+            values = [gather_near(base + c * pitch, index, dx) for c in range(7)]
+            values[0] = jnp.where(valid, values[0] + F32(EDGE * dx), FAR)
+            values = values[:6] + list(near_noise(values[6]))
+            for c in range(9):
+                at = c * capacity + filled + k * (2 * SUB) + i * SUB
+                liste[pl.ds(at, SUB), :] = values[c]
+
+    def fill_home(slot, k):
+        for i, index in enumerate(choose(slot, k)):
+            for c in range(9):
+                v = gathered(home, c * pitch, index)
+                if c == 0:
+                    v = jnp.where(index >= 0, v, -FAR)
+                pick[pl.ds(aligned(c * pitch + k * (2 * SUB) + i * SUB), SUB), :] = v
+
+    def steps(size):
+        return (size + 2 * SUB - 1) // (2 * SUB)
+
+    def each(first, size, fill):
+        def body(k, _):
+            fill(k)
             return 0
 
-        size = sizes[slot]
-        lax.fori_loop(0, (size + 2 * SUB - 1) // (2 * SUB), fill, 0)
-        return filled + size
+        lax.fori_loop(first, steps(size), body, 0)
 
     def close(filled):
         liste[pl.ds(filled, SUB), :] = jnp.full((SUB, lanes), FAR, F32)
@@ -346,10 +358,11 @@
             for c in range(9):
                 at = c * capacity + g * SUB
                 liste[at : at + SUB, :] = values[c]
-        close(fill_near(0, 2, 1, slots))
+        size = sizes[2]
+        each(0, size, functools.partial(fill_near, 0, 2, 1, slots))
+        close(slots + size)
         run_pairs(slots, home, groups)
         collect()
-        size = sizes[2]
         run_pairs(size, home, groups, start=slots, react=True)
         collect()
 
@@ -372,23 +385,25 @@
 
     def direction(r, _):
         base = r * (7 * pitch)
-        filled = jnp.int32(0)
-        for d, dx in enumerate((0, -1, 1)):
-            filled = fill_near(base, 4 * r + d, dx, filled)
-        close(filled)
         slot = 4 * r + 3
         needed = (sizes[slot] + SUB - 1) // SUB
-
-        def fill_home(k, _):
-            for i, index in enumerate(choose(slot, k)):
-                for c in range(9):
-                    v = gathered(home, c * pitch, index)
-                    if c == 0:
-                        v = jnp.where(index >= 0, v, -FAR)
-                    pick[pl.ds(aligned(c * pitch + k * (2 * SUB) + i * SUB), SUB), :] = v
-            return 0
-
-        lax.fori_loop(0, (needed + 1) // 2, fill_home, 0)
+        parts, filled, longest = [], jnp.int32(0), sizes[slot]
+        for d, dx in enumerate((0, -1, 1)):
+            size = sizes[4 * r + d]
+            parts.append((size, functools.partial(fill_near, base, 4 * r + d, dx, filled)))
+            filled = filled + size
+            longest = jnp.maximum(longest, size)
+
+        @pl.when(longest > 2 * SUB)
+        def _():
+            for size, fill in parts:
+                each(1, size, fill)
+            each(1, sizes[slot], functools.partial(fill_home, slot))
+
+        for _, fill in parts:
+            fill(jnp.int32(0))
+        fill_home(slot, jnp.int32(0))
+        close(filled)
         for blocks in range(1, groups + 1):
             pl.when(needed == blocks)(functools.partial(run_pairs, filled, pick, blocks))
 

time: 44 us -> 41.2 us (0.936)
  Pallas kernels: 31.3 us -> 27.1 us
  starting transfers between devices: 9.22 us -> 10.7 us
    pallas_call x8, Pallas kernels: 29.7 us -> 25.5 us  [pairs(): pl.pallas_call(functools.partial(pair_kernel, slots=slots, lanes=lanes, s...]
    ppermute x2, starting transfers between devices: 4.98 us -> 5.78 us  [shards(): far = lax.ppermute(stacked, 'xy', swap(xy, 1))]
    ppermute x2, starting transfers between devices: 4.1 us -> 4.74 us  [shards(): planes = [lax.ppermute(state, 'gz', ring(gz, -1))]]
  transfers between devices with their start and end apart: 6 -> 6, of which waited for: 2 -> 2; matrix products, arithmetic and copies ran while one was open for 0% -> 0% of each run, Pallas kernels for 47% -> 43%
where the time goes in v5:
time: 41.2 us; the launch traced here: 40.9 us
  Pallas kernels  27.1 us (66%)
  starting transfers between devices  10.7 us (26%)
  waiting for transfers between devices  1.51 us (4%)
  local copies, waits for them, and re-layouts  0.94 us (2%)
  between operations  0.73 us (2%)
    pallas_call x8, Pallas kernels, pairs(): pl.pallas_call(functools.partial(pair_kernel, slots=slots, lanes=lanes, s...  25.5 us
    ppermute x2, starting transfers between devices, shards(): far = lax.ppermute(stacked, 'xy', swap(xy, 1))  5.78 us
    ppermute x2, starting transfers between devices, shards(): planes = [lax.ppermute(state, 'gz', ring(gz, -1))]  4.74 us
    pallas_call x1, Pallas kernels, shards(): pl.pallas_call(functools.partial(kick_kernel, slots=slots, lanes=lanes),...  1.62 us
    ppermute x2, waiting for transfers between devices, shards(): planes = [lax.ppermute(state, 'gz', ring(gz, -1))]  1.5 us
    unnamed x4, local copies, waits for them, and re-layouts  0.94 us
  transfers between devices with their start and end apart: 6, of which 2 were waited for; matrix products, arithmetic and copies ran while one was open for 0% of the time, Pallas kernels for 43%

profile of v5, /device:TPU:0, one launch (start us, length us, event | category | flops | bytes accessed | tf_op | source)
XLA Modules:
  0.0 40.9 jit_solution(13231093698236728466)
XLA Ops:
  0.6 1.6 %kick.1.refs_0_.refs_1_.refs_2_.refs_3_ = f32[232,128]{1,0:T(8,128)} custom-call(f32[96,128]{1,0:T(8,128)} %bitcast.15, f32[96,128]{1,0:T(8,128)} %bitcast.16, f32[96,128]{1,0:T(8,128)} %bitcast.17, s32[32,128]{1,0:T(8,128)} %bitcast.18, s32[1,128]{1,0:T(1,128)} %bitcast.19, s32[1,2]{1,0:T(1,128)} %bitcast.20), custom_call_target="tpu_custom_call" | custom-call | tf_op jit(solution)/shard_map/kick/pallas_call | solution.py:560
  2.3 3.0 %collective-permute-start = (f32[232,128]{1,0:T(8,128)}, f32[232,128]{1,0:T(8,128)S(1)}, u32[]{:S(2)}, u32[]{:S(2)}) collective-permute-start(f32[232,128]{1,0:T(8,128)} %kick.1.refs_0_.refs_1_.refs_2_.refs_3_), channel_id=1, source_target_pairs={{0,1},{1,0},{2,3},{3,2},{4,5},{5,4},{6,7},{7,6},{8,9},{9,8},{10,11... | collective-permute-start | bytes 356360 | tf_op jit(solution)/shard_map/ppermute | solution.py:575
  5.3 0.0 copy-start
  5.3 0.9 %copy-done = f32[232,128]{1,0:T(8,128)S(1)} copy-done((f32[232,128]{1,0:T(8,128)S(1)}, f32[232,128]{1,0:T(8,128)}, u32[]{:S(2)}) %copy-start) | copy-done | bytes 118808
  6.2 0.0 copy-start.1
  6.2 1.9 %pairs_0_0.2 = (f32[96,128]{1,0:T(8,128)S(1)}, f32[408,128]{1,0:T(8,128)S(1)}) custom-call(f32[232,128]{1,0:T(8,128)S(1)} %copy-done, f32[232,128]{1,0:T(8,128)S(1)} %copy-done, f32[232,128]{1,0:T(8,128)S(1)} %copy-done), custom_call_target="tpu_custom_call" | custom-call | flops 100000000 | bytes 1 | tf_op jit(solution)/shard_map/pairs_0_0/pallas_call | solution.py:481
  8.1 0.6 %collective-permute-done.refs_3_.refs_4_ = f32[232,128]{1,0:T(8,128)S(1)} collective-permute-done((f32[232,128]{1,0:T(8,128)}, f32[232,128]{1,0:T(8,128)S(1)}, u32[]{:S(2)}, u32[]{:S(2)}) %collective-permute-start) | collective-permute-done | bytes 118816 | tf_op jit(solution)/shard_map/ppermute | solution.py:575
  8.7 0.0 copy-done.1
  8.8 0.1 collective-permute-start.2
  8.8 4.9 %collective-permute-start.1 = (f32[464,128]{1,0:T(8,128)S(1)}, f32[464,128]{1,0:T(8,128)S(1)}, u32[]{:S(2)}, u32[]{:S(2)}) collective-permute-start(f32[464,128]{1,0:T(8,128)S(1)} %pad_maximum_fusion), channel_id=1, source_target_pairs={{2,4},{6,8},{10,12},{14,16},{18,20},{22,24},{26,28},{30,0},{4,2},{... | collective-permute-start | bytes 712712 | tf_op jit(solution)/shard_map/ppermute | solution.py:594
  13.7 2.9 %pairs_0_0.3.refs_4_ = f32[96,128]{1,0:T(8,128)S(1)} custom-call(f32[232,128]{1,0:T(8,128)S(1)} %copy-done.1, f32[232,128]{1,0:T(8,128)S(1)} %copy-done.1, f32[408,128]{1,0:T(8,128)S(1)} %get-tuple-element.24.refs_2_, f32[232,128]{1,0:T(8,128)S(1)} %collective-permute-done.refs_3_.refs_4_, f32[96,128]{1,0:T(8,128)S(1)} %get-tuple-element.26.refs_4_), custom_call_target="tpu_custom_call" | custom-call | flops 100000000 | bytes 1 | tf_op jit(solution)/shard_map/pairs_0_0/pallas_call | solution.py:481
  16.7 0.0 collective-permute-done.2.refs_3_.refs_4_
  16.7 3.6 %pairs_1_0.1.refs_4_ = f32[96,128]{1,0:T(8,128)S(1)} custom-call(f32[232,128]{1,0:T(8,128)S(1)} %copy-done.1, f32[232,128]{1,0:T(8,128)S(1)} %copy-done.1, f32[408,128]{1,0:T(8,128)S(1)} %get-tuple-element.24.refs_2_, f32[464,128]{1,0:T(8,128)S(1)} %collective-permute-done.2.refs_3_.refs_4_, f32[96,128]{1,0:T(8,128)S(1)} %pairs_0_0.3.refs_4_), custom_call_target="tpu_custom_call" | custom-call | flops 100000000 | bytes 1 | tf_op jit(solution)/shard_map/pairs_1_0/pallas_call | solution.py:481
  20.3 0.0 collective-permute-done.1.refs_3_.refs_4_
  20.3 3.6 %pairs_2_0.1.refs_0_.refs_2_ = f32[192,128]{1,0:T(8,128)S(1)} custom-call(f32[232,128]{1,0:T(8,128)S(1)} %copy-done.1, f32[232,128]{1,0:T(8,128)S(1)} %copy-done.1, f32[408,128]{1,0:T(8,128)S(1)} %get-tuple-element.24.refs_2_, f32[464,128]{1,0:T(8,128)S(1)} %collective-permute-done.1.refs_3_.refs_4_, f32[96,128]{1,0:T(8,128)S(1)} %pairs_1_0.1.refs_4_), custom_call_target="tpu_custom_call" | custom-call | flops 100000000 | bytes 1 | tf_op jit(solution)/shard_map/pairs_2_0/pallas_call | solution.py:481
  23.9 1.7 %collective-permute-start.3 = (f32[192,128]{1,0:T(8,128)S(1)}, f32[192,128]{1,0:T(8,128)S(1)}, u32[]{:S(2)}, u32[]{:S(2)}) collective-permute-start(f32[192,128]{1,0:T(8,128)S(1)} %pairs_2_0.1.refs_0_.refs_2_), channel_id=1, source_target_pairs={{0,1},{1,0},{2,3},{3,2},{4,5},{5,4},{6,7},{7,6},{8,9},{9,8},{10,11... | collective-permute-start | bytes 294920 | tf_op jit(solution)/shard_map/ppermute | solution.py:575
  25.6 2.1 %pairs_0_1.2 = (f32[96,128]{1,0:T(8,128)S(1)}, f32[48,128]{1,0:T(8,128)S(1)}, f32[408,128]{1,0:T(8,128)S(1)}) custom-call(f32[192,128]{1,0:T(8,128)S(1)} %pairs_2_0.1.refs_0_.refs_2_, f32[232,128]{1,0:T(8,128)S(1)} %copy-done.1, f32[192,128]{1,0:T(8,128)S(1)} %pairs_2_0.1.refs_0_.refs_2_, f32[232,128]{1,0:T(8,128)S(1)} %copy-done.1), custom_call_target="tpu_custom_call" | custom-call | flops 100000000 | bytes 1 | tf_op jit(solution)/shard_map/pairs_0_1/pallas_call | solution.py:481
  27.7 0.9 %collective-permute-done.3.refs_3_ = f32[192,128]{1,0:T(8,128)S(1)} collective-permute-done((f32[192,128]{1,0:T(8,128)S(1)}, f32[192,128]{1,0:T(8,128)S(1)}, u32[]{:S(2)}, u32[]{:S(2)}) %collective-permute-start.3) | collective-permute-done | bytes 98336 | tf_op jit(solution)/shard_map/ppermute | solution.py:575
  28.6 0.1 collective-permute-start.5
  28.7 0.9 %collective-permute-start.4 = (f32[384,128]{1,0:T(8,128)S(1)}, f32[384,128]{1,0:T(8,128)S(1)}, u32[]{:S(2)}, u32[]{:S(2)}) collective-permute-start(f32[384,128]{1,0:T(8,128)S(1)} %pad_maximum_fusion.1), channel_id=1, source_target_pairs={{2,4},{6,8},{10,12},{14,16},{18,20},{22,24},{26,28},{30,0},{4,2},{... | collective-permute-start | bytes 589832 | tf_op jit(solution)/shard_map/ppermute | solution.py:594
  29.5 3.2 %pairs_0_1.3 = (f32[96,128]{1,0:T(8,128)S(1)}, f32[48,128]{1,0:T(8,128)S(1)}) custom-call(f32[192,128]{1,0:T(8,128)S(1)} %pairs_2_0.1.refs_0_.refs_2_, f32[232,128]{1,0:T(8,128)S(1)} %copy-done.1, f32[408,128]{1,0:T(8,128)S(1)} %get-tuple-element.30.refs_2_, f32[192,128]{1,0:T(8,128)S(1)} %collective-permute-done.3.refs_3_, ...), custom_call_target="tpu_custom_call" | custom-call | flops 100000000 | bytes 1 | tf_op jit(solution)/shard_map/pairs_0_1/pallas_call | solution.py:481
  32.8 0.0 collective-permute-done.5.refs_3_
  32.8 3.8 %pairs_1_1.1 = (f32[96,128]{1,0:T(8,128)S(1)}, f32[48,128]{1,0:T(8,128)S(1)}) custom-call(f32[192,128]{1,0:T(8,128)S(1)} %pairs_2_0.1.refs_0_.refs_2_, f32[232,128]{1,0:T(8,128)S(1)} %copy-done.1, f32[408,128]{1,0:T(8,128)S(1)} %get-tuple-element.30.refs_2_, f32[384,128]{1,0:T(8,128)S(1)} %collective-permute-done.5.refs_3_, ...), custom_call_target="tpu_custom_call" | custom-call | flops 100000000 | bytes 1 | tf_op jit(solution)/shard_map/pairs_1_1/pallas_call | solution.py:481
  36.6 0.0 collective-permute-done.4.refs_3_
  36.6 4.3 %pairs_2_1.1 = (f32[96,128]{1,0:T(8,128)}, f32[96,128]{1,0:T(8,128)}, f32[6,1,128]{2,1,0:T(1,128)}) custom-call(f32[192,128]{1,0:T(8,128)S(1)} %pairs_2_0.1.refs_0_.refs_2_, f32[232,128]{1,0:T(8,128)S(1)} %copy-done.1, f32[408,128]{1,0:T(8,128)S(1)} %get-tuple-element.30.refs_2_, f32[384,128]{1,0:T(8,128)S(1)} %collective-permute-done.4.refs_3_, ...), custom_call_target="tpu_custom_call" | custom-call | flops 100000000 | bytes 1 | tf_op jit(solution)/shard_map/pairs_2_1/pallas_call | solution.py:481
  (2 shorter events, 0.0 us)
Async XLA Ops:
  2.3 6.5 %collective-permute-start = (f32[232,128]{1,0:T(8,128)}, f32[232,128]{1,0:T(8,128)S(1)}, u32[]{:S(2)}, u32[]{:S(2)}) collective-permute-start(f32[232,128]{1,0:T(8,128)} %kick.1.refs_0_.refs_1_.refs_2_.refs_3_), channel_id=1, source_target_pairs={{0,1},{1,0},{2,3},{3,2},{4,5},{5,4},{6,7},{7,6},{8,9},{9,8},{10,11... | collective-permute-start | bytes 356360 | tf_op jit(solution)/shard_map/ppermute | solution.py:575
  5.3 0.9 %copy-start = (f32[232,128]{1,0:T(8,128)S(1)}, f32[232,128]{1,0:T(8,128)}, u32[]{:S(2)}) copy-start(f32[232,128]{1,0:T(8,128)} %kick.1.refs_0_.refs_1_.refs_2_.refs_3_) | copy-start | bytes 356356
  6.2 2.5 %copy-start.1 = (f32[232,128]{1,0:T(8,128)S(1)}, f32[232,128]{1,0:T(8,128)}, u32[]{:S(2)}) copy-start(f32[232,128]{1,0:T(8,128)} %kick.1.refs_0_.refs_1_.refs_2_.refs_3_) | copy-start | bytes 356356
  8.8 7.9 %collective-permute-start.2 = (f32[464,128]{1,0:T(8,128)S(1)}, f32[464,128]{1,0:T(8,128)S(1)}, u32[]{:S(2)}, u32[]{:S(2)}) collective-permute-start(f32[464,128]{1,0:T(8,128)S(1)} %pad_maximum_fusion), channel_id=1, source_target_pairs={{0,2},{4,6},{8,10},{12,14},{16,18},{20,22},{24,26},{28,30},{2,0},{... | collective-permute-start | bytes 712712 | tf_op jit(solution)/shard_map/ppermute | solution.py:595
  8.8 11.5 %collective-permute-start.1 = (f32[464,128]{1,0:T(8,128)S(1)}, f32[464,128]{1,0:T(8,128)S(1)}, u32[]{:S(2)}, u32[]{:S(2)}) collective-permute-start(f32[464,128]{1,0:T(8,128)S(1)} %pad_maximum_fusion), channel_id=1, source_target_pairs={{2,4},{6,8},{10,12},{14,16},{18,20},{22,24},{26,28},{30,0},{4,2},{... | collective-permute-start | bytes 712712 | tf_op jit(solution)/shard_map/ppermute | solution.py:594
  23.9 4.7 %collective-permute-start.3 = (f32[192,128]{1,0:T(8,128)S(1)}, f32[192,128]{1,0:T(8,128)S(1)}, u32[]{:S(2)}, u32[]{:S(2)}) collective-permute-start(f32[192,128]{1,0:T(8,128)S(1)} %pairs_2_0.1.refs_0_.refs_2_), channel_id=1, source_target_pairs={{0,1},{1,0},{2,3},{3,2},{4,5},{5,4},{6,7},{7,6},{8,9},{9,8},{10,11... | collective-permute-start | bytes 294920 | tf_op jit(solution)/shard_map/ppermute | solution.py:575
  28.6 4.2 %collective-permute-start.5 = (f32[384,128]{1,0:T(8,128)S(1)}, f32[384,128]{1,0:T(8,128)S(1)}, u32[]{:S(2)}, u32[]{:S(2)}) collective-permute-start(f32[384,128]{1,0:T(8,128)S(1)} %pad_maximum_fusion.1), channel_id=1, source_target_pairs={{0,2},{4,6},{8,10},{12,14},{16,18},{20,22},{24,26},{28,30},{2,0},{... | collective-permute-start | bytes 589832 | tf_op jit(solution)/shard_map/ppermute | solution.py:595
  28.7 7.9 %collective-permute-start.4 = (f32[384,128]{1,0:T(8,128)S(1)}, f32[384,128]{1,0:T(8,128)S(1)}, u32[]{:S(2)}, u32[]{:S(2)}) collective-permute-start(f32[384,128]{1,0:T(8,128)S(1)} %pad_maximum_fusion.1), channel_id=1, source_target_pairs={{2,4},{6,8},{10,12},{14,16},{18,20},{22,24},{26,28},{30,0},{4,2},{... | collective-permute-start | bytes 589832 | tf_op jit(solution)/shard_map/ppermute | solution.py:594

commit v6 on v5

--- a/solution.py
+++ b/solution.py
@@ -93,7 +93,7 @@
         (force_out,) = take(1)
     if own:
         (home,) = take(1)
-    near, answer, rank, pick, liste, part, total, tally, sizes = take(9)
+    near, answer, rank, upto, pick, liste, part, total, tally, sizes = take(10)
     groups = slots // SUB
     pitch = slots + SUB
     capacity = liste.shape[0] // 9
@@ -189,12 +189,13 @@
 
     def ranked(slot, marks):
         ones = jnp.concatenate([jnp.where(m, 1.0, 0.0) for m in marks], axis=0)
-        upto = jnp.dot(triangle, ones.astype(jnp.bfloat16), preferred_element_type=F32)
+        running = jnp.dot(triangle, ones.astype(jnp.bfloat16), preferred_element_type=F32)
+        upto[slot * slots : (slot + 1) * slots, :] = running
         for g in range(groups):
             rows_of = slice(g * SUB, (g + 1) * SUB)
-            place = jnp.where(marks[g], upto[rows_of, :] - 1.0, -1.0)
+            place = jnp.where(marks[g], running[rows_of, :] - 1.0, -1.0)
             rank[(slot * slots + g * SUB) : (slot * slots + (g + 1) * SUB), :] = place
-        sizes[slot] = jnp.max(upto[slots - 1 : slots, :]).astype(jnp.int32)
+        sizes[slot] = jnp.max(running[slots - 1 : slots, :]).astype(jnp.int32)
 
     for r, (source, offset, dz) in enumerate(rows):
         base = r * 7 * pitch
@@ -226,13 +227,30 @@
             ranked(4 * r + 3, marks)
 
     def choose(slot, k):
-        target = iota_f + (k * (2 * SUB)).astype(F32)
-        index = [jnp.full((SUB, lanes), -1, jnp.int32) for _ in range(2)]
-        for s in range(slots):
-            place = rank[pl.ds(slot * slots + s, SUB, stride=0), :]
-            for i in range(2):
-                index[i] = jnp.where(place == target + F32(i * SUB), s, index[i])
-        return index
+        at = slot * slots
+        line = lambda row: upto[pl.ds(at + row, SUB, stride=0), :]
+        ends = [line(g * SUB + SUB - 1) for g in range(groups)]
+        middles = [line(g * SUB + SUB // 2 - 1) for g in range(groups)]
+        counts = [upto[pl.ds(aligned(at + g * SUB), SUB), :] for g in range(groups)]
+        result = []
+        for i in range(2):
+            target = iota_f + ((k * (2 * SUB)).astype(F32) + F32(i * SUB))
+            beyond = [ends[g] <= target for g in range(groups - 1)]
+
+            def chosen(values):
+                v = values[0]
+                for g in range(1, groups):
+                    v = jnp.where(beyond[g - 1], values[g], v)
+                return v
+
+            first = chosen([jnp.full((SUB, lanes), g * SUB, jnp.int32) for g in range(groups)])
+            place = jnp.where(chosen(middles) <= target, SUB // 2, 0)
+            for width in (2, 1):
+                probe = place + (width - 1)
+                found = chosen([take_rows(v, probe) for v in counts])
+                place = jnp.where(found <= target, place + width, place)
+            result.append(jnp.where(ends[groups - 1] > target, first + place, -1))
+        return result
 
     def gathered(ref, base, index):
         within = index & (SUB - 1)
@@ -499,6 +517,7 @@
         scratch_shapes=[
             pltpu.VMEM((count * 7 * pitch, lanes), F32),
             pltpu.VMEM((4 * slots, lanes), F32),
+            pltpu.VMEM((count * 4 * slots, lanes), F32),
             pltpu.VMEM((count * 4 * slots, lanes), F32),
             pltpu.VMEM((9 * pitch, lanes), F32),
             pltpu.VMEM((9 * capacity, lanes), F32),

time: 41.2 us -> 40.8 us (level)
  waiting for transfers between devices: 1.51 us -> 0.8 us
  starting transfers between devices: 10.7 us -> 11.4 us
  Pallas kernels: 27.1 us -> 26.5 us
    ppermute x2, starting transfers between devices: 5.78 us -> 6.74 us  [shards(): far = lax.ppermute(stacked, 'xy', swap(xy, 1))]
    ppermute x2, waiting for transfers between devices: 1.5 us -> 0.79 us  [shards(): planes = [lax.ppermute(state, 'gz', ring(gz, -1))]]
    pallas_call x8, Pallas kernels: 25.5 us -> 24.9 us  [pairs(): pl.pallas_call(functools.partial(pair_kernel, slots=slots, lanes=lanes, s...]
  transfers between devices with their start and end apart: 6 -> 6, of which waited for: 2 -> 2; matrix products, arithmetic and copies ran while one was open for 0% -> 0% of each run, Pallas kernels for 43% -> 45%
where the time goes in v6:
time: 40.8 us; the launch traced here: 40.4 us
  Pallas kernels  26.5 us (65%)
  starting transfers between devices  11.4 us (28%)
  local copies, waits for them, and re-layouts  0.94 us (2%)
  waiting for transfers between devices  0.8 us (2%)
  between operations  0.74 us (2%)
    pallas_call x8, Pallas kernels, pairs(): pl.pallas_call(functools.partial(pair_kernel, slots=slots, lanes=lanes, s...  24.9 us
    ppermute x2, starting transfers between devices, shards(): far = lax.ppermute(stacked, 'xy', swap(xy, 1))  6.74 us
    ppermute x2, starting transfers between devices, shards(): planes = [lax.ppermute(state, 'gz', ring(gz, -1))]  4.47 us
    pallas_call x1, Pallas kernels, shards(): pl.pallas_call(functools.partial(kick_kernel, slots=slots, lanes=lanes),...  1.62 us
    unnamed x4, local copies, waits for them, and re-layouts  0.94 us
  transfers between devices with their start and end apart: 6, of which 2 were waited for; matrix products, arithmetic and copies ran while one was open for 0% of the time, Pallas kernels for 45%

profile of v6, /device:TPU:0, one launch (start us, length us, event | category | flops | bytes accessed | tf_op | source)
XLA Modules:
  0.0 40.4 jit_solution(16369839487543088656)
XLA Ops:
  0.6 1.6 %kick.1.refs_0_.refs_1_.refs_2_.refs_3_ = f32[232,128]{1,0:T(8,128)} custom-call(f32[96,128]{1,0:T(8,128)} %bitcast.15, f32[96,128]{1,0:T(8,128)} %bitcast.16, f32[96,128]{1,0:T(8,128)} %bitcast.17, s32[32,128]{1,0:T(8,128)} %bitcast.18, s32[1,128]{1,0:T(1,128)} %bitcast.19, s32[1,2]{1,0:T(1,128)} %bitcast.20), custom_call_target="tpu_custom_call" | custom-call | tf_op jit(solution)/shard_map/kick/pallas_call | solution.py:579
  2.3 3.0 %collective-permute-start = (f32[232,128]{1,0:T(8,128)}, f32[232,128]{1,0:T(8,128)S(1)}, u32[]{:S(2)}, u32[]{:S(2)}) collective-permute-start(f32[232,128]{1,0:T(8,128)} %kick.1.refs_0_.refs_1_.refs_2_.refs_3_), channel_id=1, source_target_pairs={{0,1},{1,0},{2,3},{3,2},{4,5},{5,4},{6,7},{7,6},{8,9},{9,8},{10,11... | collective-permute-start | bytes 356360 | tf_op jit(solution)/shard_map/ppermute | solution.py:594
  5.3 0.0 copy-start
  5.3 0.9 %copy-done = f32[232,128]{1,0:T(8,128)S(1)} copy-done((f32[232,128]{1,0:T(8,128)S(1)}, f32[232,128]{1,0:T(8,128)}, u32[]{:S(2)}) %copy-start) | copy-done | bytes 118808
  6.2 0.0 copy-start.1
  6.2 2.4 %pairs_0_0.2 = (f32[96,128]{1,0:T(8,128)S(1)}, f32[408,128]{1,0:T(8,128)S(1)}) custom-call(f32[232,128]{1,0:T(8,128)S(1)} %copy-done, f32[232,128]{1,0:T(8,128)S(1)} %copy-done, f32[232,128]{1,0:T(8,128)S(1)} %copy-done), custom_call_target="tpu_custom_call" | custom-call | flops 100000000 | bytes 1 | tf_op jit(solution)/shard_map/pairs_0_0/pallas_call | solution.py:499
  8.6 0.1 collective-permute-done.refs_3_.refs_4_
  8.7 0.0 copy-done.1
  8.8 0.1 collective-permute-start.2
  8.8 4.9 %collective-permute-start.1 = (f32[464,128]{1,0:T(8,128)S(1)}, f32[464,128]{1,0:T(8,128)S(1)}, u32[]{:S(2)}, u32[]{:S(2)}) collective-permute-start(f32[464,128]{1,0:T(8,128)S(1)} %pad_maximum_fusion), channel_id=1, source_target_pairs={{2,4},{6,8},{10,12},{14,16},{18,20},{22,24},{26,28},{30,0},{4,2},{... | collective-permute-start | bytes 712712 | tf_op jit(solution)/shard_map/ppermute | solution.py:613
  13.7 2.9 %pairs_0_0.3.refs_4_ = f32[96,128]{1,0:T(8,128)S(1)} custom-call(f32[232,128]{1,0:T(8,128)S(1)} %copy-done.1, f32[232,128]{1,0:T(8,128)S(1)} %copy-done.1, f32[408,128]{1,0:T(8,128)S(1)} %get-tuple-element.24.refs_2_, f32[232,128]{1,0:T(8,128)S(1)} %collective-permute-done.refs_3_.refs_4_, f32[96,128]{1,0:T(8,128)S(1)} %get-tuple-element.26.refs_4_), custom_call_target="tpu_custom_call" | custom-call | flops 100000000 | bytes 1 | tf_op jit(solution)/shard_map/pairs_0_0/pallas_call | solution.py:499
  16.7 0.0 collective-permute-done.2.refs_3_.refs_4_
  16.7 3.1 %pairs_1_0.1.refs_4_ = f32[96,128]{1,0:T(8,128)S(1)} custom-call(f32[232,128]{1,0:T(8,128)S(1)} %copy-done.1, f32[232,128]{1,0:T(8,128)S(1)} %copy-done.1, f32[408,128]{1,0:T(8,128)S(1)} %get-tuple-element.24.refs_2_, f32[464,128]{1,0:T(8,128)S(1)} %collective-permute-done.2.refs_3_.refs_4_, f32[96,128]{1,0:T(8,128)S(1)} %pairs_0_0.3.refs_4_), custom_call_target="tpu_custom_call" | custom-call | flops 100000000 | bytes 1 | tf_op jit(solution)/shard_map/pairs_1_0/pallas_call | solution.py:499
  19.8 0.0 collective-permute-done.1.refs_3_.refs_4_
  19.8 3.1 %pairs_2_0.1.refs_0_.refs_2_ = f32[192,128]{1,0:T(8,128)S(1)} custom-call(f32[232,128]{1,0:T(8,128)S(1)} %copy-done.1, f32[232,128]{1,0:T(8,128)S(1)} %copy-done.1, f32[408,128]{1,0:T(8,128)S(1)} %get-tuple-element.24.refs_2_, f32[464,128]{1,0:T(8,128)S(1)} %collective-permute-done.1.refs_3_.refs_4_, f32[96,128]{1,0:T(8,128)S(1)} %pairs_1_0.1.refs_4_), custom_call_target="tpu_custom_call" | custom-call | flops 100000000 | bytes 1 | tf_op jit(solution)/shard_map/pairs_2_0/pallas_call | solution.py:499
  22.9 1.4 %collective-permute-start.3 = (f32[192,128]{1,0:T(8,128)S(1)}, f32[192,128]{1,0:T(8,128)S(1)}, u32[]{:S(2)}, u32[]{:S(2)}) collective-permute-start(f32[192,128]{1,0:T(8,128)S(1)} %pairs_2_0.1.refs_0_.refs_2_), channel_id=1, source_target_pairs={{0,1},{1,0},{2,3},{3,2},{4,5},{5,4},{6,7},{7,6},{8,9},{9,8},{10,11... | collective-permute-start | bytes 294920 | tf_op jit(solution)/shard_map/ppermute | solution.py:594
  24.3 2.6 %pairs_0_1.2 = (f32[96,128]{1,0:T(8,128)S(1)}, f32[48,128]{1,0:T(8,128)S(1)}, f32[408,128]{1,0:T(8,128)S(1)}) custom-call(f32[192,128]{1,0:T(8,128)S(1)} %pairs_2_0.1.refs_0_.refs_2_, f32[232,128]{1,0:T(8,128)S(1)} %copy-done.1, f32[192,128]{1,0:T(8,128)S(1)} %pairs_2_0.1.refs_0_.refs_2_, f32[232,128]{1,0:T(8,128)S(1)} %copy-done.1), custom_call_target="tpu_custom_call" | custom-call | flops 100000000 | bytes 1 | tf_op jit(solution)/shard_map/pairs_0_1/pallas_call | solution.py:499
  26.9 0.6 %collective-permute-done.3.refs_3_ = f32[192,128]{1,0:T(8,128)S(1)} collective-permute-done((f32[192,128]{1,0:T(8,128)S(1)}, f32[192,128]{1,0:T(8,128)S(1)}, u32[]{:S(2)}, u32[]{:S(2)}) %collective-permute-start.3) | collective-permute-done | bytes 98336 | tf_op jit(solution)/shard_map/ppermute | solution.py:594
  27.6 0.1 collective-permute-start.5
  27.7 1.8 %collective-permute-start.4 = (f32[384,128]{1,0:T(8,128)S(1)}, f32[384,128]{1,0:T(8,128)S(1)}, u32[]{:S(2)}, u32[]{:S(2)}) collective-permute-start(f32[384,128]{1,0:T(8,128)S(1)} %pad_maximum_fusion.1), channel_id=1, source_target_pairs={{2,4},{6,8},{10,12},{14,16},{18,20},{22,24},{26,28},{30,0},{4,2},{... | collective-permute-start | bytes 589832 | tf_op jit(solution)/shard_map/ppermute | solution.py:613
  29.5 3.6 %pairs_0_1.3 = (f32[96,128]{1,0:T(8,128)S(1)}, f32[48,128]{1,0:T(8,128)S(1)}) custom-call(f32[192,128]{1,0:T(8,128)S(1)} %pairs_2_0.1.refs_0_.refs_2_, f32[232,128]{1,0:T(8,128)S(1)} %copy-done.1, f32[408,128]{1,0:T(8,128)S(1)} %get-tuple-element.30.refs_2_, f32[192,128]{1,0:T(8,128)S(1)} %collective-permute-done.3.refs_3_, ...), custom_call_target="tpu_custom_call" | custom-call | flops 100000000 | bytes 1 | tf_op jit(solution)/shard_map/pairs_0_1/pallas_call | solution.py:499
  33.1 0.0 collective-permute-done.5.refs_3_
  33.1 3.4 %pairs_1_1.1 = (f32[96,128]{1,0:T(8,128)S(1)}, f32[48,128]{1,0:T(8,128)S(1)}) custom-call(f32[192,128]{1,0:T(8,128)S(1)} %pairs_2_0.1.refs_0_.refs_2_, f32[232,128]{1,0:T(8,128)S(1)} %copy-done.1, f32[408,128]{1,0:T(8,128)S(1)} %get-tuple-element.30.refs_2_, f32[384,128]{1,0:T(8,128)S(1)} %collective-permute-done.5.refs_3_, ...), custom_call_target="tpu_custom_call" | custom-call | flops 100000000 | bytes 1 | tf_op jit(solution)/shard_map/pairs_1_1/pallas_call | solution.py:499
  36.5 0.0 collective-permute-done.4.refs_3_
  36.5 3.8 %pairs_2_1.1 = (f32[96,128]{1,0:T(8,128)}, f32[96,128]{1,0:T(8,128)}, f32[6,1,128]{2,1,0:T(1,128)}) custom-call(f32[192,128]{1,0:T(8,128)S(1)} %pairs_2_0.1.refs_0_.refs_2_, f32[232,128]{1,0:T(8,128)S(1)} %copy-done.1, f32[408,128]{1,0:T(8,128)S(1)} %get-tuple-element.30.refs_2_, f32[384,128]{1,0:T(8,128)S(1)} %collective-permute-done.4.refs_3_, ...), custom_call_target="tpu_custom_call" | custom-call | flops 100000000 | bytes 1 | tf_op jit(solution)/shard_map/pairs_2_1/pallas_call | solution.py:499
  (2 shorter events, 0.0 us)
Async XLA Ops:
  2.3 6.5 %collective-permute-start = (f32[232,128]{1,0:T(8,128)}, f32[232,128]{1,0:T(8,128)S(1)}, u32[]{:S(2)}, u32[]{:S(2)}) collective-permute-start(f32[232,128]{1,0:T(8,128)} %kick.1.refs_0_.refs_1_.refs_2_.refs_3_), channel_id=1, source_target_pairs={{0,1},{1,0},{2,3},{3,2},{4,5},{5,4},{6,7},{7,6},{8,9},{9,8},{10,11... | collective-permute-start | bytes 356360 | tf_op jit(solution)/shard_map/ppermute | solution.py:594
  5.3 0.9 %copy-start = (f32[232,128]{1,0:T(8,128)S(1)}, f32[232,128]{1,0:T(8,128)}, u32[]{:S(2)}) copy-start(f32[232,128]{1,0:T(8,128)} %kick.1.refs_0_.refs_1_.refs_2_.refs_3_) | copy-start | bytes 356356
  6.2 2.5 %copy-start.1 = (f32[232,128]{1,0:T(8,128)S(1)}, f32[232,128]{1,0:T(8,128)}, u32[]{:S(2)}) copy-start(f32[232,128]{1,0:T(8,128)} %kick.1.refs_0_.refs_1_.refs_2_.refs_3_) | copy-start | bytes 356356
  8.8 7.9 %collective-permute-start.2 = (f32[464,128]{1,0:T(8,128)S(1)}, f32[464,128]{1,0:T(8,128)S(1)}, u32[]{:S(2)}, u32[]{:S(2)}) collective-permute-start(f32[464,128]{1,0:T(8,128)S(1)} %pad_maximum_fusion), channel_id=1, source_target_pairs={{0,2},{4,6},{8,10},{12,14},{16,18},{20,22},{24,26},{28,30},{2,0},{... | collective-permute-start | bytes 712712 | tf_op jit(solution)/shard_map/ppermute | solution.py:614
  8.8 11.0 %collective-permute-start.1 = (f32[464,128]{1,0:T(8,128)S(1)}, f32[464,128]{1,0:T(8,128)S(1)}, u32[]{:S(2)}, u32[]{:S(2)}) collective-permute-start(f32[464,128]{1,0:T(8,128)S(1)} %pad_maximum_fusion), channel_id=1, source_target_pairs={{2,4},{6,8},{10,12},{14,16},{18,20},{22,24},{26,28},{30,0},{4,2},{... | collective-permute-start | bytes 712712 | tf_op jit(solution)/shard_map/ppermute | solution.py:613
  22.9 4.7 %collective-permute-start.3 = (f32[192,128]{1,0:T(8,128)S(1)}, f32[192,128]{1,0:T(8,128)S(1)}, u32[]{:S(2)}, u32[]{:S(2)}) collective-permute-start(f32[192,128]{1,0:T(8,128)S(1)} %pairs_2_0.1.refs_0_.refs_2_), channel_id=1, source_target_pairs={{0,1},{1,0},{2,3},{3,2},{4,5},{5,4},{6,7},{7,6},{8,9},{9,8},{10,11... | collective-permute-start | bytes 294920 | tf_op jit(solution)/shard_map/ppermute | solution.py:594
  27.6 5.5 %collective-permute-start.5 = (f32[384,128]{1,0:T(8,128)S(1)}, f32[384,128]{1,0:T(8,128)S(1)}, u32[]{:S(2)}, u32[]{:S(2)}) collective-permute-start(f32[384,128]{1,0:T(8,128)S(1)} %pad_maximum_fusion.1), channel_id=1, source_target_pairs={{0,2},{4,6},{8,10},{12,14},{16,18},{20,22},{24,26},{28,30},{2,0},{... | collective-permute-start | bytes 589832 | tf_op jit(solution)/shard_map/ppermute | solution.py:614
  27.7 8.9 %collective-permute-start.4 = (f32[384,128]{1,0:T(8,128)S(1)}, f32[384,128]{1,0:T(8,128)S(1)}, u32[]{:S(2)}, u32[]{:S(2)}) collective-permute-start(f32[384,128]{1,0:T(8,128)S(1)} %pad_maximum_fusion.1), channel_id=1, source_target_pairs={{2,4},{6,8},{10,12},{14,16},{18,20},{22,24},{26,28},{30,0},{4,2},{... | collective-permute-start | bytes 589832 | tf_op jit(solution)/shard_map/ppermute | solution.py:613

commit v7 on v6

--- a/solution.py
+++ b/solution.py
@@ -442,7 +442,8 @@
     if own:
         own_row()
     else:
-        lax.fori_loop(0, len(rows), direction, 0)
+        for r in range(len(rows)):
+            direction(jnp.int32(r), 0)
 
     half = F32(0.5 * TIME_STEP)
     for c in range(3):

time: 40.8 us -> 41 us (level)
  Pallas kernels: 26.5 us -> 27 us
    pallas_call x8, Pallas kernels: 24.9 us -> 25.4 us  [pairs(): pl.pallas_call(functools.partial(pair_kernel, slots=slots, lanes=lanes, s...]
  transfers between devices with their start and end apart: 6 -> 6, of which waited for: 2 -> 1; matrix products, arithmetic and copies ran while one was open for 0% -> 0% of each run, Pallas kernels for 45% -> 44%
where the time goes in v7:
time: 41 us; the launch traced here: 40.8 us
  Pallas kernels  27 us (66%)
  starting transfers between devices  11.6 us (28%)
  local copies, waits for them, and re-layouts  0.94 us (2%)
  between operations  0.75 us (2%)
  waiting for transfers between devices  0.42 us (1%)
    pallas_call x8, Pallas kernels, pairs(): pl.pallas_call(functools.partial(pair_kernel, slots=slots, lanes=lanes, s...  25.4 us
    ppermute x2, starting transfers between devices, shards(): far = lax.ppermute(stacked, 'xy', swap(xy, 1))  6.97 us
    ppermute x2, starting transfers between devices, shards(): planes = [lax.ppermute(state, 'gz', ring(gz, -1))]  4.51 us
    pallas_call x1, Pallas kernels, shards(): pl.pallas_call(functools.partial(kick_kernel, slots=slots, lanes=lanes),...  1.62 us
    unnamed x4, local copies, waits for them, and re-layouts  0.94 us
  transfers between devices with their start and end apart: 6, of which 1 were waited for; matrix products, arithmetic and copies ran while one was open for 0% of the time, Pallas kernels for 44%

profile of v7, /device:TPU:0, one launch (start us, length us, event | category | flops | bytes accessed | tf_op | source)
XLA Modules:
  0.0 40.8 jit_solution(945248803811958889)
XLA Ops:
  0.6 1.6 %kick.1.refs_0_.refs_1_.refs_2_.refs_3_ = f32[232,128]{1,0:T(8,128)} custom-call(f32[96,128]{1,0:T(8,128)} %bitcast.15, f32[96,128]{1,0:T(8,128)} %bitcast.16, f32[96,128]{1,0:T(8,128)} %bitcast.17, s32[32,128]{1,0:T(8,128)} %bitcast.18, s32[1,128]{1,0:T(1,128)} %bitcast.19, s32[1,2]{1,0:T(1,128)} %bitcast.20), custom_call_target="tpu_custom_call" | custom-call | tf_op jit(solution)/shard_map/kick/pallas_call | solution.py:580
  2.3 3.0 %collective-permute-start = (f32[232,128]{1,0:T(8,128)}, f32[232,128]{1,0:T(8,128)S(1)}, u32[]{:S(2)}, u32[]{:S(2)}) collective-permute-start(f32[232,128]{1,0:T(8,128)} %kick.1.refs_0_.refs_1_.refs_2_.refs_3_), channel_id=1, source_target_pairs={{0,1},{1,0},{2,3},{3,2},{4,5},{5,4},{6,7},{7,6},{8,9},{9,8},{10,11... | collective-permute-start | bytes 356360 | tf_op jit(solution)/shard_map/ppermute | solution.py:595
  5.3 0.0 copy-start
  5.3 0.9 %copy-done = f32[232,128]{1,0:T(8,128)S(1)} copy-done((f32[232,128]{1,0:T(8,128)S(1)}, f32[232,128]{1,0:T(8,128)}, u32[]{:S(2)}) %copy-start) | copy-done | bytes 118808
  6.2 0.0 copy-start.1
  6.2 2.5 %pairs_0_0.2 = (f32[96,128]{1,0:T(8,128)S(1)}, f32[408,128]{1,0:T(8,128)S(1)}) custom-call(f32[232,128]{1,0:T(8,128)S(1)} %copy-done, f32[232,128]{1,0:T(8,128)S(1)} %copy-done, f32[232,128]{1,0:T(8,128)S(1)} %copy-done), custom_call_target="tpu_custom_call" | custom-call | flops 100000000 | bytes 1 | tf_op jit(solution)/shard_map/pairs_0_0/pallas_call | solution.py:500
  8.8 0.0 collective-permute-done.refs_3_.refs_4_
  8.8 0.0 copy-done.1
  8.8 0.1 collective-permute-start.2
  8.9 4.8 %collective-permute-start.1 = (f32[464,128]{1,0:T(8,128)S(1)}, f32[464,128]{1,0:T(8,128)S(1)}, u32[]{:S(2)}, u32[]{:S(2)}) collective-permute-start(f32[464,128]{1,0:T(8,128)S(1)} %pad_maximum_fusion), channel_id=1, source_target_pairs={{2,4},{6,8},{10,12},{14,16},{18,20},{22,24},{26,28},{30,0},{4,2},{... | collective-permute-start | bytes 712712 | tf_op jit(solution)/shard_map/ppermute | solution.py:614
  13.7 2.7 %pairs_0_0.3.refs_4_ = f32[96,128]{1,0:T(8,128)S(1)} custom-call(f32[232,128]{1,0:T(8,128)S(1)} %copy-done.1, f32[232,128]{1,0:T(8,128)S(1)} %copy-done.1, f32[408,128]{1,0:T(8,128)S(1)} %get-tuple-element.24.refs_2_, f32[232,128]{1,0:T(8,128)S(1)} %collective-permute-done.refs_3_.refs_4_, f32[96,128]{1,0:T(8,128)S(1)} %get-tuple-element.26.refs_4_), custom_call_target="tpu_custom_call" | custom-call | flops 100000000 | bytes 1 | tf_op jit(solution)/shard_map/pairs_0_0/pallas_call | solution.py:500
  16.4 0.0 collective-permute-done.2.refs_3_.refs_4_
  16.5 3.1 %pairs_1_0.1.refs_4_ = f32[96,128]{1,0:T(8,128)S(1)} custom-call(f32[232,128]{1,0:T(8,128)S(1)} %copy-done.1, f32[232,128]{1,0:T(8,128)S(1)} %copy-done.1, f32[408,128]{1,0:T(8,128)S(1)} %get-tuple-element.24.refs_2_, f32[464,128]{1,0:T(8,128)S(1)} %collective-permute-done.2.refs_3_.refs_4_, f32[96,128]{1,0:T(8,128)S(1)} %pairs_0_0.3.refs_4_), custom_call_target="tpu_custom_call" | custom-call | flops 100000000 | bytes 1 | tf_op jit(solution)/shard_map/pairs_1_0/pallas_call | solution.py:500
  19.5 0.0 collective-permute-done.1.refs_3_.refs_4_
  19.5 3.2 %pairs_2_0.1.refs_0_.refs_2_ = f32[192,128]{1,0:T(8,128)S(1)} custom-call(f32[232,128]{1,0:T(8,128)S(1)} %copy-done.1, f32[232,128]{1,0:T(8,128)S(1)} %copy-done.1, f32[408,128]{1,0:T(8,128)S(1)} %get-tuple-element.24.refs_2_, f32[464,128]{1,0:T(8,128)S(1)} %collective-permute-done.1.refs_3_.refs_4_, f32[96,128]{1,0:T(8,128)S(1)} %pairs_1_0.1.refs_4_), custom_call_target="tpu_custom_call" | custom-call | flops 100000000 | bytes 1 | tf_op jit(solution)/shard_map/pairs_2_0/pallas_call | solution.py:500
  22.7 1.5 %collective-permute-start.3 = (f32[192,128]{1,0:T(8,128)S(1)}, f32[192,128]{1,0:T(8,128)S(1)}, u32[]{:S(2)}, u32[]{:S(2)}) collective-permute-start(f32[192,128]{1,0:T(8,128)S(1)} %pairs_2_0.1.refs_0_.refs_2_), channel_id=1, source_target_pairs={{0,1},{1,0},{2,3},{3,2},{4,5},{5,4},{6,7},{7,6},{8,9},{9,8},{10,11... | collective-permute-start | bytes 294920 | tf_op jit(solution)/shard_map/ppermute | solution.py:595
  24.2 2.8 %pairs_0_1.2 = (f32[96,128]{1,0:T(8,128)S(1)}, f32[48,128]{1,0:T(8,128)S(1)}, f32[408,128]{1,0:T(8,128)S(1)}) custom-call(f32[192,128]{1,0:T(8,128)S(1)} %pairs_2_0.1.refs_0_.refs_2_, f32[232,128]{1,0:T(8,128)S(1)} %copy-done.1, f32[192,128]{1,0:T(8,128)S(1)} %pairs_2_0.1.refs_0_.refs_2_, f32[232,128]{1,0:T(8,128)S(1)} %copy-done.1), custom_call_target="tpu_custom_call" | custom-call | flops 100000000 | bytes 1 | tf_op jit(solution)/shard_map/pairs_0_1/pallas_call | solution.py:500
  27.0 0.4 collective-permute-done.3.refs_3_
  27.4 0.1 collective-permute-start.5
  27.5 2.1 %collective-permute-start.4 = (f32[384,128]{1,0:T(8,128)S(1)}, f32[384,128]{1,0:T(8,128)S(1)}, u32[]{:S(2)}, u32[]{:S(2)}) collective-permute-start(f32[384,128]{1,0:T(8,128)S(1)} %pad_maximum_fusion.1), channel_id=1, source_target_pairs={{2,4},{6,8},{10,12},{14,16},{18,20},{22,24},{26,28},{30,0},{4,2},{... | collective-permute-start | bytes 589832 | tf_op jit(solution)/shard_map/ppermute | solution.py:614
  29.6 3.4 %pairs_0_1.3 = (f32[96,128]{1,0:T(8,128)S(1)}, f32[48,128]{1,0:T(8,128)S(1)}) custom-call(f32[192,128]{1,0:T(8,128)S(1)} %pairs_2_0.1.refs_0_.refs_2_, f32[232,128]{1,0:T(8,128)S(1)} %copy-done.1, f32[408,128]{1,0:T(8,128)S(1)} %get-tuple-element.30.refs_2_, f32[192,128]{1,0:T(8,128)S(1)} %collective-permute-done.3.refs_3_, ...), custom_call_target="tpu_custom_call" | custom-call | flops 100000000 | bytes 1 | tf_op jit(solution)/shard_map/pairs_0_1/pallas_call | solution.py:500
  33.0 0.0 collective-permute-done.5.refs_3_
  33.0 3.6 %pairs_1_1.1 = (f32[96,128]{1,0:T(8,128)S(1)}, f32[48,128]{1,0:T(8,128)S(1)}) custom-call(f32[192,128]{1,0:T(8,128)S(1)} %pairs_2_0.1.refs_0_.refs_2_, f32[232,128]{1,0:T(8,128)S(1)} %copy-done.1, f32[408,128]{1,0:T(8,128)S(1)} %get-tuple-element.30.refs_2_, f32[384,128]{1,0:T(8,128)S(1)} %collective-permute-done.5.refs_3_, ...), custom_call_target="tpu_custom_call" | custom-call | flops 100000000 | bytes 1 | tf_op jit(solution)/shard_map/pairs_1_1/pallas_call | solution.py:500
  36.6 0.0 collective-permute-done.4.refs_3_
  36.6 4.2 %pairs_2_1.1 = (f32[96,128]{1,0:T(8,128)}, f32[96,128]{1,0:T(8,128)}, f32[6,1,128]{2,1,0:T(1,128)}) custom-call(f32[192,128]{1,0:T(8,128)S(1)} %pairs_2_0.1.refs_0_.refs_2_, f32[232,128]{1,0:T(8,128)S(1)} %copy-done.1, f32[408,128]{1,0:T(8,128)S(1)} %get-tuple-element.30.refs_2_, f32[384,128]{1,0:T(8,128)S(1)} %collective-permute-done.4.refs_3_, ...), custom_call_target="tpu_custom_call" | custom-call | flops 100000000 | bytes 1 | tf_op jit(solution)/shard_map/pairs_2_1/pallas_call | solution.py:500
  (2 shorter events, 0.0 us)
Async XLA Ops:
  2.3 6.5 %collective-permute-start = (f32[232,128]{1,0:T(8,128)}, f32[232,128]{1,0:T(8,128)S(1)}, u32[]{:S(2)}, u32[]{:S(2)}) collective-permute-start(f32[232,128]{1,0:T(8,128)} %kick.1.refs_0_.refs_1_.refs_2_.refs_3_), channel_id=1, source_target_pairs={{0,1},{1,0},{2,3},{3,2},{4,5},{5,4},{6,7},{7,6},{8,9},{9,8},{10,11... | collective-permute-start | bytes 356360 | tf_op jit(solution)/shard_map/ppermute | solution.py:595
  5.3 0.9 %copy-start = (f32[232,128]{1,0:T(8,128)S(1)}, f32[232,128]{1,0:T(8,128)}, u32[]{:S(2)}) copy-start(f32[232,128]{1,0:T(8,128)} %kick.1.refs_0_.refs_1_.refs_2_.refs_3_) | copy-start | bytes 356356
  6.2 2.6 %copy-start.1 = (f32[232,128]{1,0:T(8,128)S(1)}, f32[232,128]{1,0:T(8,128)}, u32[]{:S(2)}) copy-start(f32[232,128]{1,0:T(8,128)} %kick.1.refs_0_.refs_1_.refs_2_.refs_3_) | copy-start | bytes 356356
  8.8 7.6 %collective-permute-start.2 = (f32[464,128]{1,0:T(8,128)S(1)}, f32[464,128]{1,0:T(8,128)S(1)}, u32[]{:S(2)}, u32[]{:S(2)}) collective-permute-start(f32[464,128]{1,0:T(8,128)S(1)} %pad_maximum_fusion), channel_id=1, source_target_pairs={{0,2},{4,6},{8,10},{12,14},{16,18},{20,22},{24,26},{28,30},{2,0},{... | collective-permute-start | bytes 712712 | tf_op jit(solution)/shard_map/ppermute | solution.py:615
  8.9 10.6 %collective-permute-start.1 = (f32[464,128]{1,0:T(8,128)S(1)}, f32[464,128]{1,0:T(8,128)S(1)}, u32[]{:S(2)}, u32[]{:S(2)}) collective-permute-start(f32[464,128]{1,0:T(8,128)S(1)} %pad_maximum_fusion), channel_id=1, source_target_pairs={{2,4},{6,8},{10,12},{14,16},{18,20},{22,24},{26,28},{30,0},{4,2},{... | collective-permute-start | bytes 712712 | tf_op jit(solution)/shard_map/ppermute | solution.py:614
  22.7 4.7 %collective-permute-start.3 = (f32[192,128]{1,0:T(8,128)S(1)}, f32[192,128]{1,0:T(8,128)S(1)}, u32[]{:S(2)}, u32[]{:S(2)}) collective-permute-start(f32[192,128]{1,0:T(8,128)S(1)} %pairs_2_0.1.refs_0_.refs_2_), channel_id=1, source_target_pairs={{0,1},{1,0},{2,3},{3,2},{4,5},{5,4},{6,7},{7,6},{8,9},{9,8},{10,11... | collective-permute-start | bytes 294920 | tf_op jit(solution)/shard_map/ppermute | solution.py:595
  27.4 5.6 %collective-permute-start.5 = (f32[384,128]{1,0:T(8,128)S(1)}, f32[384,128]{1,0:T(8,128)S(1)}, u32[]{:S(2)}, u32[]{:S(2)}) collective-permute-start(f32[384,128]{1,0:T(8,128)S(1)} %pad_maximum_fusion.1), channel_id=1, source_target_pairs={{0,2},{4,6},{8,10},{12,14},{16,18},{20,22},{24,26},{28,30},{2,0},{... | collective-permute-start | bytes 589832 | tf_op jit(solution)/shard_map/ppermute | solution.py:615
  27.5 9.1 %collective-permute-start.4 = (f32[384,128]{1,0:T(8,128)S(1)}, f32[384,128]{1,0:T(8,128)S(1)}, u32[]{:S(2)}, u32[]{:S(2)}) collective-permute-start(f32[384,128]{1,0:T(8,128)S(1)} %pad_maximum_fusion.1), channel_id=1, source_target_pairs={{2,4},{6,8},{10,12},{14,16},{18,20},{22,24},{26,28},{30,0},{4,2},{... | collective-permute-start | bytes 589832 | tf_op jit(solution)/shard_map/ppermute | solution.py:614

commit v8 on v7

--- a/solution.py
+++ b/solution.py
@@ -352,11 +352,8 @@
         return (size + 2 * SUB - 1) // (2 * SUB)
 
     def each(first, size, fill):
-        def body(k, _):
-            fill(k)
-            return 0
-
-        lax.fori_loop(first, steps(size), body, 0)
+        for k in range(first, (groups + 1) // 2):
+            pl.when(steps(size) > k)(functools.partial(fill, jnp.int32(k)))
 
     def close(filled):
         liste[pl.ds(filled, SUB), :] = jnp.full((SUB, lanes), FAR, F32)

time: 41 us -> 41.1 us (level)
  Pallas kernels: 27 us -> 26.4 us
    pallas_call x8, Pallas kernels: 25.4 us -> 24.8 us  [pairs(): pl.pallas_call(functools.partial(pair_kernel, slots=slots, lanes=lanes, s...]
  transfers between devices with their start and end apart: 6 -> 6, of which waited for: 1 -> 2; matrix products, arithmetic and copies ran while one was open for 0% -> 0% of each run, Pallas kernels for 44% -> 42%
where the time goes in v8:
time: 41.1 us; the launch traced here: 40.8 us
  Pallas kernels  26.4 us (64%)
  starting transfers between devices  11.9 us (29%)
  local copies, waits for them, and re-layouts  0.94 us (2%)
  waiting for transfers between devices  0.74 us (2%)
  between operations  0.73 us (2%)
    pallas_call x8, Pallas kernels, pairs(): pl.pallas_call(functools.partial(pair_kernel, slots=slots, lanes=lanes, s...  24.8 us
    ppermute x2, starting transfers between devices, shards(): far = lax.ppermute(stacked, 'xy', swap(xy, 1))  7 us
    ppermute x2, starting transfers between devices, shards(): planes = [lax.ppermute(state, 'gz', ring(gz, -1))]  4.78 us
    pallas_call x1, Pallas kernels, shards(): pl.pallas_call(functools.partial(kick_kernel, slots=slots, lanes=lanes),...  1.62 us
    unnamed x4, local copies, waits for them, and re-layouts  0.94 us
  transfers between devices with their start and end apart: 6, of which 2 were waited for; matrix products, arithmetic and copies ran while one was open for 0% of the time, Pallas kernels for 42%

profile of v8, /device:TPU:0, one launch (start us, length us, event | category | flops | bytes accessed | tf_op | source)
XLA Modules:
  0.0 40.8 jit_solution(11677648092553999095)
XLA Ops:
  0.6 1.6 %kick.1.refs_0_.refs_1_.refs_2_.refs_3_ = f32[232,128]{1,0:T(8,128)} custom-call(f32[96,128]{1,0:T(8,128)} %bitcast.15, f32[96,128]{1,0:T(8,128)} %bitcast.16, f32[96,128]{1,0:T(8,128)} %bitcast.17, s32[32,128]{1,0:T(8,128)} %bitcast.18, s32[1,128]{1,0:T(1,128)} %bitcast.19, s32[1,2]{1,0:T(1,128)} %bitcast.20), custom_call_target="tpu_custom_call" | custom-call | tf_op jit(solution)/shard_map/kick/pallas_call | solution.py:577
  2.3 3.0 %collective-permute-start = (f32[232,128]{1,0:T(8,128)}, f32[232,128]{1,0:T(8,128)S(1)}, u32[]{:S(2)}, u32[]{:S(2)}) collective-permute-start(f32[232,128]{1,0:T(8,128)} %kick.1.refs_0_.refs_1_.refs_2_.refs_3_), channel_id=1, source_target_pairs={{0,1},{1,0},{2,3},{3,2},{4,5},{5,4},{6,7},{7,6},{8,9},{9,8},{10,11... | collective-permute-start | bytes 356360 | tf_op jit(solution)/shard_map/ppermute | solution.py:592
  5.3 0.0 copy-start
  5.3 0.9 %copy-done = f32[232,128]{1,0:T(8,128)S(1)} copy-done((f32[232,128]{1,0:T(8,128)S(1)}, f32[232,128]{1,0:T(8,128)}, u32[]{:S(2)}) %copy-start) | copy-done | bytes 118808
  6.2 0.0 copy-start.1
  6.2 2.2 %pairs_0_0.2 = (f32[96,128]{1,0:T(8,128)S(1)}, f32[408,128]{1,0:T(8,128)S(1)}) custom-call(f32[232,128]{1,0:T(8,128)S(1)} %copy-done, f32[232,128]{1,0:T(8,128)S(1)} %copy-done, f32[232,128]{1,0:T(8,128)S(1)} %copy-done), custom_call_target="tpu_custom_call" | custom-call | flops 100000000 | bytes 1 | tf_op jit(solution)/shard_map/pairs_0_0/pallas_call | solution.py:497
  8.5 0.3 collective-permute-done.refs_3_.refs_4_
  8.7 0.0 copy-done.1
  8.8 0.1 collective-permute-start.2
  8.8 4.9 %collective-permute-start.1 = (f32[464,128]{1,0:T(8,128)S(1)}, f32[464,128]{1,0:T(8,128)S(1)}, u32[]{:S(2)}, u32[]{:S(2)}) collective-permute-start(f32[464,128]{1,0:T(8,128)S(1)} %pad_maximum_fusion), channel_id=1, source_target_pairs={{2,4},{6,8},{10,12},{14,16},{18,20},{22,24},{26,28},{30,0},{4,2},{... | collective-permute-start | bytes 712712 | tf_op jit(solution)/shard_map/ppermute | solution.py:611
  13.7 2.7 %pairs_0_0.3.refs_4_ = f32[96,128]{1,0:T(8,128)S(1)} custom-call(f32[232,128]{1,0:T(8,128)S(1)} %copy-done.1, f32[232,128]{1,0:T(8,128)S(1)} %copy-done.1, f32[408,128]{1,0:T(8,128)S(1)} %get-tuple-element.24.refs_2_, f32[232,128]{1,0:T(8,128)S(1)} %collective-permute-done.refs_3_.refs_4_, f32[96,128]{1,0:T(8,128)S(1)} %get-tuple-element.26.refs_4_), custom_call_target="tpu_custom_call" | custom-call | flops 100000000 | bytes 1 | tf_op jit(solution)/shard_map/pairs_0_0/pallas_call | solution.py:497
  16.4 0.0 collective-permute-done.2.refs_3_.refs_4_
  16.5 2.8 %pairs_1_0.1.refs_4_ = f32[96,128]{1,0:T(8,128)S(1)} custom-call(f32[232,128]{1,0:T(8,128)S(1)} %copy-done.1, f32[232,128]{1,0:T(8,128)S(1)} %copy-done.1, f32[408,128]{1,0:T(8,128)S(1)} %get-tuple-element.24.refs_2_, f32[464,128]{1,0:T(8,128)S(1)} %collective-permute-done.2.refs_3_.refs_4_, f32[96,128]{1,0:T(8,128)S(1)} %pairs_0_0.3.refs_4_), custom_call_target="tpu_custom_call" | custom-call | flops 100000000 | bytes 1 | tf_op jit(solution)/shard_map/pairs_1_0/pallas_call | solution.py:497
  19.2 0.0 collective-permute-done.1.refs_3_.refs_4_
  19.3 3.3 %pairs_2_0.1.refs_0_.refs_2_ = f32[192,128]{1,0:T(8,128)S(1)} custom-call(f32[232,128]{1,0:T(8,128)S(1)} %copy-done.1, f32[232,128]{1,0:T(8,128)S(1)} %copy-done.1, f32[408,128]{1,0:T(8,128)S(1)} %get-tuple-element.24.refs_2_, f32[464,128]{1,0:T(8,128)S(1)} %collective-permute-done.1.refs_3_.refs_4_, f32[96,128]{1,0:T(8,128)S(1)} %pairs_1_0.1.refs_4_), custom_call_target="tpu_custom_call" | custom-call | flops 100000000 | bytes 1 | tf_op jit(solution)/shard_map/pairs_2_0/pallas_call | solution.py:497
  22.6 1.7 %collective-permute-start.3 = (f32[192,128]{1,0:T(8,128)S(1)}, f32[192,128]{1,0:T(8,128)S(1)}, u32[]{:S(2)}, u32[]{:S(2)}) collective-permute-start(f32[192,128]{1,0:T(8,128)S(1)} %pairs_2_0.1.refs_0_.refs_2_), channel_id=1, source_target_pairs={{0,1},{1,0},{2,3},{3,2},{4,5},{5,4},{6,7},{7,6},{8,9},{9,8},{10,11... | collective-permute-start | bytes 294920 | tf_op jit(solution)/shard_map/ppermute | solution.py:592
  24.3 2.5 %pairs_0_1.2 = (f32[96,128]{1,0:T(8,128)S(1)}, f32[48,128]{1,0:T(8,128)S(1)}, f32[408,128]{1,0:T(8,128)S(1)}) custom-call(f32[192,128]{1,0:T(8,128)S(1)} %pairs_2_0.1.refs_0_.refs_2_, f32[232,128]{1,0:T(8,128)S(1)} %copy-done.1, f32[192,128]{1,0:T(8,128)S(1)} %pairs_2_0.1.refs_0_.refs_2_, f32[232,128]{1,0:T(8,128)S(1)} %copy-done.1), custom_call_target="tpu_custom_call" | custom-call | flops 100000000 | bytes 1 | tf_op jit(solution)/shard_map/pairs_0_1/pallas_call | solution.py:497
  26.8 0.5 %collective-permute-done.3.refs_3_ = f32[192,128]{1,0:T(8,128)S(1)} collective-permute-done((f32[192,128]{1,0:T(8,128)S(1)}, f32[192,128]{1,0:T(8,128)S(1)}, u32[]{:S(2)}, u32[]{:S(2)}) %collective-permute-start.3) | collective-permute-done | bytes 98336 | tf_op jit(solution)/shard_map/ppermute | solution.py:592
  27.3 0.1 collective-permute-start.5
  27.4 2.1 %collective-permute-start.4 = (f32[384,128]{1,0:T(8,128)S(1)}, f32[384,128]{1,0:T(8,128)S(1)}, u32[]{:S(2)}, u32[]{:S(2)}) collective-permute-start(f32[384,128]{1,0:T(8,128)S(1)} %pad_maximum_fusion.1), channel_id=1, source_target_pairs={{2,4},{6,8},{10,12},{14,16},{18,20},{22,24},{26,28},{30,0},{4,2},{... | collective-permute-start | bytes 589832 | tf_op jit(solution)/shard_map/ppermute | solution.py:611
  29.5 3.5 %pairs_0_1.3 = (f32[96,128]{1,0:T(8,128)S(1)}, f32[48,128]{1,0:T(8,128)S(1)}) custom-call(f32[192,128]{1,0:T(8,128)S(1)} %pairs_2_0.1.refs_0_.refs_2_, f32[232,128]{1,0:T(8,128)S(1)} %copy-done.1, f32[408,128]{1,0:T(8,128)S(1)} %get-tuple-element.30.refs_2_, f32[192,128]{1,0:T(8,128)S(1)} %collective-permute-done.3.refs_3_, ...), custom_call_target="tpu_custom_call" | custom-call | flops 100000000 | bytes 1 | tf_op jit(solution)/shard_map/pairs_0_1/pallas_call | solution.py:497
  33.0 0.0 collective-permute-done.5.refs_3_
  33.0 3.4 %pairs_1_1.1 = (f32[96,128]{1,0:T(8,128)S(1)}, f32[48,128]{1,0:T(8,128)S(1)}) custom-call(f32[192,128]{1,0:T(8,128)S(1)} %pairs_2_0.1.refs_0_.refs_2_, f32[232,128]{1,0:T(8,128)S(1)} %copy-done.1, f32[408,128]{1,0:T(8,128)S(1)} %get-tuple-element.30.refs_2_, f32[384,128]{1,0:T(8,128)S(1)} %collective-permute-done.5.refs_3_, ...), custom_call_target="tpu_custom_call" | custom-call | flops 100000000 | bytes 1 | tf_op jit(solution)/shard_map/pairs_1_1/pallas_call | solution.py:497
  36.4 0.0 collective-permute-done.4.refs_3_
  36.4 4.4 %pairs_2_1.1 = (f32[96,128]{1,0:T(8,128)}, f32[96,128]{1,0:T(8,128)}, f32[6,1,128]{2,1,0:T(1,128)}) custom-call(f32[192,128]{1,0:T(8,128)S(1)} %pairs_2_0.1.refs_0_.refs_2_, f32[232,128]{1,0:T(8,128)S(1)} %copy-done.1, f32[408,128]{1,0:T(8,128)S(1)} %get-tuple-element.30.refs_2_, f32[384,128]{1,0:T(8,128)S(1)} %collective-permute-done.4.refs_3_, ...), custom_call_target="tpu_custom_call" | custom-call | flops 100000000 | bytes 1 | tf_op jit(solution)/shard_map/pairs_2_1/pallas_call | solution.py:497
  (2 shorter events, 0.0 us)
Async XLA Ops:
  2.3 6.5 %collective-permute-start = (f32[232,128]{1,0:T(8,128)}, f32[232,128]{1,0:T(8,128)S(1)}, u32[]{:S(2)}, u32[]{:S(2)}) collective-permute-start(f32[232,128]{1,0:T(8,128)} %kick.1.refs_0_.refs_1_.refs_2_.refs_3_), channel_id=1, source_target_pairs={{0,1},{1,0},{2,3},{3,2},{4,5},{5,4},{6,7},{7,6},{8,9},{9,8},{10,11... | collective-permute-start | bytes 356360 | tf_op jit(solution)/shard_map/ppermute | solution.py:592
  5.3 0.9 %copy-start = (f32[232,128]{1,0:T(8,128)S(1)}, f32[232,128]{1,0:T(8,128)}, u32[]{:S(2)}) copy-start(f32[232,128]{1,0:T(8,128)} %kick.1.refs_0_.refs_1_.refs_2_.refs_3_) | copy-start | bytes 356356
  6.2 2.5 %copy-start.1 = (f32[232,128]{1,0:T(8,128)S(1)}, f32[232,128]{1,0:T(8,128)}, u32[]{:S(2)}) copy-start(f32[232,128]{1,0:T(8,128)} %kick.1.refs_0_.refs_1_.refs_2_.refs_3_) | copy-start | bytes 356356
  8.8 7.7 %collective-permute-start.2 = (f32[464,128]{1,0:T(8,128)S(1)}, f32[464,128]{1,0:T(8,128)S(1)}, u32[]{:S(2)}, u32[]{:S(2)}) collective-permute-start(f32[464,128]{1,0:T(8,128)S(1)} %pad_maximum_fusion), channel_id=1, source_target_pairs={{0,2},{4,6},{8,10},{12,14},{16,18},{20,22},{24,26},{28,30},{2,0},{... | collective-permute-start | bytes 712712 | tf_op jit(solution)/shard_map/ppermute | solution.py:612
  8.8 10.4 %collective-permute-start.1 = (f32[464,128]{1,0:T(8,128)S(1)}, f32[464,128]{1,0:T(8,128)S(1)}, u32[]{:S(2)}, u32[]{:S(2)}) collective-permute-start(f32[464,128]{1,0:T(8,128)S(1)} %pad_maximum_fusion), channel_id=1, source_target_pairs={{2,4},{6,8},{10,12},{14,16},{18,20},{22,24},{26,28},{30,0},{4,2},{... | collective-permute-start | bytes 712712 | tf_op jit(solution)/shard_map/ppermute | solution.py:611
  22.6 4.7 %collective-permute-start.3 = (f32[192,128]{1,0:T(8,128)S(1)}, f32[192,128]{1,0:T(8,128)S(1)}, u32[]{:S(2)}, u32[]{:S(2)}) collective-permute-start(f32[192,128]{1,0:T(8,128)S(1)} %pairs_2_0.1.refs_0_.refs_2_), channel_id=1, source_target_pairs={{0,1},{1,0},{2,3},{3,2},{4,5},{5,4},{6,7},{7,6},{8,9},{9,8},{10,11... | collective-permute-start | bytes 294920 | tf_op jit(solution)/shard_map/ppermute | solution.py:592
  27.3 5.7 %collective-permute-start.5 = (f32[384,128]{1,0:T(8,128)S(1)}, f32[384,128]{1,0:T(8,128)S(1)}, u32[]{:S(2)}, u32[]{:S(2)}) collective-permute-start(f32[384,128]{1,0:T(8,128)S(1)} %pad_maximum_fusion.1), channel_id=1, source_target_pairs={{0,2},{4,6},{8,10},{12,14},{16,18},{20,22},{24,26},{28,30},{2,0},{... | collective-permute-start | bytes 589832 | tf_op jit(solution)/shard_map/ppermute | solution.py:612
  27.4 9.0 %collective-permute-start.4 = (f32[384,128]{1,0:T(8,128)S(1)}, f32[384,128]{1,0:T(8,128)S(1)}, u32[]{:S(2)}, u32[]{:S(2)}) collective-permute-start(f32[384,128]{1,0:T(8,128)S(1)} %pad_maximum_fusion.1), channel_id=1, source_target_pairs={{2,4},{6,8},{10,12},{14,16},{18,20},{22,24},{26,28},{30,0},{4,2},{... | collective-permute-start | bytes 589832 | tf_op jit(solution)/shard_map/ppermute | solution.py:611
